TPU v7x, 32 devices: a whole 2x2x4 slice. The times are simulated.
32 devices in a mesh: role: 2 (over x), grp: 8 (over z, y), tp: 2 (over core).
Axes of the slice: x: 2, y: 2, z: 4, core: 2. Of those that a mesh axis runs over, the one named last changes fastest.
Arguments:
- q_new: bfloat16 [256, 4096], P('grp', ('role', 'tp')), may hold values from -9 to 9
- k_new: bfloat16 [256, 512], P('grp', ('role', 'tp')), may hold values from -6 to 6
- v_new: bfloat16 [256, 512], P('grp', ('role', 'tp')), may hold values from -6 to 6
- k_cache: bfloat16 [256, 128, 512], P('grp', None, ('role', 'tp')), may hold values from -9 to 9
- v_cache: bfloat16 [256, 128, 512], P('grp', None, ('role', 'tp')), may hold values from -6 to 6
- cache_len: int32 [256], P('grp'), may hold values from 1 to 127
- cycle_start: int32 [256], P('grp'), may hold values from 0 to 127
- residual: bfloat16 [256, 2880], P('grp', ('role', 'tp')), may hold values from -6 to 6
- out_proj: bfloat16 [4096, 2880], P(('role', 'tp')), may hold values from -0.09375 to 0.09375
- norm_gain: float32 [2880], replicated, may hold values from 0.25 to 1.75
- router: bfloat16 [2880, 8], P(('role', 'tp')), may hold values from -0.21875 to 0.21875
- route_ids: int32 [256, 4], P('grp'), may hold values from 0 to 7, all different within a row; in each aligned block of 32 rows (0 to 31, 32 to 63, ...) at most 18 rows name the same one
- w_gate: bfloat16 [8, 2880, 1440], P('grp', None, ('role', 'tp')), may hold values from -0.109375 to 0.109375
- w_up: bfloat16 [8, 2880, 1440], P('grp', None, ('role', 'tp')), may hold values from -0.109375 to 0.109375
- w_down: bfloat16 [8, 1440, 2880], P('grp', ('role', 'tp')), may hold values from -0.15625 to 0.15625
Outputs:
- attended: bfloat16 [256, 2880], P('grp', ('role', 'tp'))
- expert_mix: bfloat16 [256, 2880], P('grp', ('role', 'tp'))
Inputs may be any that keep to these rules, and one draw needn't show every extreme that they name: `route_ids`: the 4 experts of a token differ. Among the tokens of one grp index (aligned blocks of 32 tokens) no expert is named more than 18 times, a bound that some block reaches.
All inputs are finite; a program needn't handle non-finite values.
Results may differ from a plain program's by a relative error of at most 0.017.
Values may be sent and summed in bfloat16 or wider, within the bound.
No kernel may reach another device: no remote copies, remote signals or barrier semaphores. Data moves between devices by JAX's collectives and lax.ppermute only.
A program may use at most 64 MiB of HBM per device.

v0:
```python
import jax
import jax.numpy as jnp
from jax import lax
from jax.sharding import PartitionSpec as P

HEADS = 64
KV_HEADS = 8
HD = 64


epsilon = 1e-05


def attend(q_new, k_new, v_new, k_cache, v_cache, cache_len, cycle_start):
    tokens = q_new.shape[0]
    window = k_cache.shape[1]
    kv_local = k_new.shape[1] // HD
    grouped = HEADS // KV_HEADS
    queries = q_new.reshape(tokens, kv_local, grouped, HD)
    cached_keys = k_cache.reshape(tokens, window, kv_local, HD)
    cached_values = v_cache.reshape(tokens, window, kv_local, HD)
    own_key = k_new.reshape(tokens, kv_local, HD)
    own_value = v_new.reshape(tokens, kv_local, HD)
    factor = HD ** (-0.5)
    scores = (
        jnp.einsum("tkgd,tskd->tkgs", queries, cached_keys, preferred_element_type=jnp.float32)
        * factor
    )
    own_score = (
        jnp.einsum("tkgd,tkd->tkg", queries, own_key, preferred_element_type=jnp.float32) * factor
    )
    positions = jnp.arange(window, dtype=jnp.int32)
    usable = (positions[None, :] - cycle_start[:, None]) % window < cache_len[:, None]
    usable = usable[:, None, None, :]
    masked = jnp.where(usable, scores, -1e30)
    highest = jnp.maximum(jnp.max(masked, axis=3), own_score)
    lifted = jnp.where(usable, jnp.exp(masked - highest[..., None]), 0.0)
    own_lift = jnp.exp(own_score - highest)
    denominator = jnp.sum(lifted, axis=3) + own_lift
    weights = (lifted / denominator[..., None]).astype(jnp.bfloat16)
    own_weight = (own_lift / denominator).astype(jnp.bfloat16)
    combined = jnp.einsum(
        "tkgs,tskd->tkgd", weights, cached_values, preferred_element_type=jnp.float32
    )
    combined = (
        combined
        + own_weight.astype(jnp.float32)[..., None] * own_value.astype(jnp.float32)[:, :, None, :]
    )
    return combined.reshape(tokens, -1).astype(jnp.bfloat16)


def slot_tables(route_ids, logits, capacity):
    experts_count = logits.shape[1]
    named = route_ids[:, :, None] == jnp.arange(experts_count, dtype=jnp.int32)
    chosen = jnp.sum(jnp.where(named, logits[:, None, :], 0.0), axis=2)
    lifted = jnp.exp(chosen)
    route_weight = lifted / jnp.sum(lifted, axis=1, keepdims=True)
    counts = jnp.sum(named.astype(jnp.int32), axis=1)
    earlier = jnp.cumsum(counts, axis=0) - counts
    ranks = jnp.sum(jnp.where(named, earlier[:, None, :], 0), axis=2)
    placed = named[:, :, :, None] & (
        ranks[:, :, None, None] == jnp.arange(capacity, dtype=jnp.int32)
    )
    select = jnp.sum(placed.astype(jnp.float32), axis=1).reshape(route_ids.shape[0], -1)
    mixing = jnp.sum(jnp.where(placed, route_weight[:, :, None, None], 0.0), axis=1).reshape(
        route_ids.shape[0], -1
    )
    return (select, mixing)


def serve(received, w_gate, w_up, w_down):
    sources = received.shape[0]
    items = received.shape[1]
    inputs = received.reshape(sources * items, received.shape[2])
    gate_lin = jnp.dot(inputs, w_gate[0], preferred_element_type=jnp.float32)
    up_lin = jnp.dot(inputs, w_up[0], preferred_element_type=jnp.float32)
    activated = (gate_lin * jax.nn.sigmoid(1.702 * gate_lin) * (up_lin + 1.0)).astype(jnp.bfloat16)
    partial_out = jnp.dot(activated, w_down[0], preferred_element_type=jnp.float32).reshape(
        sources, items, -1
    )
    rounded = lax.optimization_barrier(partial_out.astype(jnp.bfloat16))
    return lax.all_to_all(rounded, "grp", split_axis=0, concat_axis=0, tiled=True)


def local(
    q_new,
    k_new,
    v_new,
    k_cache,
    v_cache,
    cache_len,
    cycle_start,
    residual,
    out_proj,
    norm_gain,
    router,
    route_ids,
    w_gate,
    w_up,
    w_down,
):
    share = lax.axis_index(("role", "tp"))
    quarter = residual.shape[1]
    heads_out = attend(q_new, k_new, v_new, k_cache, v_cache, cache_len, cycle_start)
    projected = jnp.dot(heads_out, out_proj, preferred_element_type=jnp.float32)
    stream = lax.all_gather(residual, ("role", "tp"), axis=1, tiled=True).astype(
        jnp.float32
    ) + lax.psum(projected.astype(jnp.bfloat16), ("role", "tp")).astype(jnp.float32)
    scale = lax.rsqrt(jnp.mean(stream * stream, axis=1, keepdims=True) + epsilon)
    outgoing = (stream * scale * norm_gain).astype(jnp.bfloat16)
    own_normed = lax.dynamic_slice_in_dim(outgoing, share * quarter, quarter, 1)
    attended = lax.dynamic_slice_in_dim(stream, share * quarter, quarter, 1)
    logits = lax.psum(
        jnp.dot(own_normed, router, preferred_element_type=jnp.float32), ("role", "tp")
    )
    tokens = route_ids.shape[0]
    experts_count = logits.shape[1]
    capacity = max(3, tokens * route_ids.shape[1] // experts_count + 2)
    select, mixing = slot_tables(route_ids, logits, capacity)
    outbound = jnp.einsum(
        "ts,tf->sf", select.astype(jnp.bfloat16), outgoing, preferred_element_type=jnp.float32
    )
    outbound = outbound.astype(jnp.bfloat16).reshape(experts_count, capacity, -1)
    returned = serve(
        lax.all_to_all(outbound, "grp", split_axis=0, concat_axis=0, tiled=True),
        w_gate,
        w_up,
        w_down,
    )
    stacked = returned.reshape(-1, returned.shape[2]).astype(jnp.float32)
    combined = jnp.dot(mixing, stacked, precision=lax.Precision.HIGHEST)
    combined = lax.psum_scatter(
        combined.astype(jnp.bfloat16), ("role", "tp"), scatter_dimension=1, tiled=True
    ).astype(jnp.float32)
    return (attended.astype(jnp.bfloat16), combined.astype(jnp.bfloat16))


def solution(mesh):
    placed = (
        P("grp", ("role", "tp")),
        P("grp", ("role", "tp")),
        P("grp", ("role", "tp")),
        P("grp", None, ("role", "tp")),
        P("grp", None, ("role", "tp")),
        P("grp"),
        P("grp"),
        P("grp", ("role", "tp")),
        P(("role", "tp"), None),
        P(),
        P(("role", "tp"), None),
        P("grp", None),
        P("grp", None, ("role", "tp")),
        P("grp", None, ("role", "tp")),
        P("grp", ("role", "tp"), None),
    )
    return jax.shard_map(
        local,
        mesh=mesh,
        in_specs=placed,
        out_specs=(P("grp", ("role", "tp")), P("grp", ("role", "tp"))),
        check_vma=False,
    )
```

profile of v0, /device:TPU:0, one launch (start us, length us, event | category | flops | bytes accessed | tf_op | source)
XLA Modules:
  0.0 172.5 jit_solution(14774596593833444122)
XLA Ops:
  7.2 0.9 reshape.146
  8.2 0.8 reshape.137
  8.9 1.0 reshape.131
  10.2 0.4 copy-done.2
  10.7 1.6 copy.52
  12.4 1.4 fusion.37
  14.0 0.3 fusion.19
  14.4 0.7 copy.58
  15.1 1.6 copy.57
  16.8 2.1 %fusion.13 = bf16[32,2,8,64]{3,2,1,0:T(8,128)(2,1)} fusion(bf16[32,128,2,64]{1,3,2,0:T(8,128)(2,1)S(1)} %bitcast.66, f32[32,2,8,128]{3,2,1,0:T(8,128)S(1)} %get-tuple-element.9, f32[32,2,64]{2,1,0:T(2,128)S(1)} %reshape.137, f32[32,2,8]{2,1,0:T(2,128)} %copy.58, f32[32,2,8]{2,1,0:T(2,128)S(1)} %copy.56, f32[32,2,8]{2,1,0:T(2,128)S(1)} %copy.54, ...), kind=kOutput, calls=%fused_computation.15 | convolution fusion | flops 8749056 | bytes 1402880 | tf_op jit(solution)/shard_map/tkgs,tskd->tkgd/dot_general | solution.py:42
  18.9 1.0 convert_element_type.74
  20.0 5.2 %convolution_convert_fusion.2 = bf16[32,2880]{1,0:T(8,128)(2,1)} fusion(bf16[32,1024]{1,0:T(8,128)(2,1)S(1)} %convert_element_type.74, bf16[1024,2880]{0,1:T(8,128)(2,1)} %param.23), kind=kOutput, calls=%fused_computation.4 | convolution fusion | flops 188835840 | bytes 6148096 | tf_op jit(solution)/shard_map/dot_general | solution.py:105
  25.6 6.9 %all-gather = bf16[4,720,32]{1,2,0:T(8,128)(2,1)S(1)} all-gather(bf16[1,720,32]{1,2,0:T(8,128)(2,1)S(1)} %bitcast.68), channel_id=1, replica_groups=mesh['role'=2,'grp'=8,'tp'=2] {'role','tp'}, dimensions={0}, use_global_device_ids=true | all-gather | bytes 230400 | tf_op jit(solution)/shard_map/all_gather | solution.py:106
  32.6 0.2 reshape.140
  32.9 27.2 %all-reduce.2.cloned.1.call-done = bf16[32,2880]{1,0:T(8,128)(2,1)} async-done(((bf16[32,2880]{1,0:T(8,128)(2,1)}), bf16[32,2880]{1,0:T(8,128)(2,1)}) %all-reduce.2.cloned.1.call-update) | async-done | bytes 184336 | tf_op jit(solution)/shard_map/psum | solution.py:108
  60.0 1.1 multiply_reduce_fusion
  61.1 0.7 copy-done.1
  62.0 0.2 fusion.25
  62.2 5.7 %psum.15 = f32[32,8]{0,1:T(8,128)S(1)} all-reduce(f32[32,8]{0,1:T(8,128)S(1)} %fusion.25), channel_id=1, replica_groups=mesh['role'=2,'grp'=8,'tp'=2] {'role','tp'}, use_global_device_ids=true, to_apply=%region_7.8 | all-reduce | flops 256 | bytes 2048 | tf_op jit(solution)/shard_map/psum | solution.py:113
  68.4 1.3 convolution_convert_fusion.1
  69.7 1.4 reshape.135
  71.1 33.4 %all_to_all.10 = bf16[8,18,2880]{2,1,0:T(8,128)(2,1)} all-to-all(bf16[8,18,2880]{2,1,0:T(8,128)(2,1)S(1)} %reshape.135), channel_id=1, replica_groups=mesh['role'=2,'grp'=8,'tp'=2] {'grp'}, dimensions={0} | all-to-all | bytes 1658880 | tf_op jit(solution)/shard_map/all_to_all | solution.py:125
  104.6 1.7 reshape.136
  106.3 2.6 %fusion.4 = f32[144,360]{1,0:T(8,128)S(1)} fusion(bf16[144,2880]{1,0:T(8,128)(2,1)S(1)} %reshape.136, bf16[1,2880,360]{1,2,0:T(8,128)(2,1)} %param.27), kind=kOutput, calls=%fused_computation.8 | convolution fusion | flops 298598400 | bytes 3110400 | tf_op jit(solution)/shard_map/dot_general | solution.py:75
  108.9 0.8 fusion.14
  109.8 0.8 convolution_convert_fusion
  110.6 30.5 %all_to_all.11 = bf16[8,18,2880]{2,1,0:T(8,128)(2,1)S(1)} all-to-all(bf16[8,18,2880]{2,1,0:T(8,128)(2,1)S(1)} %convolution_convert_fusion), channel_id=1, replica_groups=mesh['role'=2,'grp'=8,'tp'=2] {'grp'}, dimensions={0} | all-to-all | bytes 1658880 | tf_op jit(solution)/shard_map/all_to_all | solution.py:82
  141.1 0.8 fusion
  141.9 1.2 copy.66
  143.1 1.6 dynamic-slice_convert_fusion
  144.7 19.3 %reduce-scatter.4.cloned.1.call-done = bf16[720,32]{1,0:T(8,128)(2,1)} async-done(((bf16[2880,32]{1,0:T(8,128)(2,1)}), bf16[720,32]{1,0:T(8,128)(2,1)}) %reduce-scatter.4.cloned.1.call-update) | async-done | bytes 46096
  164.0 1.7 copy.67
  (49 shorter events, 1.8 us)
Async XLA Ops:
  7.2 102.6 %copy-start = (bf16[1,360,2880]{2,1,0:T(8,128)(2,1)S(1)}, bf16[1,360,2880]{2,1,0:T(8,128)(2,1)}, u32[]{:S(2)}) copy-start(bf16[1,360,2880]{2,1,0:T(8,128)(2,1)} %param.29) | copy-start | bytes 6220804
  7.2 5.1 %copy-start.8 = (s32[32]{0:T(128)S(1)}, s32[32]{0:T(128)}, u32[]{:S(2)}) copy-start(s32[32]{0:T(128)} %param.21) | copy-start | bytes 388
  7.2 5.1 %copy-start.7 = (s32[32]{0:T(128)S(1)}, s32[32]{0:T(128)}, u32[]{:S(2)}) copy-start(s32[32]{0:T(128)} %param.20) | copy-start | bytes 388
  7.2 52.8 %all-reduce.2.cloned.1.call-start = ((), (), s32[]{:S(2)}) async-start(), calls=%async_computation.3 | async-start | bytes 376832 | tf_op jit(solution)/shard_map/psum | solution.py:108
  10.0 0.6 copy-start.2
  19.9 5.3 %copy-start.4 = (s32[32,4]{0,1:T(4,128)S(1)}, s32[32,4]{0,1:T(4,128)}, u32[]{:S(2)}) copy-start(s32[32,4]{0,1:T(4,128)} %param.26) | copy-start | bytes 1540
  20.0 5.6 %copy-start.3 = (bf16[32,720]{1,0:T(8,128)(2,1)S(1)}, bf16[32,720]{1,0:T(8,128)(2,1)}, u32[]{:S(2)}) copy-start(bf16[32,720]{1,0:T(8,128)(2,1)} %param.22) | copy-start | bytes 138244
  25.2 36.7 %copy-start.6 = (f32[2880]{0:T(1024)S(1)}, f32[2880]{0:T(1024)}, u32[]{:S(2)}) copy-start(f32[2880]{0:T(1024)} %param.24) | copy-start | bytes 34564
  25.2 36.8 %copy-start.5 = (bf16[720,8]{0,1:T(8,128)(2,1)S(1)}, bf16[720,8]{0,1:T(8,128)(2,1)}, u32[]{:S(2)}) copy-start(bf16[720,8]{0,1:T(8,128)(2,1)} %param.25) | copy-start | bytes 34564
  25.2 138.8 %reduce-scatter.4.cloned.1.call-start = ((), (), s32[]{:S(2)}) async-start(), calls=%async_computation.4 | async-start | bytes 921600
  61.1 0.8 copy-start.1
  106.3 2.6 %copy-start.9 = (bf16[1,2880,360]{1,2,0:T(8,128)(2,1)S(1)}, bf16[1,2880,360]{1,2,0:T(8,128)(2,1)}, u32[]{:S(2)}) copy-start(bf16[1,2880,360]{1,2,0:T(8,128)(2,1)} %param.28) | copy-start | bytes 6220804
Sparse Core Ops, SparseCore 0:
  25.3 34.6 all-reduce.1
  143.2 20.7 reduce-scatter.3
where the time goes:
time: 173 us
  blocking collectives  76.6 us (44%)
  waiting for transfers between devices  46.5 us (27%)
  local copies, waits for them, and re-layouts  17.7 us (10%)
  matrix products  15.4 us (9%)
  between operations  14.3 us (8%)
  other arithmetic  1.84 us (1%)
    all_to_all x1, blocking collectives, local(): lax.all_to_all(outbound, 'grp', split_axis=0, concat_axis=0, tiled=True)  33.4 us
    all_to_all x1, blocking collectives, serve(): lax.all_to_all(rounded, 'grp', split_axis=0, concat_axis=0, tiled=True)  30.5 us
    psum x1, waiting for transfers between devices, local(): lax.psum(projected.astype(jnp.bfloat16), ('role', 'tp')).astype(jnp.float32)  27.2 us
    unnamed x3, waiting for transfers between devices  19.3 us
    unnamed x24, local copies, waits for them, and re-layouts  7.26 us
    all_gather x1, blocking collectives, local(): lax.all_gather(residual, ('role', 'tp'), axis=1, tiled=True)  6.87 us
    psum x1, blocking collectives, local(): lax.psum(jnp.dot(own_normed, router, preferred_element_type=jnp.float32),...  5.74 us
    dot_general x1, matrix products, local(): projected = jnp.dot(heads_out, out_proj, preferred_element_type=jnp.float32)  5.22 us
  transfers between devices with their start and end apart: 2, of which 2 were waited for; matrix products, arithmetic and copies ran while one was open for 1% of the time, Pallas kernels for 0%

commit v1 on v0

v1 whole, which is shorter than its diff:
```python
import math

import jax
import jax.numpy as jnp
import numpy as np
from jax import lax
from jax.sharding import PartitionSpec as P

HEADS = 64
KV_HEADS = 8
HD = 64


epsilon = 1e-05


def attend(q_new, k_new, v_new, k_cache, v_cache, cache_len, cycle_start):
    tokens = q_new.shape[0]
    window = k_cache.shape[1]
    kv_local = k_new.shape[1] // HD
    grouped = HEADS // KV_HEADS
    queries = q_new.reshape(tokens, kv_local, grouped, HD)
    cached_keys = k_cache.reshape(tokens, window, kv_local, HD)
    cached_values = v_cache.reshape(tokens, window, kv_local, HD)
    own_key = k_new.reshape(tokens, kv_local, HD)
    own_value = v_new.reshape(tokens, kv_local, HD)
    factor = HD ** (-0.5)
    scores = (
        jnp.einsum("tkgd,tskd->tkgs", queries, cached_keys, preferred_element_type=jnp.float32)
        * factor
    )
    own_score = (
        jnp.einsum("tkgd,tkd->tkg", queries, own_key, preferred_element_type=jnp.float32) * factor
    )
    positions = jnp.arange(window, dtype=jnp.int32)
    usable = (positions[None, :] - cycle_start[:, None]) % window < cache_len[:, None]
    usable = usable[:, None, None, :]
    masked = jnp.where(usable, scores, -1e30)
    highest = jnp.maximum(jnp.max(masked, axis=3), own_score)
    lifted = jnp.where(usable, jnp.exp(masked - highest[..., None]), 0.0)
    own_lift = jnp.exp(own_score - highest)
    denominator = jnp.sum(lifted, axis=3) + own_lift
    weights = (lifted / denominator[..., None]).astype(jnp.bfloat16)
    own_weight = (own_lift / denominator).astype(jnp.bfloat16)
    combined = jnp.einsum(
        "tkgs,tskd->tkgd", weights, cached_values, preferred_element_type=jnp.float32
    )
    combined = (
        combined
        + own_weight.astype(jnp.float32)[..., None] * own_value.astype(jnp.float32)[:, :, None, :]
    )
    return combined.reshape(tokens, -1).astype(jnp.bfloat16)


def split3(x):
    high = lax.reduce_precision(x, 8, 7)
    rest = x - high
    middle = lax.reduce_precision(rest, 8, 7)
    low = rest - middle
    return [part.astype(jnp.bfloat16) for part in (high, middle, low)]


def swap_table(mesh, grp_of, role_flip, tp_flip):
    names = mesh.axis_names
    sizes = [mesh.shape[n] for n in names]
    pairs = []
    for flat in range(math.prod(sizes)):
        at = dict(zip(names, [int(v) for v in np.unravel_index(flat, sizes)]))
        to = dict(
            role=at["role"] ^ role_flip, tp=at["tp"] ^ tp_flip, grp=grp_of(at["grp"])
        )
        pairs.append((flat, int(np.ravel_multi_index([to[n] for n in names], sizes))))
    return pairs


def make_local(mesh):
    n_role, n_grp, n_tp = (mesh.shape[n] for n in ("role", "grp", "tp"))
    n_near = 2 if n_grp % 2 == 0 else 1
    n_far = n_grp // n_near
    xor_far = n_far & (n_far - 1) == 0
    names = mesh.axis_names

    def send(x, near=0, role=0, tp=0):
        return lax.ppermute(x, names, swap_table(mesh, lambda g: g ^ near, role, tp))

    def send_far(x, k):
        def grp_of(g):
            far, near = divmod(g, n_near)
            return (far ^ k if xor_far else (far + k) % n_far) * n_near + near

        return lax.ppermute(x, names, swap_table(mesh, grp_of, 0, 0))

    def local(
        q_new, k_new, v_new, k_cache, v_cache, cache_len, cycle_start, residual,
        out_proj, norm_gain, router, route_ids, w_gate, w_up, w_down,
    ):
        role, grp, tp = (lax.axis_index(n) for n in ("role", "grp", "tp"))
        tokens, quarter = residual.shape
        width = quarter * n_role * n_tp
        topk = route_ids.shape[1]
        experts = n_grp * w_gate.shape[0]
        cap = max(3, tokens * topk // experts + 2)
        far, near = grp // n_near, grp % n_near
        share = role * n_tp + tp
        heads_out = attend(q_new, k_new, v_new, k_cache, v_cache, cache_len, cycle_start)
        projected = jnp.dot(heads_out, out_proj, preferred_element_type=jnp.float32)
        blocks = projected.reshape(tokens, n_role, n_tp, quarter)

        def block(i, l):
            mine = lax.dynamic_index_in_dim(blocks, role ^ i, 1, keepdims=False)
            return lax.dynamic_index_in_dim(mine, tp ^ l, 1, keepdims=False)

        stream = residual.astype(jnp.float32) + block(0, 0)
        for i, l in ((1, 0), (1, 1), (0, 1)):
            stream = stream + send(block(i, l).astype(jnp.bfloat16), role=i, tp=l).astype(jnp.float32)
        attended = stream.astype(jnp.bfloat16)
        gain = lax.dynamic_slice_in_dim(norm_gain, share * quarter, quarter, 0)
        scaled = (stream * gain).astype(jnp.bfloat16)
        squares = jnp.sum(stream * stream, axis=1, keepdims=True)
        logits = jnp.dot(scaled, router, preferred_element_type=jnp.float32)
        named = route_ids[:, :, None] == jnp.arange(experts, dtype=jnp.int32)
        chosen = jnp.sum(jnp.where(named, logits[:, None, :], 0.0), axis=2)
        stats = split3(jnp.concatenate([squares, chosen], axis=1))
        packed = jnp.concatenate([scaled, route_ids.astype(jnp.bfloat16)] + stats, axis=1)
        lanes = -(-packed.shape[1] // 128) * 128
        packed = jnp.pad(packed, ((0, 0), (0, lanes - packed.shape[1])))
        gathered = jnp.stack([packed] + [send_far(packed, k) for k in range(1, n_far)])
        ids = gathered[:, :, quarter : quarter + topk].astype(jnp.float32)
        rows = {}
        selects = []
        for j in range(n_near):
            expert = (far * n_near + (near ^ j)).astype(jnp.float32)
            hit = jnp.sum((ids == expert).astype(jnp.int32), axis=2)
            rank = jnp.cumsum(hit, axis=1) - hit
            select = (hit[:, None, :] > 0) & (
                rank[:, None, :] == jnp.arange(cap, dtype=jnp.int32)[:, None]
            )
            select = select.astype(jnp.bfloat16)
            selects.append(select)
            rows[j] = jnp.einsum(
                "kct,ktw->kcw", select, gathered, preferred_element_type=jnp.float32
            ).astype(jnp.bfloat16).reshape(n_far * cap, lanes)
        arrived = {(0, 0): rows[0]}
        for j in range(n_near):
            for i in range(n_role):
                if (j, i) != (0, 0):
                    arrived[j, i] = send(rows[j], near=j, role=i)
        half = jnp.stack(
            [jnp.concatenate([arrived[j, i] for j in range(n_near)], 0) for i in range(n_role)]
        )
        other = send(half, tp=1)
        both = jnp.stack([half, other], 1)
        both = jnp.where(role == 0, both, both[::-1])
        both = jnp.where(tp == 0, both, both[:, ::-1])
        quarters = both.reshape(n_role * n_tp, -1, lanes)
        tail = jnp.sum(quarters[:, :, quarter + topk :].astype(jnp.float32), axis=0)
        own_ids = quarters[0, :, quarter : quarter + topk].astype(jnp.float32)
        n_stat = 1 + topk
        total = sum(tail[:, p * n_stat : (p + 1) * n_stat] for p in range(3))
        scale = lax.rsqrt(total[:, :1] / width + epsilon)
        picked = total[:, 1:] * scale
        lifted = jnp.exp(picked - jnp.max(picked, axis=1, keepdims=True))
        mine = jnp.where(own_ids == grp.astype(jnp.float32), lifted, 0.0)
        weight = jnp.sum(mine, axis=1, keepdims=True) / jnp.sum(lifted, axis=1, keepdims=True)
        inputs = jnp.concatenate([quarters[p, :, :quarter] for p in range(n_role * n_tp)], axis=1)
        gate_lin = jnp.dot(inputs, w_gate[0], preferred_element_type=jnp.float32) * scale
        up_lin = jnp.dot(inputs, w_up[0], preferred_element_type=jnp.float32) * scale
        activated = (gate_lin * jax.nn.sigmoid(1.702 * gate_lin) * (up_lin + 1.0)).astype(
            jnp.bfloat16
        )
        result = jnp.dot(activated, w_down[0], preferred_element_type=jnp.float32) * weight
        blocks_out = result.astype(jnp.bfloat16).reshape(-1, n_role, n_tp, quarter)
        blocks_out = jnp.where(role == 0, blocks_out, blocks_out[:, ::-1])
        blocks_out = jnp.where(tp == 0, blocks_out, blocks_out[:, :, ::-1])
        acc = blocks_out[:, :, 0].astype(jnp.float32) + send(blocks_out[:, :, 1], tp=1).astype(
            jnp.float32
        )
        acc = acc.astype(jnp.bfloat16).reshape(n_near, n_far * cap, n_role, quarter)
        back = []
        for j in range(n_near):
            total_rows = 0.0
            for i in range(n_role):
                piece = acc[j, :, i]
                if (j, i) != (0, 0):
                    piece = send(piece, near=j, role=i)
                total_rows = total_rows + piece.astype(jnp.float32)
            back.append(total_rows.astype(jnp.bfloat16).reshape(n_far, cap, quarter))
        spread = sum(
            jnp.einsum("kct,kcw->ktw", s, b, preferred_element_type=jnp.float32)
            for s, b in zip(selects, back)
        ).astype(jnp.bfloat16)
        mix = spread[0].astype(jnp.float32)
        for k in range(1, n_far):
            mix = mix + send_far(spread[k], k if xor_far else n_far - k).astype(jnp.float32)
        return (attended, mix.astype(jnp.bfloat16))

    return local


def solution(mesh):
    placed = (
        P("grp", ("role", "tp")),
        P("grp", ("role", "tp")),
        P("grp", ("role", "tp")),
        P("grp", None, ("role", "tp")),
        P("grp", None, ("role", "tp")),
        P("grp"),
        P("grp"),
        P("grp", ("role", "tp")),
        P(("role", "tp"), None),
        P(),
        P(("role", "tp"), None),
        P("grp", None),
        P("grp", None, ("role", "tp")),
        P("grp", None, ("role", "tp")),
        P("grp", ("role", "tp"), None),
    )
    return jax.shard_map(
        make_local(mesh),
        mesh=mesh,
        in_specs=placed,
        out_specs=(P("grp", ("role", "tp")), P("grp", ("role", "tp"))),
        check_vma=False,
    )
```

time: 173 us -> 80.9 us (0.47)
  blocking collectives: 76.6 us -> 0 us
  waiting for transfers between devices: 46.5 us -> 24.3 us
  starting transfers between devices: 0.08 us -> 18.7 us
  between operations: 14.3 us -> 1.08 us
  other arithmetic: 1.84 us -> 4.34 us
    all_to_all x2 -> x0, blocking collectives: 64 us -> none  [the longest x1 33.4 us: local(): lax.all_to_all(outbound, 'grp', split_axis=0, concat_axis=0, tiled=True)]
    psum x1 -> x0, waiting for transfers between devices: 27.2 us -> none  [local(): lax.psum(projected.astype(jnp.bfloat16), ('role', 'tp')).astype(jnp.float32)]
    ppermute x0 -> x17, waiting for transfers between devices: none -> 24.3 us  [the longest x11 14.5 us: send(): lax.ppermute(x, names, swap_table(mesh, lambda g: g ^ near, role, tp))]
    unnamed x3 -> x0, waiting for transfers between devices: 19.3 us -> none
    ppermute x0 -> x17, starting transfers between devices: none -> 18.7 us  [the longest x11 10.7 us: send(): lax.ppermute(x, names, swap_table(mesh, lambda g: g ^ near, role, tp))]
    all_gather x1 -> x0, blocking collectives: 6.87 us -> none  [local(): lax.all_gather(residual, ('role', 'tp'), axis=1, tiled=True)]
    psum x1 -> x0, blocking collectives: 5.74 us -> none  [local(): lax.psum(jnp.dot(own_normed, router, preferred_element_type=jnp.float32),...]
    unnamed x24 -> x16, local copies, waits for them, and re-layouts: 7.26 us -> 3.7 us
  transfers between devices with their start and end apart: 2 -> 17, of which waited for: 2 -> 15; matrix products, arithmetic and copies ran while one was open for 1% -> 1% of each run, Pallas kernels for 0% -> 0%
where the time goes in v1:
time: 80.9 us; the launch traced here: 80.4 us
  waiting for transfers between devices  24.3 us (30%)
  starting transfers between devices  18.7 us (23%)
  local copies, waits for them, and re-layouts  16.3 us (20%)
  matrix products  15.7 us (19%)
  other arithmetic  4.34 us (5%)
  between operations  1.08 us (1%)
    ppermute x11, waiting for transfers between devices, send(): lax.ppermute(x, names, swap_table(mesh, lambda g: g ^ near, role, tp))  14.5 us
    ppermute x11, starting transfers between devices, send(): lax.ppermute(x, names, swap_table(mesh, lambda g: g ^ near, role, tp))  10.7 us
    ppermute x6, waiting for transfers between devices, send_far(): return lax.ppermute(x, names, swap_table(mesh, grp_of, 0, 0))  9.79 us
    ppermute x6, starting transfers between devices, send_far(): return lax.ppermute(x, names, swap_table(mesh, grp_of, 0, 0))  8 us
    dot_general x1, matrix products, local(): projected = jnp.dot(heads_out, out_proj, preferred_element_type=jnp.float32)  4.41 us
    dot_general x1, matrix products, local(): jnp.dot(activated, w_down[0], preferred_element_type=jnp.float32) * weight  4.22 us
    reshape x2, local copies, waits for them, and re-layouts, local(): blocks_out = result.astype(jnp.bfloat16).reshape(-1, n_role, n_tp, quarter)  3.79 us
    unnamed x16, local copies, waits for them, and re-layouts  3.7 us
  transfers between devices with their start and end apart: 17, of which 15 were waited for; matrix products, arithmetic and copies ran while one was open for 1% of the time, Pallas kernels for 0%

profile of v1, /device:TPU:0, one launch (start us, length us, event | category | flops | bytes accessed | tf_op | source)
XLA Modules:
  0.0 80.4 jit_solution(10542047756455026516)
XLA Ops:
  2.4 1.0 %reshape.148 = bf16[32,2,8,64]{3,2,1,0:T(8,128)(2,1)S(1)} reshape(bf16[32,1024]{1,0:T(8,128)(2,1)} %param.15) | data formatting | bytes 131072 | tf_op jit(solution)/shard_map/reshape | solution.py:22
  4.1 1.6 %copy.83 = bf16[32,128,128]{1,2,0:T(8,128)(2,1)S(1)} copy(bf16[32,128,128]{2,1,0:T(8,128)(2,1)} %param.18) | data formatting | bytes 2097152 | tf_op args[3]
  5.9 1.4 %fusion.90 = (f32[32,2,8]{2,1,0:T(2,128)S(1)}, f32[32,2,8,128]{3,2,1,0:T(8,128)S(1)}) fusion(bf16[32,2,8,64]{3,2,1,0:T(8,128)(2,1)} %copy-done.1, bf16[32,128,2,64]{1,3,2,0:T(8,128)(2,1)S(1)} %bitcast.142, pred[32,128]{1,0:T(8,128)(4,1)S(1)} %fusion.75), kind=kOutput, calls=%fused_computation.145 | convolution fusion | flops 8584704 | bytes 1382400 | tf_op jit(solution)/shard_map/tkgd,tskd->tkgs/dot_general | solution.py:29
  8.6 1.6 %copy.88 = bf16[32,128,128]{1,2,0:T(8,128)(2,1)S(1)} copy(bf16[32,128,128]{2,1,0:T(8,128)(2,1)} %param.19) | data formatting | bytes 2097152 | tf_op args[4]
  10.2 2.1 %fusion.20 = bf16[32,2,8,64]{3,2,1,0:T(8,128)(2,1)} fusion(bf16[32,128,2,64]{1,3,2,0:T(8,128)(2,1)S(1)} %bitcast.145, f32[32,2,8,128]{3,2,1,0:T(8,128)S(1)} %get-tuple-element.33, f32[32,2,64]{2,1,0:T(2,128)S(1)} %reshape.159, f32[32,2,8]{2,1,0:T(2,128)} %copy.89, f32[32,2,8]{2,1,0:T(2,128)S(1)} %copy.87, f32[32,2,8]{2,1,0:T(2,128)S(1)} %copy.85, ...), kind=kOutput, calls=%fused_computation.22 | convolution fusion | flops 8749056 | bytes 1402880 | tf_op jit(solution)/shard_map/tkgs,tskd->tkgd/dot_general | solution.py:45
  12.3 1.0 %reshape.165 = bf16[32,1024,1,1]{1,0,2,3:T(8,128)(2,1)S(1)} reshape(bf16[32,2,8,64]{3,2,1,0:T(8,128)(2,1)} %fusion.20) | data formatting | bytes 131072 | tf_op jit(solution)/shard_map/convert_element_type | solution.py:52
  13.4 4.4 %fusion.52 = f32[32,2,2,720]{3,0,2,1:T(8,128)S(1)} fusion(bf16[2,2,720,1024]{3,2,1,0:T(8,128)(2,1)} %bitcast.138, bf16[32,1024,1,1]{1,0,2,3:T(8,128)(2,1)S(1)} %reshape.165), kind=kOutput, calls=%fused_computation.87 | convolution fusion | flops 188743680 | bytes 6332416 | tf_op jit(solution)/shard_map/dot_general | solution.py:106
  17.9 3.0 %collective-permute-start = (bf16[32,720]{1,0:T(8,128)(2,1)S(1)}, bf16[32,720]{1,0:T(8,128)(2,1)S(1)}, u32[]{:S(2)}, u32[]{:S(2)}) collective-permute-start(bf16[32,720]{1,0:T(8,128)(2,1)S(1)} %get-tuple-element.17), channel_id=1, source_target_pairs={{0,16},{1,17},{2,18},{3,19},{4,20},{5,21},{6,22},{7,23},{8,24},{9,... | collective-permute-start | bytes 138248 | tf_op jit(solution)/shard_map/ppermute | solution.py:84
  23.0 1.4 %collective-permute-done.1 = bf16[32,720]{1,0:T(8,128)(2,1)S(1)} collective-permute-done((bf16[32,720]{1,0:T(8,128)(2,1)S(1)}, bf16[32,720]{1,0:T(8,128)(2,1)S(1)}, u32[]{:S(2)}, u32[]{:S(2)}) %collective-permute-start.1) | collective-permute-done | bytes 46112 | tf_op jit(solution)/shard_map/ppermute | solution.py:84
  25.8 2.7 %collective-permute-start.4 = (bf16[32,768]{1,0:T(8,128)(2,1)S(1)}, bf16[32,768]{1,0:T(8,128)(2,1)S(1)}, u32[]{:S(2)}, u32[]{:S(2)}) collective-permute-start(bf16[32,768]{1,0:T(8,128)(2,1)S(1)} %get-tuple-element.26), channel_id=1, source_target_pairs={{0,8},{1,9},{2,10},{3,11},{4,12},{5,13},{6,14},{7,15},{8,0},{9,1},... | collective-permute-start | bytes 147464 | tf_op jit(solution)/shard_map/ppermute | solution.py:91
  28.5 1.6 %collective-permute-start.3 = (bf16[32,768]{1,0:T(8,128)(2,1)S(1)}, bf16[32,768]{1,0:T(8,128)(2,1)S(1)}, u32[]{:S(2)}, u32[]{:S(2)}) collective-permute-start(bf16[32,768]{1,0:T(8,128)(2,1)S(1)} %get-tuple-element.26), channel_id=1, source_target_pairs={{0,4},{1,5},{2,6},{3,7},{4,0},{5,1},{6,2},{7,3},{8,12},{9,13},{10,... | collective-permute-start | bytes 147464 | tf_op jit(solution)/shard_map/ppermute | solution.py:91
  30.9 1.6 %collective-permute-done.3 = bf16[32,768]{1,0:T(8,128)(2,1)S(1)} collective-permute-done((bf16[32,768]{1,0:T(8,128)(2,1)S(1)}, bf16[32,768]{1,0:T(8,128)(2,1)S(1)}, u32[]{:S(2)}, u32[]{:S(2)}) %collective-permute-start.3) | collective-permute-done | bytes 49184 | tf_op jit(solution)/shard_map/ppermute | solution.py:91
  32.5 3.4 %collective-permute-done.5 = bf16[32,768]{1,0:T(8,128)(2,1)S(1)} collective-permute-done((bf16[32,768]{1,0:T(8,128)(2,1)S(1)}, bf16[32,768]{1,0:T(8,128)(2,1)S(1)}, u32[]{:S(2)}, u32[]{:S(2)}) %collective-permute-start.5) | collective-permute-done | bytes 49184 | tf_op jit(solution)/shard_map/ppermute | solution.py:91
  36.9 2.1 %collective-permute-start.8 = (bf16[72,768]{1,0:T(8,128)(2,1)S(1)}, bf16[72,768]{1,0:T(8,128)(2,1)S(1)}, u32[]{:S(2)}, u32[]{:S(2)}) collective-permute-start(bf16[72,768]{1,0:T(8,128)(2,1)S(1)} %reshape.153), channel_id=1, source_target_pairs={{0,18},{1,19},{2,16},{3,17},{4,22},{5,23},{6,20},{7,21},{8,26},{9,... | collective-permute-start | bytes 331784 | tf_op jit(solution)/shard_map/ppermute | solution.py:84
  39.7 1.0 %collective-permute-start.7 = (bf16[72,768]{1,0:T(8,128)(2,1)S(1)}, bf16[72,768]{1,0:T(8,128)(2,1)S(1)}, u32[]{:S(2)}, u32[]{:S(2)}) collective-permute-start(bf16[72,768]{1,0:T(8,128)(2,1)S(1)} %reshape.152), channel_id=1, source_target_pairs={{0,16},{1,17},{2,18},{3,19},{4,20},{5,21},{6,22},{7,23},{8,24},{9,... | collective-permute-start | bytes 331784 | tf_op jit(solution)/shard_map/ppermute | solution.py:84
  40.7 3.6 %collective-permute-done.6 = bf16[72,768]{1,0:T(8,128)(2,1)S(1)} collective-permute-done((bf16[72,768]{1,0:T(8,128)(2,1)S(1)}, bf16[72,768]{1,0:T(8,128)(2,1)S(1)}, u32[]{:S(2)}, u32[]{:S(2)}) %collective-permute-start.6) | collective-permute-done | bytes 110624 | tf_op jit(solution)/shard_map/ppermute | solution.py:84
  44.7 1.8 %collective-permute-done.9 = bf16[2,144,768]{2,1,0:T(8,128)(2,1)S(1)} collective-permute-done((bf16[2,144,768]{2,1,0:T(8,128)(2,1)S(1)}, bf16[2,144,768]{2,1,0:T(8,128)(2,1)S(1)}, u32[]{:S(2)}, u32[]{:S(2)}) %collective-permute-start.9) | collective-permute-done | bytes 442400 | tf_op jit(solution)/shard_map/ppermute | solution.py:84
  48.6 1.5 %concatenate.19 = bf16[144,2880]{1,0:T(8,128)(2,1)S(1)} concatenate(bf16[144,720]{1,0:T(8,128)(2,1)} %get-tuple-element.11, bf16[144,720]{1,0:T(8,128)(2,1)} %get-tuple-element.10, bf16[144,720]{1,0:T(8,128)(2,1)S(1)} %get-tuple-element.9, bf16[144,720]{1,0:T(8,128)(2,1)S(1)} %get-tuple-element.8), dimensions={1} | concatenate | bytes 1658880 | tf_op jit(solution)/shard_map/concatenate | solution.py:165
  50.1 2.4 %fusion.8 = f32[144,360]{1,0:T(8,128)S(1)} fusion(bf16[144,2880]{1,0:T(8,128)(2,1)S(1)} %concatenate.19, bf16[1,2880,360]{1,2,0:T(8,128)(2,1)} %param.27, f32[144]{0:T(256)S(1)} %fusion.50), kind=kOutput, calls=%fused_computation.16 | convolution fusion | flops 298650240 | bytes 3110976 | tf_op jit(solution)/shard_map/dot_general | solution.py:166
  52.6 4.2 %fusion = bf16[144,2880]{1,0:T(8,128)(2,1)} fusion(bf16[1,360,2880]{2,1,0:T(8,128)(2,1)S(1)} %copy-done, bf16[144,2880]{1,0:T(8,128)(2,1)S(1)} %concatenate.19, bf16[1,2880,360]{1,2,0:T(8,128)(2,1)} %param.28, f32[144]{0:T(256)S(1)} %div.45, f32[144,360]{1,0:T(8,128)S(1)} %fusion.8, f32[144]{0:T(256)S(1)} %fusion.50), kind=kOutput, calls=%fused_computation.1 | convolution fusion | flops 598492800 | bytes 6014592 | tf_op jit(solution)/shard_map/dot_general | solution.py:171
  56.8 3.7 %reshape.155 = bf16[144,2,2,720]{3,2,1,0:T(2,128)(2,1)S(1)} reshape(bf16[144,2880]{1,0:T(8,128)(2,1)} %fusion) | data formatting | bytes 1658880 | tf_op jit(solution)/shard_map/reshape | solution.py:172
  61.1 1.7 %collective-permute-done.10 = bf16[144,2,720]{2,0,1:T(8,128)(2,1)S(1)} collective-permute-done((bf16[144,2,720]{2,0,1:T(8,128)(2,1)S(1)}, bf16[144,2,720]{2,0,1:T(8,128)(2,1)S(1)}, u32[]{:S(2)}, u32[]{:S(2)}) %collective-permute-start.10) | collective-permute-done | bytes 414752 | tf_op jit(solution)/shard_map/ppermute | solution.py:84
  62.9 1.0 %collective-permute-start.11 = (bf16[72,720]{1,0:T(8,128)(2,1)S(1)}, bf16[72,720]{1,0:T(8,128)(2,1)S(1)}, u32[]{:S(2)}, u32[]{:S(2)}) collective-permute-start(bf16[72,720]{1,0:T(8,128)(2,1)S(1)} %get-tuple-element.12), channel_id=1, source_target_pairs={{0,16},{1,17},{2,18},{3,19},{4,20},{5,21},{6,22},{7,23},{8,24},{9,... | collective-permute-start | bytes 311048 | tf_op jit(solution)/shard_map/ppermute | solution.py:84
  64.0 1.5 %collective-permute-start.12 = (bf16[72,720]{1,0:T(8,128)(2,1)S(1)}, bf16[72,720]{1,0:T(8,128)(2,1)S(1)}, u32[]{:S(2)}, u32[]{:S(2)}) collective-permute-start(bf16[72,720]{1,0:T(8,128)(2,1)S(1)} %get-tuple-element.13), channel_id=1, source_target_pairs={{0,2},{1,3},{2,0},{3,1},{4,6},{5,7},{6,4},{7,5},{8,10},{9,11},{10,... | collective-permute-start | bytes 311048 | tf_op jit(solution)/shard_map/ppermute | solution.py:84
  65.5 1.0 %collective-permute-start.13 = (bf16[72,720]{1,0:T(8,128)(2,1)S(1)}, bf16[72,720]{1,0:T(8,128)(2,1)S(1)}, u32[]{:S(2)}, u32[]{:S(2)}) collective-permute-start(bf16[72,720]{1,0:T(8,128)(2,1)S(1)} %get-tuple-element.14), channel_id=1, source_target_pairs={{0,18},{1,19},{2,16},{3,17},{4,22},{5,23},{6,20},{7,21},{8,26},{9,... | collective-permute-start | bytes 311048 | tf_op jit(solution)/shard_map/ppermute | solution.py:84
  66.5 2.1 %collective-permute-done.11 = bf16[72,720]{1,0:T(8,128)(2,1)S(1)} collective-permute-done((bf16[72,720]{1,0:T(8,128)(2,1)S(1)}, bf16[72,720]{1,0:T(8,128)(2,1)S(1)}, u32[]{:S(2)}, u32[]{:S(2)}) %collective-permute-start.11) | collective-permute-done | bytes 103712 | tf_op jit(solution)/shard_map/ppermute | solution.py:84
  68.7 1.5 %collective-permute-done.12 = bf16[72,720]{1,0:T(8,128)(2,1)S(1)} collective-permute-done((bf16[72,720]{1,0:T(8,128)(2,1)S(1)}, bf16[72,720]{1,0:T(8,128)(2,1)S(1)}, u32[]{:S(2)}, u32[]{:S(2)}) %collective-permute-start.12) | collective-permute-done | bytes 103712 | tf_op jit(solution)/shard_map/ppermute | solution.py:84
  70.2 1.2 %collective-permute-done.13 = bf16[72,720]{1,0:T(8,128)(2,1)S(1)} collective-permute-done((bf16[72,720]{1,0:T(8,128)(2,1)S(1)}, bf16[72,720]{1,0:T(8,128)(2,1)S(1)}, u32[]{:S(2)}, u32[]{:S(2)}) %collective-permute-start.13) | collective-permute-done | bytes 103712 | tf_op jit(solution)/shard_map/ppermute | solution.py:84
  72.1 2.6 %collective-permute-start.16 = (bf16[32,720]{1,0:T(8,128)(2,1)S(1)}, bf16[32,720]{1,0:T(8,128)(2,1)S(1)}, u32[]{:S(2)}, u32[]{:S(2)}) collective-permute-start(bf16[32,720]{1,0:T(8,128)(2,1)S(1)} %get-tuple-element.21), channel_id=1, source_target_pairs={{0,12},{1,13},{2,14},{3,15},{4,8},{5,9},{6,10},{7,11},{8,4},{9,5},... | collective-permute-start | bytes 138248 | tf_op jit(solution)/shard_map/ppermute | solution.py:91
  75.6 1.2 %collective-permute-done.14 = bf16[32,720]{1,0:T(8,128)(2,1)S(1)} collective-permute-done((bf16[32,720]{1,0:T(8,128)(2,1)S(1)}, bf16[32,720]{1,0:T(8,128)(2,1)S(1)}, u32[]{:S(2)}, u32[]{:S(2)}) %collective-permute-start.14) | collective-permute-done | bytes 46112 | tf_op jit(solution)/shard_map/ppermute | solution.py:91
  76.9 1.2 %collective-permute-done.16 = bf16[32,720]{1,0:T(8,128)(2,1)S(1)} collective-permute-done((bf16[32,720]{1,0:T(8,128)(2,1)S(1)}, bf16[32,720]{1,0:T(8,128)(2,1)S(1)}, u32[]{:S(2)}, u32[]{:S(2)}) %collective-permute-start.16) | collective-permute-done | bytes 46112 | tf_op jit(solution)/shard_map/ppermute | solution.py:91
  78.1 1.6 %collective-permute-done.15 = bf16[32,720]{1,0:T(8,128)(2,1)S(1)} collective-permute-done((bf16[32,720]{1,0:T(8,128)(2,1)S(1)}, bf16[32,720]{1,0:T(8,128)(2,1)S(1)}, u32[]{:S(2)}, u32[]{:S(2)}) %collective-permute-start.15) | collective-permute-done | bytes 46112 | tf_op jit(solution)/shard_map/ppermute | solution.py:91
  (92 shorter events, 15.3 us)
Async XLA Ops:
  0.6 51.9 %copy-start = (bf16[1,360,2880]{2,1,0:T(8,128)(2,1)S(1)}, bf16[1,360,2880]{2,1,0:T(8,128)(2,1)}, u32[]{:S(2)}) copy-start(bf16[1,360,2880]{2,1,0:T(8,128)(2,1)} %param.29) | copy-start | bytes 6220804
  0.6 5.1 %copy-start.6 = (s32[32]{0:T(128)S(1)}, s32[32]{0:T(128)}, u32[]{:S(2)}) copy-start(s32[32]{0:T(128)} %param.21) | copy-start | bytes 388
  0.7 5.1 %copy-start.5 = (s32[32]{0:T(128)S(1)}, s32[32]{0:T(128)}, u32[]{:S(2)}) copy-start(s32[32]{0:T(128)} %param.20) | copy-start | bytes 388
  3.4 0.6 copy-start.1
  13.4 7.7 %copy-start.4 = (s32[32,4]{0,1:T(4,128)S(1)}, s32[32,4]{0,1:T(4,128)}, u32[]{:S(2)}) copy-start(s32[32,4]{0,1:T(4,128)} %param.26) | copy-start | bytes 1540
  13.4 11.0 %copy-start.2 = (bf16[32,720]{1,0:T(8,128)(2,1)S(1)}, bf16[32,720]{1,0:T(8,128)(2,1)}, u32[]{:S(2)}) copy-start(bf16[32,720]{1,0:T(8,128)(2,1)} %param.22) | copy-start | bytes 138244
  13.4 11.8 %copy-start.3 = (bf16[720,8]{0,1:T(8,128)(2,1)S(1)}, bf16[720,8]{0,1:T(8,128)(2,1)}, u32[]{:S(2)}) copy-start(bf16[720,8]{0,1:T(8,128)(2,1)} %param.25) | copy-start | bytes 34564
  17.9 5.1 %collective-permute-start = (bf16[32,720]{1,0:T(8,128)(2,1)S(1)}, bf16[32,720]{1,0:T(8,128)(2,1)S(1)}, u32[]{:S(2)}, u32[]{:S(2)}) collective-permute-start(bf16[32,720]{1,0:T(8,128)(2,1)S(1)} %get-tuple-element.17), channel_id=1, source_target_pairs={{0,16},{1,17},{2,18},{3,19},{4,20},{5,21},{6,22},{7,23},{8,24},{9,... | collective-permute-start | bytes 138248 | tf_op jit(solution)/shard_map/ppermute | solution.py:84
  20.9 2.1 %collective-permute-start.2 = (bf16[32,720]{1,0:T(8,128)(2,1)S(1)}, bf16[32,720]{1,0:T(8,128)(2,1)S(1)}, u32[]{:S(2)}, u32[]{:S(2)}) collective-permute-start(bf16[32,720]{1,0:T(8,128)(2,1)S(1)} %get-tuple-element.18), channel_id=1, source_target_pairs={{0,1},{1,0},{2,3},{3,2},{4,5},{5,4},{6,7},{7,6},{8,9},{9,8},{10,11... | collective-permute-start | bytes 138248 | tf_op jit(solution)/shard_map/ppermute | solution.py:84
  20.9 3.5 %collective-permute-start.1 = (bf16[32,720]{1,0:T(8,128)(2,1)S(1)}, bf16[32,720]{1,0:T(8,128)(2,1)S(1)}, u32[]{:S(2)}, u32[]{:S(2)}) collective-permute-start(bf16[32,720]{1,0:T(8,128)(2,1)S(1)} %get-tuple-element.19), channel_id=1, source_target_pairs={{0,17},{1,16},{2,19},{3,18},{4,21},{5,20},{6,23},{7,22},{8,25},{9,... | collective-permute-start | bytes 138248 | tf_op jit(solution)/shard_map/ppermute | solution.py:84
  25.8 5.1 %collective-permute-start.4 = (bf16[32,768]{1,0:T(8,128)(2,1)S(1)}, bf16[32,768]{1,0:T(8,128)(2,1)S(1)}, u32[]{:S(2)}, u32[]{:S(2)}) collective-permute-start(bf16[32,768]{1,0:T(8,128)(2,1)S(1)} %get-tuple-element.26), channel_id=1, source_target_pairs={{0,8},{1,9},{2,10},{3,11},{4,12},{5,13},{6,14},{7,15},{8,0},{9,1},... | collective-permute-start | bytes 147464 | tf_op jit(solution)/shard_map/ppermute | solution.py:91
  28.5 4.1 %collective-permute-start.3 = (bf16[32,768]{1,0:T(8,128)(2,1)S(1)}, bf16[32,768]{1,0:T(8,128)(2,1)S(1)}, u32[]{:S(2)}, u32[]{:S(2)}) collective-permute-start(bf16[32,768]{1,0:T(8,128)(2,1)S(1)} %get-tuple-element.26), channel_id=1, source_target_pairs={{0,4},{1,5},{2,6},{3,7},{4,0},{5,1},{6,2},{7,3},{8,12},{9,13},{10,... | collective-permute-start | bytes 147464 | tf_op jit(solution)/shard_map/ppermute | solution.py:91
  30.0 5.9 %collective-permute-start.5 = (bf16[32,768]{1,0:T(8,128)(2,1)S(1)}, bf16[32,768]{1,0:T(8,128)(2,1)S(1)}, u32[]{:S(2)}, u32[]{:S(2)}) collective-permute-start(bf16[32,768]{1,0:T(8,128)(2,1)S(1)} %get-tuple-element.26), channel_id=1, source_target_pairs={{0,12},{1,13},{2,14},{3,15},{4,8},{5,9},{6,10},{7,11},{8,4},{9,5},... | collective-permute-start | bytes 147464 | tf_op jit(solution)/shard_map/ppermute | solution.py:91
  36.9 7.5 %collective-permute-start.8 = (bf16[72,768]{1,0:T(8,128)(2,1)S(1)}, bf16[72,768]{1,0:T(8,128)(2,1)S(1)}, u32[]{:S(2)}, u32[]{:S(2)}) collective-permute-start(bf16[72,768]{1,0:T(8,128)(2,1)S(1)} %reshape.153), channel_id=1, source_target_pairs={{0,18},{1,19},{2,16},{3,17},{4,22},{5,23},{6,20},{7,21},{8,26},{9,... | collective-permute-start | bytes 331784 | tf_op jit(solution)/shard_map/ppermute | solution.py:84
  39.0 5.4 %collective-permute-start.6 = (bf16[72,768]{1,0:T(8,128)(2,1)S(1)}, bf16[72,768]{1,0:T(8,128)(2,1)S(1)}, u32[]{:S(2)}, u32[]{:S(2)}) collective-permute-start(bf16[72,768]{1,0:T(8,128)(2,1)S(1)} %reshape.153), channel_id=1, source_target_pairs={{0,2},{1,3},{2,0},{3,1},{4,6},{5,7},{6,4},{7,5},{8,10},{9,11},{10,... | collective-permute-start | bytes 331784 | tf_op jit(solution)/shard_map/ppermute | solution.py:84
  39.7 4.8 %collective-permute-start.7 = (bf16[72,768]{1,0:T(8,128)(2,1)S(1)}, bf16[72,768]{1,0:T(8,128)(2,1)S(1)}, u32[]{:S(2)}, u32[]{:S(2)}) collective-permute-start(bf16[72,768]{1,0:T(8,128)(2,1)S(1)} %reshape.152), channel_id=1, source_target_pairs={{0,16},{1,17},{2,18},{3,19},{4,20},{5,21},{6,22},{7,23},{8,24},{9,... | collective-permute-start | bytes 331784 | tf_op jit(solution)/shard_map/ppermute | solution.py:84
  44.6 1.9 %collective-permute-start.9 = (bf16[2,144,768]{2,1,0:T(8,128)(2,1)S(1)}, bf16[2,144,768]{2,1,0:T(8,128)(2,1)S(1)}, u32[]{:S(2)}, u32[]{:S(2)}) collective-permute-start(bf16[2,144,768]{2,1,0:T(8,128)(2,1)S(1)} %get-tuple-element.16), channel_id=1, source_target_pairs={{0,1},{1,0},{2,3},{3,2},{4,5},{5,4},{6,7},{7,6},{8,9},{9,8},{10,11... | collective-permute-start | bytes 1327112 | tf_op jit(solution)/shard_map/ppermute | solution.py:84
  60.9 1.9 %collective-permute-start.10 = (bf16[144,2,720]{2,0,1:T(8,128)(2,1)S(1)}, bf16[144,2,720]{2,0,1:T(8,128)(2,1)S(1)}, u32[]{:S(2)}, u32[]{:S(2)}) collective-permute-start(bf16[144,2,720]{2,0,1:T(8,128)(2,1)S(1)} %slice_bitcast_fusion), channel_id=1, source_target_pairs={{0,1},{1,0},{2,3},{3,2},{4,5},{5,4},{6,7},{7,6},{8,9},{9,8},{10,11... | collective-permute-start | bytes 1244168 | tf_op jit(solution)/shard_map/ppermute | solution.py:84
  62.9 5.7 %collective-permute-start.11 = (bf16[72,720]{1,0:T(8,128)(2,1)S(1)}, bf16[72,720]{1,0:T(8,128)(2,1)S(1)}, u32[]{:S(2)}, u32[]{:S(2)}) collective-permute-start(bf16[72,720]{1,0:T(8,128)(2,1)S(1)} %get-tuple-element.12), channel_id=1, source_target_pairs={{0,16},{1,17},{2,18},{3,19},{4,20},{5,21},{6,22},{7,23},{8,24},{9,... | collective-permute-start | bytes 311048 | tf_op jit(solution)/shard_map/ppermute | solution.py:84
  64.0 6.2 %collective-permute-start.12 = (bf16[72,720]{1,0:T(8,128)(2,1)S(1)}, bf16[72,720]{1,0:T(8,128)(2,1)S(1)}, u32[]{:S(2)}, u32[]{:S(2)}) collective-permute-start(bf16[72,720]{1,0:T(8,128)(2,1)S(1)} %get-tuple-element.13), channel_id=1, source_target_pairs={{0,2},{1,3},{2,0},{3,1},{4,6},{5,7},{6,4},{7,5},{8,10},{9,11},{10,... | collective-permute-start | bytes 311048 | tf_op jit(solution)/shard_map/ppermute | solution.py:84
  65.5 6.0 %collective-permute-start.13 = (bf16[72,720]{1,0:T(8,128)(2,1)S(1)}, bf16[72,720]{1,0:T(8,128)(2,1)S(1)}, u32[]{:S(2)}, u32[]{:S(2)}) collective-permute-start(bf16[72,720]{1,0:T(8,128)(2,1)S(1)} %get-tuple-element.14), channel_id=1, source_target_pairs={{0,18},{1,19},{2,16},{3,17},{4,22},{5,23},{6,20},{7,21},{8,26},{9,... | collective-permute-start | bytes 311048 | tf_op jit(solution)/shard_map/ppermute | solution.py:84
  72.1 4.8 %collective-permute-start.14 = (bf16[32,720]{1,0:T(8,128)(2,1)S(1)}, bf16[32,720]{1,0:T(8,128)(2,1)S(1)}, u32[]{:S(2)}, u32[]{:S(2)}) collective-permute-start(bf16[32,720]{1,0:T(8,128)(2,1)S(1)} %get-tuple-element.20), channel_id=1, source_target_pairs={{0,4},{1,5},{2,6},{3,7},{4,0},{5,1},{6,2},{7,3},{8,12},{9,13},{10,... | collective-permute-start | bytes 138248 | tf_op jit(solution)/shard_map/ppermute | solution.py:91
  72.1 6.0 %collective-permute-start.16 = (bf16[32,720]{1,0:T(8,128)(2,1)S(1)}, bf16[32,720]{1,0:T(8,128)(2,1)S(1)}, u32[]{:S(2)}, u32[]{:S(2)}) collective-permute-start(bf16[32,720]{1,0:T(8,128)(2,1)S(1)} %get-tuple-element.21), channel_id=1, source_target_pairs={{0,12},{1,13},{2,14},{3,15},{4,8},{5,9},{6,10},{7,11},{8,4},{9,5},... | collective-permute-start | bytes 138248 | tf_op jit(solution)/shard_map/ppermute | solution.py:91
  74.8 5.0 %collective-permute-start.15 = (bf16[32,720]{1,0:T(8,128)(2,1)S(1)}, bf16[32,720]{1,0:T(8,128)(2,1)S(1)}, u32[]{:S(2)}, u32[]{:S(2)}) collective-permute-start(bf16[32,720]{1,0:T(8,128)(2,1)S(1)} %get-tuple-element.22), channel_id=1, source_target_pairs={{0,8},{1,9},{2,10},{3,11},{4,12},{5,13},{6,14},{7,15},{8,0},{9,1},... | collective-permute-start | bytes 138248 | tf_op jit(solution)/shard_map/ppermute | solution.py:91

commit v2 on v1

--- a/solution.py
+++ b/solution.py
@@ -1,9 +1,12 @@
+import functools
 import math
 
 import jax
 import jax.numpy as jnp
 import numpy as np
 from jax import lax
+from jax.experimental import pallas as pl
+from jax.experimental.pallas import tpu as pltpu
 from jax.sharding import PartitionSpec as P
 
 HEADS = 64
@@ -14,42 +17,217 @@
 epsilon = 1e-05
 
 
-def attend(q_new, k_new, v_new, k_cache, v_cache, cache_len, cycle_start):
-    tokens = q_new.shape[0]
-    window = k_cache.shape[1]
-    kv_local = k_new.shape[1] // HD
-    grouped = HEADS // KV_HEADS
-    queries = q_new.reshape(tokens, kv_local, grouped, HD)
-    cached_keys = k_cache.reshape(tokens, window, kv_local, HD)
-    cached_values = v_cache.reshape(tokens, window, kv_local, HD)
-    own_key = k_new.reshape(tokens, kv_local, HD)
-    own_value = v_new.reshape(tokens, kv_local, HD)
+def attend_kernel(
+    share_ref, len_hbm, start_hbm, q_hbm, kn_hbm, vn_hbm, k_hbm, v_hbm, wo_hbm,
+    *rest, grouped, chunks, parts,
+):
+    outs, rest = rest[:parts], rest[parts:]
+    len_ref, start_ref, q_ref, kn_ref, vn_ref, kbuf, vbuf, wobuf = rest[:8]
+    queries, heads, small, ksem, vsem, wsem = rest[8:]
+    tokens, window, lanes = k_hbm.shape
+    pairs = (
+        (q_hbm, q_ref), (kn_hbm, kn_ref), (vn_hbm, vn_ref), (len_hbm, len_ref),
+        (start_hbm, start_ref),
+    )
+    firsts = [pltpu.make_async_copy(a, b, small.at[n]) for n, (a, b) in enumerate(pairs)]
+    for copy in firsts:
+        copy.start()
+    n_heads = q_ref.shape[1] // HD
+    step = tokens // chunks
+    rows = wo_hbm.shape[0] // parts
+
+    def kcopy(n):
+        at = pl.ds(n * step, step)
+        return pltpu.make_async_copy(k_hbm.at[at], kbuf.at[at], ksem.at[n])
+
+    def vcopy(n):
+        at = pl.ds(n * step, step)
+        return pltpu.make_async_copy(v_hbm.at[at], vbuf.at[at], vsem.at[n])
+
+    def wrows(k):
+        return pl.ds(pl.multiple_of((share_ref[0] ^ k) * rows, 16), rows)
+
+    def wcopy(k):
+        return pltpu.make_async_copy(wo_hbm.at[wrows(k)], wobuf.at[wrows(k)], wsem.at[k])
+
+    for n in range(chunks):
+        kcopy(n).start()
+        vcopy(n).start()
+    for k in reversed(range(parts)):
+        wcopy(k).start()
+    for copy in firsts:
+        copy.wait()
+    lane = lax.broadcasted_iota(jnp.int32, (tokens, lanes), 1)
+    per = lanes // HD
+
+    def shifted(x, source, target):
+        if source == target:
+            return x
+        return pltpu.roll(x, ((target - source) * HD) % lanes, 1)
+
+    for h in range(n_heads):
+        at = h // per * lanes
+        x = q_ref[:, at : at + lanes].astype(jnp.float32)
+        kv = h // grouped
+        x = jnp.where(lane // HD == kv, shifted(x, h % per, kv), 0.0)
+        queries[h * tokens : (h + 1) * tokens, :] = x
     factor = HD ** (-0.5)
-    scores = (
-        jnp.einsum("tkgd,tskd->tkgs", queries, cached_keys, preferred_element_type=jnp.float32)
-        * factor
-    )
-    own_score = (
-        jnp.einsum("tkgd,tkd->tkg", queries, own_key, preferred_element_type=jnp.float32) * factor
-    )
-    positions = jnp.arange(window, dtype=jnp.int32)
-    usable = (positions[None, :] - cycle_start[:, None]) % window < cache_len[:, None]
-    usable = usable[:, None, None, :]
-    masked = jnp.where(usable, scores, -1e30)
-    highest = jnp.maximum(jnp.max(masked, axis=3), own_score)
-    lifted = jnp.where(usable, jnp.exp(masked - highest[..., None]), 0.0)
-    own_lift = jnp.exp(own_score - highest)
-    denominator = jnp.sum(lifted, axis=3) + own_lift
-    weights = (lifted / denominator[..., None]).astype(jnp.bfloat16)
-    own_weight = (own_lift / denominator).astype(jnp.bfloat16)
-    combined = jnp.einsum(
-        "tkgs,tskd->tkgd", weights, cached_values, preferred_element_type=jnp.float32
-    )
-    combined = (
-        combined
-        + own_weight.astype(jnp.float32)[..., None] * own_value.astype(jnp.float32)[:, :, None, :]
-    )
-    return combined.reshape(tokens, -1).astype(jnp.bfloat16)
+    slots = lax.broadcasted_iota(jnp.int32, (1, window), 1)
+    own_keys = kn_ref[...].astype(jnp.float32)
+    own_values = vn_ref[...].astype(jnp.float32)
+    for n in range(chunks):
+        kcopy(n).wait()
+        vcopy(n).wait()
+        for t in range(n * step, (n + 1) * step):
+            at = pl.ds(t, n_heads, stride=tokens)
+            query = queries[at, :]
+            scores = factor * lax.dot_general(
+                query.astype(jnp.bfloat16), kbuf[t], (((1,), (1,)), ((), ())),
+                preferred_element_type=jnp.float32,
+            )
+            own = factor * jnp.sum(query * own_keys[t : t + 1, :], axis=1, keepdims=True)
+            age = slots - start_ref[t]
+            age = jnp.where(age < 0, age + window, age)
+            usable = age < len_ref[t]
+            masked = jnp.where(usable, scores, -1e30)
+            highest = jnp.maximum(jnp.max(masked, axis=1, keepdims=True), own)
+            lifted = jnp.where(usable, jnp.exp(masked - highest), 0.0)
+            own_lift = jnp.exp(own - highest)
+            denominator = jnp.sum(lifted, axis=1, keepdims=True) + own_lift
+            weights = (lifted / denominator).astype(jnp.bfloat16)
+            own_weight = (own_lift / denominator).astype(jnp.bfloat16).astype(jnp.float32)
+            mixed = jnp.dot(weights, vbuf[t], preferred_element_type=jnp.float32)
+            heads[at, :] = mixed + own_weight * own_values[t : t + 1, :]
+    columns = []
+    for c in range(n_heads // per):
+        column = None
+        for p in range(per):
+            h = c * per + p
+            x = shifted(heads[h * tokens : (h + 1) * tokens, :], h // grouped, p)
+            column = x if column is None else jnp.where(lane // HD == p, x, column)
+        columns.append(column.astype(jnp.bfloat16))
+    stacked = jnp.concatenate(columns, axis=1)
+    for k in reversed(range(parts)):
+        wcopy(k).wait()
+        piece = lax.dot_general(
+            stacked, wobuf[wrows(k), :], (((1,), (1,)), ((), ())),
+            preferred_element_type=jnp.float32,
+        )
+        outs[k][...] = piece.astype(outs[k].dtype)
+
+
+def attend_project(
+    share, q_new, k_new, v_new, k_cache, v_cache, cache_len, cycle_start, out_proj, parts
+):
+    tokens, window, lanes = k_cache.shape
+    n_heads = q_new.shape[1] // HD
+    quarter = out_proj.shape[0] // parts
+    chunks = 4
+    smem = pl.BlockSpec(memory_space=pltpu.SMEM)
+    vmem = pl.BlockSpec(memory_space=pltpu.VMEM)
+    hbm = pl.BlockSpec(memory_space=pltpu.HBM)
+    inputs = [
+        pltpu.with_memory_space_constraint(x, pltpu.HBM)
+        for x in (
+            cache_len, cycle_start, q_new, k_new, v_new, k_cache, v_cache, out_proj
+        )
+    ]
+    kinds = [jnp.float32] + [jnp.bfloat16] * (parts - 1)
+    return pl.pallas_call(
+        functools.partial(
+            attend_kernel, grouped=HEADS // KV_HEADS, chunks=chunks, parts=parts
+        ),
+        in_specs=[smem] + [hbm] * 8,
+        out_specs=[vmem] * parts,
+        out_shape=[jax.ShapeDtypeStruct((tokens, quarter), kind) for kind in kinds],
+        scratch_shapes=[
+            pltpu.SMEM(cache_len.shape, jnp.int32),
+            pltpu.SMEM(cycle_start.shape, jnp.int32),
+            pltpu.VMEM(q_new.shape, q_new.dtype),
+            pltpu.VMEM(k_new.shape, k_new.dtype),
+            pltpu.VMEM(v_new.shape, v_new.dtype),
+            pltpu.VMEM(k_cache.shape, k_cache.dtype),
+            pltpu.VMEM(v_cache.shape, v_cache.dtype),
+            pltpu.VMEM(out_proj.shape, out_proj.dtype),
+            pltpu.VMEM((n_heads * tokens, lanes), jnp.float32),
+            pltpu.VMEM((n_heads * tokens, lanes), jnp.float32),
+            pltpu.SemaphoreType.DMA((5,)),
+            pltpu.SemaphoreType.DMA((chunks,)),
+            pltpu.SemaphoreType.DMA((chunks,)),
+            pltpu.SemaphoreType.DMA((parts,)),
+        ],
+        compiler_params=pltpu.CompilerParams(vmem_limit_bytes=16 << 20),
+        name="attend_project",
+    )(share, *inputs)
+
+
+def expert_kernel(
+    place_ref, own_ref, other_ref, gate_ref, up_ref, down_ref, keep_ref, send_ref, pieces,
+    *, quarter, topk,
+):
+    n_role, items, lanes = own_ref.shape
+    n_tp = 2
+    parts = n_role * n_tp
+    share = place_ref[0]
+    tail_at = quarter // 128 * 128
+    first = quarter - tail_at
+    tail = 0.0
+    columns = []
+    for p in range(parts):
+        slot = share ^ p
+        i, l = slot // n_tp, slot % n_tp
+        x = jnp.where(l == 0, own_ref[i], other_ref[i])
+        tail = tail + x[:, tail_at:].astype(jnp.float32)
+        columns.append(x[:, :quarter])
+    inputs = jnp.concatenate(columns, axis=1)
+    turned = (((1,), (1,)), ((), ()))
+    gate_lin = lax.dot_general(inputs, gate_ref[0], turned, preferred_element_type=jnp.float32)
+    up_lin = lax.dot_general(inputs, up_ref[0], turned, preferred_element_type=jnp.float32)
+    ids = own_ref[0, :, tail_at:].astype(jnp.float32)
+    n_stat = 1 + topk
+
+    def total(c):
+        at = first + topk + c
+        return sum(tail[:, at + p * n_stat : at + p * n_stat + 1] for p in range(3))
+
+    scale = lax.rsqrt(total(0) / (parts * quarter) + epsilon)
+    picked = [total(1 + k) * scale for k in range(topk)]
+    top = functools.reduce(jnp.maximum, picked)
+    lifted = [jnp.exp(x - top) for x in picked]
+    expert = place_ref[1].astype(jnp.float32)
+    mine = sum(
+        jnp.where(ids[:, first + k : first + k + 1] == expert, lifted[k], 0.0)
+        for k in range(topk)
+    )
+    weight = mine / sum(lifted)
+    gate_lin = gate_lin * scale
+    up_lin = up_lin * scale
+    activated = gate_lin * jax.nn.sigmoid(1.702 * gate_lin) * (up_lin + 1.0)
+    result = jnp.dot(
+        activated.astype(jnp.bfloat16), down_ref[0], preferred_element_type=jnp.float32
+    )
+    result = result * weight
+    for p in range(parts):
+        pieces[p ^ share] = result[:, p * quarter : (p + 1) * quarter].astype(jnp.bfloat16)
+    for i in range(n_role):
+        keep_ref[i] = pieces[i * n_tp]
+        send_ref[i] = pieces[i * n_tp + 1]
+
+
+def run_expert(place, own, other, w_gate, w_up, w_down, quarter, topk):
+    n_role, items, _ = own.shape
+    smem = pl.BlockSpec(memory_space=pltpu.SMEM)
+    vmem = pl.BlockSpec(memory_space=pltpu.VMEM)
+    shape = jax.ShapeDtypeStruct((n_role, items, quarter), jnp.bfloat16)
+    return pl.pallas_call(
+        functools.partial(expert_kernel, quarter=quarter, topk=topk),
+        in_specs=[smem] + [vmem] * 5,
+        out_specs=[vmem, vmem],
+        out_shape=[shape, shape],
+        scratch_shapes=[pltpu.VMEM((2 * n_role, items, quarter), jnp.bfloat16)],
+        compiler_params=pltpu.CompilerParams(vmem_limit_bytes=24 << 20),
+        name="expert",
+    )(place, own, other, w_gate, w_up, w_down)
 
 
 def split3(x):
@@ -102,17 +280,15 @@
         cap = max(3, tokens * topk // experts + 2)
         far, near = grp // n_near, grp % n_near
         share = role * n_tp + tp
-        heads_out = attend(q_new, k_new, v_new, k_cache, v_cache, cache_len, cycle_start)
-        projected = jnp.dot(heads_out, out_proj, preferred_element_type=jnp.float32)
-        blocks = projected.reshape(tokens, n_role, n_tp, quarter)
-
-        def block(i, l):
-            mine = lax.dynamic_index_in_dim(blocks, role ^ i, 1, keepdims=False)
-            return lax.dynamic_index_in_dim(mine, tp ^ l, 1, keepdims=False)
-
-        stream = residual.astype(jnp.float32) + block(0, 0)
-        for i, l in ((1, 0), (1, 1), (0, 1)):
-            stream = stream + send(block(i, l).astype(jnp.bfloat16), role=i, tp=l).astype(jnp.float32)
+        parts = n_role * n_tp
+        place = share.astype(jnp.int32).reshape(1)
+        pieces = attend_project(
+            place, q_new, k_new, v_new, k_cache, v_cache, cache_len, cycle_start, out_proj.T, parts
+        )
+        stream = residual.astype(jnp.float32) + pieces[0]
+        for k in (2, 3, 1):
+            moved = send(pieces[k], role=k // n_tp, tp=k % n_tp)
+            stream = stream + moved.astype(jnp.float32)
         attended = stream.astype(jnp.bfloat16)
         gain = lax.dynamic_slice_in_dim(norm_gain, share * quarter, quarter, 0)
         scaled = (stream * gain).astype(jnp.bfloat16)
@@ -149,38 +325,18 @@
             [jnp.concatenate([arrived[j, i] for j in range(n_near)], 0) for i in range(n_role)]
         )
         other = send(half, tp=1)
-        both = jnp.stack([half, other], 1)
-        both = jnp.where(role == 0, both, both[::-1])
-        both = jnp.where(tp == 0, both, both[:, ::-1])
-        quarters = both.reshape(n_role * n_tp, -1, lanes)
-        tail = jnp.sum(quarters[:, :, quarter + topk :].astype(jnp.float32), axis=0)
-        own_ids = quarters[0, :, quarter : quarter + topk].astype(jnp.float32)
-        n_stat = 1 + topk
-        total = sum(tail[:, p * n_stat : (p + 1) * n_stat] for p in range(3))
-        scale = lax.rsqrt(total[:, :1] / width + epsilon)
-        picked = total[:, 1:] * scale
-        lifted = jnp.exp(picked - jnp.max(picked, axis=1, keepdims=True))
-        mine = jnp.where(own_ids == grp.astype(jnp.float32), lifted, 0.0)
-        weight = jnp.sum(mine, axis=1, keepdims=True) / jnp.sum(lifted, axis=1, keepdims=True)
-        inputs = jnp.concatenate([quarters[p, :, :quarter] for p in range(n_role * n_tp)], axis=1)
-        gate_lin = jnp.dot(inputs, w_gate[0], preferred_element_type=jnp.float32) * scale
-        up_lin = jnp.dot(inputs, w_up[0], preferred_element_type=jnp.float32) * scale
-        activated = (gate_lin * jax.nn.sigmoid(1.702 * gate_lin) * (up_lin + 1.0)).astype(
-            jnp.bfloat16
-        )
-        result = jnp.dot(activated, w_down[0], preferred_element_type=jnp.float32) * weight
-        blocks_out = result.astype(jnp.bfloat16).reshape(-1, n_role, n_tp, quarter)
-        blocks_out = jnp.where(role == 0, blocks_out, blocks_out[:, ::-1])
-        blocks_out = jnp.where(tp == 0, blocks_out, blocks_out[:, :, ::-1])
-        acc = blocks_out[:, :, 0].astype(jnp.float32) + send(blocks_out[:, :, 1], tp=1).astype(
-            jnp.float32
-        )
-        acc = acc.astype(jnp.bfloat16).reshape(n_near, n_far * cap, n_role, quarter)
+        place = jnp.stack([share, grp]).astype(jnp.int32)
+        kept, sent = run_expert(
+            place, half, other, jnp.swapaxes(w_gate, 1, 2), jnp.swapaxes(w_up, 1, 2), w_down,
+            quarter, topk,
+        )
+        acc = kept.astype(jnp.float32) + send(sent, tp=1).astype(jnp.float32)
+        acc = acc.astype(jnp.bfloat16).reshape(n_role, n_near, n_far * cap, quarter)
         back = []
         for j in range(n_near):
             total_rows = 0.0
             for i in range(n_role):
-                piece = acc[j, :, i]
+                piece = acc[i, j]
                 if (j, i) != (0, 0):
                     piece = send(piece, near=j, role=i)
                 total_rows = total_rows + piece.astype(jnp.float32)

time: 80.9 us -> 71.4 us (0.88)
  Pallas kernels: 0 us -> 17.7 us
  matrix products: 15.7 us -> 0.97 us
  local copies, waits for them, and re-layouts: 16.3 us -> 4.58 us
  other arithmetic: 4.34 us -> 2.53 us
  waiting for transfers between devices: 24.3 us -> 25.9 us
    pallas_call x0 -> x2, Pallas kernels: none -> 17.7 us  [the longest x1 14.9 us: attend_project(): pl.pallas_call(functools.partial(attend_kernel, grouped=HEADS // KV_HEADS...]
    dot_general x6 -> x0, matrix products: 14.8 us -> none  [the longest x1 4.41 us: local(): projected = jnp.dot(heads_out, out_proj, preferred_element_type=jnp.float32)]
    reshape x4 -> x0, local copies, waits for them, and re-layouts: 5.7 us -> none  [the longest x2 3.79 us: local(): blocks_out = result.astype(jnp.bfloat16).reshape(-1, n_role, n_tp, quarter)]
    convert_element_type x7 -> x0, local copies, waits for them, and re-layouts: 2.87 us -> none  [the longest x1 1.05 us: attend(): return combined.reshape(tokens, -1).astype(jnp.bfloat16)]
    concatenate x1, local copies, waits for them, and re-layouts: 1.53 us -> 0.09 us  [local(): stats = split3(jnp.concatenate([squares, chosen], axis=1))]
    ppermute x11, waiting for transfers between devices: 14.5 us -> 15.9 us  [send(): lax.ppermute(x, names, swap_table(mesh, lambda g: g ^ near, role, tp))]
    squeeze x3 -> x1, local copies, waits for them, and re-layouts: 0.88 us -> 0.02 us  [local(): piece = acc[i, j]]
    unnamed x16 -> x12, local copies, waits for them, and re-layouts: 3.7 us -> 3.22 us
  transfers between devices with their start and end apart: 17 -> 17, of which waited for: 15 -> 14; matrix products, arithmetic and copies ran while one was open for 1% -> 2% of each run, Pallas kernels for 0% -> 0%
where the time goes in v2:
time: 71.4 us; the launch traced here: 71.1 us
  waiting for transfers between devices  25.9 us (36%)
  starting transfers between devices  18.7 us (26%)
  Pallas kernels  17.7 us (25%)
  local copies, waits for them, and re-layouts  4.58 us (6%)
  other arithmetic  2.53 us (4%)
  matrix products  0.97 us (1%)
  between operations  0.85 us (1%)
    ppermute x11, waiting for transfers between devices, send(): lax.ppermute(x, names, swap_table(mesh, lambda g: g ^ near, role, tp))  15.9 us
    pallas_call x1, Pallas kernels, attend_project(): pl.pallas_call(functools.partial(attend_kernel, grouped=HEADS // KV_HEADS...  14.9 us
    ppermute x11, starting transfers between devices, send(): lax.ppermute(x, names, swap_table(mesh, lambda g: g ^ near, role, tp))  10.7 us
    ppermute x6, waiting for transfers between devices, send_far(): return lax.ppermute(x, names, swap_table(mesh, grp_of, 0, 0))  9.96 us
    ppermute x6, starting transfers between devices, send_far(): return lax.ppermute(x, names, swap_table(mesh, grp_of, 0, 0))  8 us
    unnamed x12, local copies, waits for them, and re-layouts  3.22 us
    pallas_call x1, Pallas kernels, run_expert(): pl.pallas_call(functools.partial(expert_kernel, quarter=quarter, topk=top...  2.75 us
  transfers between devices with their start and end apart: 17, of which 14 were waited for; matrix products, arithmetic and copies ran while one was open for 2% of the time, Pallas kernels for 0%

profile of v2, /device:TPU:0, one launch (start us, length us, event | category | flops | bytes accessed | tf_op | source)
XLA Modules:
  0.0 71.1 jit_solution(213923310623338712)
XLA Ops:
  0.7 14.9 %attend_project.1 = (f32[32,720]{1,0:T(8,128)S(1)}, bf16[32,720]{1,0:T(8,128)(2,1)S(1)}, bf16[32,720]{1,0:T(8,128)(2,1)S(1)}, bf16[32,720]{1,0:T(8,128)(2,1)S(1)}) custom-call(s32[1]{0:T(128)} %bitcast.share_ref, s32[32]{0:T(128)} %len_hbm.1, s32[32]{0:T(128)} %start_hbm.1, bf16[32,1024]{1,0:T(8,128)(2,1)} %q_hbm.1, bf16[32,128]{1,0:T(8,128)(2,1)} %kn_hbm.1, ...), custom_call_target="tpu_custom_call" | custom-call | tf_op jit(solution)/shard_map/attend_project/pallas_call | solution.py:136
  15.6 3.0 %collective-permute-start = (bf16[32,720]{1,0:T(8,128)(2,1)S(1)}, bf16[32,720]{1,0:T(8,128)(2,1)S(1)}, u32[]{:S(2)}, u32[]{:S(2)}) collective-permute-start(bf16[32,720]{1,0:T(8,128)(2,1)S(1)} %get-tuple-element.9), channel_id=1, source_target_pairs={{0,16},{1,17},{2,18},{3,19},{4,20},{5,21},{6,22},{7,23},{8,24},{9,... | collective-permute-start | bytes 138248 | tf_op jit(solution)/shard_map/ppermute | solution.py:262
  19.0 0.8 %dynamic_slice.3 = f32[720]{0:T(1024)S(1)} dynamic-slice(f32[2880]{0:T(1024)} %param.24, s32[]{:T(128)S(6)} %select_n.18), dynamic_slice_sizes={720} | dynamic-slice | bytes 5764 | tf_op jit(solution)/shard_map/dynamic_slice | solution.py:293
  19.7 1.0 %collective-permute-done = bf16[32,720]{1,0:T(8,128)(2,1)S(1)} collective-permute-done((bf16[32,720]{1,0:T(8,128)(2,1)S(1)}, bf16[32,720]{1,0:T(8,128)(2,1)S(1)}, u32[]{:S(2)}, u32[]{:S(2)}) %collective-permute-start) | collective-permute-done | bytes 46112 | tf_op jit(solution)/shard_map/ppermute | solution.py:262
  20.7 1.7 %collective-permute-done.1 = bf16[32,720]{1,0:T(8,128)(2,1)S(1)} collective-permute-done((bf16[32,720]{1,0:T(8,128)(2,1)S(1)}, bf16[32,720]{1,0:T(8,128)(2,1)S(1)}, u32[]{:S(2)}, u32[]{:S(2)}) %collective-permute-start.1) | collective-permute-done | bytes 46112 | tf_op jit(solution)/shard_map/ppermute | solution.py:262
  22.6 0.6 multiply_convert_fusion
  23.7 2.7 %collective-permute-start.4 = (bf16[32,768]{1,0:T(8,128)(2,1)S(1)}, bf16[32,768]{1,0:T(8,128)(2,1)S(1)}, u32[]{:S(2)}, u32[]{:S(2)}) collective-permute-start(bf16[32,768]{1,0:T(8,128)(2,1)S(1)} %get-tuple-element.27), channel_id=1, source_target_pairs={{0,8},{1,9},{2,10},{3,11},{4,12},{5,13},{6,14},{7,15},{8,0},{9,1},... | collective-permute-start | bytes 147464 | tf_op jit(solution)/shard_map/ppermute | solution.py:269
  26.3 1.6 %collective-permute-start.3 = (bf16[32,768]{1,0:T(8,128)(2,1)S(1)}, bf16[32,768]{1,0:T(8,128)(2,1)S(1)}, u32[]{:S(2)}, u32[]{:S(2)}) collective-permute-start(bf16[32,768]{1,0:T(8,128)(2,1)S(1)} %get-tuple-element.27), channel_id=1, source_target_pairs={{0,4},{1,5},{2,6},{3,7},{4,0},{5,1},{6,2},{7,3},{8,12},{9,13},{10,... | collective-permute-start | bytes 147464 | tf_op jit(solution)/shard_map/ppermute | solution.py:269
  28.1 1.1 %collective-permute-done.4 = bf16[32,768]{1,0:T(8,128)(2,1)S(1)} collective-permute-done((bf16[32,768]{1,0:T(8,128)(2,1)S(1)}, bf16[32,768]{1,0:T(8,128)(2,1)S(1)}, u32[]{:S(2)}, u32[]{:S(2)}) %collective-permute-start.4) | collective-permute-done | bytes 49184 | tf_op jit(solution)/shard_map/ppermute | solution.py:269
  29.3 1.2 %collective-permute-done.3 = bf16[32,768]{1,0:T(8,128)(2,1)S(1)} collective-permute-done((bf16[32,768]{1,0:T(8,128)(2,1)S(1)}, bf16[32,768]{1,0:T(8,128)(2,1)S(1)}, u32[]{:S(2)}, u32[]{:S(2)}) %collective-permute-start.3) | collective-permute-done | bytes 49184 | tf_op jit(solution)/shard_map/ppermute | solution.py:269
  30.4 3.4 %collective-permute-done.5 = bf16[32,768]{1,0:T(8,128)(2,1)S(1)} collective-permute-done((bf16[32,768]{1,0:T(8,128)(2,1)S(1)}, bf16[32,768]{1,0:T(8,128)(2,1)S(1)}, u32[]{:S(2)}, u32[]{:S(2)}) %collective-permute-start.5) | collective-permute-done | bytes 49184 | tf_op jit(solution)/shard_map/ppermute | solution.py:269
  34.8 1.8 %collective-permute-start.8 = (bf16[72,768]{1,0:T(8,128)(2,1)S(1)}, bf16[72,768]{1,0:T(8,128)(2,1)S(1)}, u32[]{:S(2)}, u32[]{:S(2)}) collective-permute-start(bf16[72,768]{1,0:T(8,128)(2,1)S(1)} %reshape.57), channel_id=1, source_target_pairs={{0,18},{1,19},{2,16},{3,17},{4,22},{5,23},{6,20},{7,21},{8,26},{9,... | collective-permute-start | bytes 331784 | tf_op jit(solution)/shard_map/ppermute | solution.py:262
  36.6 0.5 collective-permute-start.6
  37.3 1.3 %collective-permute-start.7 = (bf16[72,768]{1,0:T(8,128)(2,1)S(1)}, bf16[72,768]{1,0:T(8,128)(2,1)S(1)}, u32[]{:S(2)}, u32[]{:S(2)}) collective-permute-start(bf16[72,768]{1,0:T(8,128)(2,1)S(1)} %reshape.56), channel_id=1, source_target_pairs={{0,16},{1,17},{2,18},{3,19},{4,20},{5,21},{6,22},{7,23},{8,24},{9,... | collective-permute-start | bytes 331784 | tf_op jit(solution)/shard_map/ppermute | solution.py:262
  38.6 3.5 %collective-permute-done.6 = bf16[72,768]{1,0:T(8,128)(2,1)S(1)} collective-permute-done((bf16[72,768]{1,0:T(8,128)(2,1)S(1)}, bf16[72,768]{1,0:T(8,128)(2,1)S(1)}, u32[]{:S(2)}, u32[]{:S(2)}) %collective-permute-start.6) | collective-permute-done | bytes 110624 | tf_op jit(solution)/shard_map/ppermute | solution.py:262
  42.4 1.7 %collective-permute-done.9.other_ref = bf16[2,144,768]{2,1,0:T(8,128)(2,1)S(1)} collective-permute-done((bf16[2,144,768]{2,1,0:T(8,128)(2,1)S(1)}, bf16[2,144,768]{2,1,0:T(8,128)(2,1)S(1)}, u32[]{:S(2)}, u32[]{:S(2)}) %collective-permute-start.9) | collective-permute-done | bytes 442400 | tf_op jit(solution)/shard_map/ppermute | solution.py:262
  44.1 1.6 %copy-done.2 = bf16[1,2880,360]{1,2,0:T(8,128)(2,1)S(1)} copy-done((bf16[1,2880,360]{1,2,0:T(8,128)(2,1)S(1)}, bf16[1,2880,360]{1,2,0:T(8,128)(2,1)}, u32[]{:S(2)}) %copy-start.2) | copy-done | bytes 2073624
  45.7 1.6 %copy-done.3 = bf16[1,360,2880]{2,1,0:T(8,128)(2,1)S(1)} copy-done((bf16[1,360,2880]{2,1,0:T(8,128)(2,1)S(1)}, bf16[1,360,2880]{2,1,0:T(8,128)(2,1)}, u32[]{:S(2)}) %copy-start.3) | copy-done | bytes 2073624
  47.3 2.8 %expert.1 = (bf16[2,144,720]{2,1,0:T(8,128)(2,1)S(1)}, bf16[2,144,720]{2,1,0:T(8,128)(2,1)S(1)}) custom-call(s32[2]{0:T(128)S(1)} %pad_add_fusion.place_ref, bf16[2,144,768]{2,1,0:T(8,128)(2,1)S(1)} %pad_maximum_fusion.own_ref, bf16[2,144,768]{2,1,0:T(8,128)(2,1)S(1)} %collective-permute-done.9.other_ref, bf16[1,360,2880]{2,1,0:T(8,128)(2,1)S(1)} %bitcast.42, ...), custom_call_target="tpu_custom_call" | custom-call | tf_op jit(solution)/shard_map/expert/pallas_call | solution.py:222
  50.2 1.7 %collective-permute-done.10 = bf16[2,144,720]{2,1,0:T(8,128)(2,1)S(1)} collective-permute-done((bf16[2,144,720]{2,1,0:T(8,128)(2,1)S(1)}, bf16[2,144,720]{2,1,0:T(8,128)(2,1)S(1)}, u32[]{:S(2)}, u32[]{:S(2)}) %collective-permute-start.10) | collective-permute-done | bytes 414752 | tf_op jit(solution)/shard_map/ppermute | solution.py:262
  52.0 1.3 %collective-permute-start.11 = (bf16[72,720]{1,0:T(8,128)(2,1)S(1)}, bf16[72,720]{1,0:T(8,128)(2,1)S(1)}, u32[]{:S(2)}, u32[]{:S(2)}) collective-permute-start(bf16[72,720]{1,0:T(8,128)(2,1)S(1)} %get-tuple-element.18), channel_id=1, source_target_pairs={{0,16},{1,17},{2,18},{3,19},{4,20},{5,21},{6,22},{7,23},{8,24},{9,... | collective-permute-start | bytes 311048 | tf_op jit(solution)/shard_map/ppermute | solution.py:262
  53.3 1.8 %collective-permute-start.13 = (bf16[72,720]{1,0:T(8,128)(2,1)S(1)}, bf16[72,720]{1,0:T(8,128)(2,1)S(1)}, u32[]{:S(2)}, u32[]{:S(2)}) collective-permute-start(bf16[72,720]{1,0:T(8,128)(2,1)S(1)} %get-tuple-element.19), channel_id=1, source_target_pairs={{0,18},{1,19},{2,16},{3,17},{4,22},{5,23},{6,20},{7,21},{8,26},{9,... | collective-permute-start | bytes 311048 | tf_op jit(solution)/shard_map/ppermute | solution.py:262
  55.1 0.5 collective-permute-start.12
  55.6 2.1 %collective-permute-done.11 = bf16[72,720]{1,0:T(8,128)(2,1)S(1)} collective-permute-done((bf16[72,720]{1,0:T(8,128)(2,1)S(1)}, bf16[72,720]{1,0:T(8,128)(2,1)S(1)}, u32[]{:S(2)}, u32[]{:S(2)}) %collective-permute-start.11) | collective-permute-done | bytes 103712 | tf_op jit(solution)/shard_map/ppermute | solution.py:262
  57.8 2.9 %collective-permute-done.13 = bf16[72,720]{1,0:T(8,128)(2,1)S(1)} collective-permute-done((bf16[72,720]{1,0:T(8,128)(2,1)S(1)}, bf16[72,720]{1,0:T(8,128)(2,1)S(1)}, u32[]{:S(2)}, u32[]{:S(2)}) %collective-permute-start.13) | collective-permute-done | bytes 103712 | tf_op jit(solution)/shard_map/ppermute | solution.py:262
  60.6 1.4 %collective-permute-done.12 = bf16[72,720]{1,0:T(8,128)(2,1)S(1)} collective-permute-done((bf16[72,720]{1,0:T(8,128)(2,1)S(1)}, bf16[72,720]{1,0:T(8,128)(2,1)S(1)}, u32[]{:S(2)}, u32[]{:S(2)}) %collective-permute-start.12) | collective-permute-done | bytes 103712 | tf_op jit(solution)/shard_map/ppermute | solution.py:262
  62.7 2.0 %collective-permute-start.16 = (bf16[32,720]{1,0:T(8,128)(2,1)S(1)}, bf16[32,720]{1,0:T(8,128)(2,1)S(1)}, u32[]{:S(2)}, u32[]{:S(2)}) collective-permute-start(bf16[32,720]{1,0:T(8,128)(2,1)S(1)} %get-tuple-element.22), channel_id=1, source_target_pairs={{0,12},{1,13},{2,14},{3,15},{4,8},{5,9},{6,10},{7,11},{8,4},{9,5},... | collective-permute-start | bytes 138248 | tf_op jit(solution)/shard_map/ppermute | solution.py:269
  64.7 1.4 %collective-permute-start.15 = (bf16[32,720]{1,0:T(8,128)(2,1)S(1)}, bf16[32,720]{1,0:T(8,128)(2,1)S(1)}, u32[]{:S(2)}, u32[]{:S(2)}) collective-permute-start(bf16[32,720]{1,0:T(8,128)(2,1)S(1)} %get-tuple-element.23), channel_id=1, source_target_pairs={{0,8},{1,9},{2,10},{3,11},{4,12},{5,13},{6,14},{7,15},{8,0},{9,1},... | collective-permute-start | bytes 138248 | tf_op jit(solution)/shard_map/ppermute | solution.py:269
  66.2 0.8 %collective-permute-done.14 = bf16[32,720]{1,0:T(8,128)(2,1)S(1)} collective-permute-done((bf16[32,720]{1,0:T(8,128)(2,1)S(1)}, bf16[32,720]{1,0:T(8,128)(2,1)S(1)}, u32[]{:S(2)}, u32[]{:S(2)}) %collective-permute-start.14) | collective-permute-done | bytes 46112 | tf_op jit(solution)/shard_map/ppermute | solution.py:269
  67.0 1.6 %collective-permute-done.16 = bf16[32,720]{1,0:T(8,128)(2,1)S(1)} collective-permute-done((bf16[32,720]{1,0:T(8,128)(2,1)S(1)}, bf16[32,720]{1,0:T(8,128)(2,1)S(1)}, u32[]{:S(2)}, u32[]{:S(2)}) %collective-permute-start.16) | collective-permute-done | bytes 46112 | tf_op jit(solution)/shard_map/ppermute | solution.py:269
  68.7 1.8 %collective-permute-done.15 = bf16[32,720]{1,0:T(8,128)(2,1)S(1)} collective-permute-done((bf16[32,720]{1,0:T(8,128)(2,1)S(1)}, bf16[32,720]{1,0:T(8,128)(2,1)S(1)}, u32[]{:S(2)}, u32[]{:S(2)}) %collective-permute-start.15) | collective-permute-done | bytes 46112 | tf_op jit(solution)/shard_map/ppermute | solution.py:269
  70.5 0.6 fusion.4
  (53 shorter events, 3.6 us)
Async XLA Ops:
  0.6 22.6 %copy-start = (bf16[720,8]{0,1:T(8,128)(2,1)S(1)}, bf16[720,8]{0,1:T(8,128)(2,1)}, u32[]{:S(2)}) copy-start(bf16[720,8]{0,1:T(8,128)(2,1)} %param.25) | copy-start | bytes 34564
  0.7 18.2 %copy-start.5 = (s32[32,4]{0,1:T(4,128)S(1)}, s32[32,4]{0,1:T(4,128)}, u32[]{:S(2)}) copy-start(s32[32,4]{0,1:T(4,128)} %param.26) | copy-start | bytes 1540
  0.7 21.8 %copy-start.4 = (bf16[32,720]{1,0:T(8,128)(2,1)S(1)}, bf16[32,720]{1,0:T(8,128)(2,1)}, u32[]{:S(2)}) copy-start(bf16[32,720]{1,0:T(8,128)(2,1)} %param.22) | copy-start | bytes 138244
  15.6 5.1 %collective-permute-start = (bf16[32,720]{1,0:T(8,128)(2,1)S(1)}, bf16[32,720]{1,0:T(8,128)(2,1)S(1)}, u32[]{:S(2)}, u32[]{:S(2)}) collective-permute-start(bf16[32,720]{1,0:T(8,128)(2,1)S(1)} %get-tuple-element.9), channel_id=1, source_target_pairs={{0,16},{1,17},{2,18},{3,19},{4,20},{5,21},{6,22},{7,23},{8,24},{9,... | collective-permute-start | bytes 138248 | tf_op jit(solution)/shard_map/ppermute | solution.py:262
  18.7 3.8 %collective-permute-start.1 = (bf16[32,720]{1,0:T(8,128)(2,1)S(1)}, bf16[32,720]{1,0:T(8,128)(2,1)S(1)}, u32[]{:S(2)}, u32[]{:S(2)}) collective-permute-start(bf16[32,720]{1,0:T(8,128)(2,1)S(1)} %get-tuple-element.10), channel_id=1, source_target_pairs={{0,17},{1,16},{2,19},{3,18},{4,21},{5,20},{6,23},{7,22},{8,25},{9,... | collective-permute-start | bytes 138248 | tf_op jit(solution)/shard_map/ppermute | solution.py:262
  18.7 3.8 %collective-permute-start.2 = (bf16[32,720]{1,0:T(8,128)(2,1)S(1)}, bf16[32,720]{1,0:T(8,128)(2,1)S(1)}, u32[]{:S(2)}, u32[]{:S(2)}) collective-permute-start(bf16[32,720]{1,0:T(8,128)(2,1)S(1)} %get-tuple-element.11), channel_id=1, source_target_pairs={{0,1},{1,0},{2,3},{3,2},{4,5},{5,4},{6,7},{7,6},{8,9},{9,8},{10,11... | collective-permute-start | bytes 138248 | tf_op jit(solution)/shard_map/ppermute | solution.py:262
  23.7 20.4 %copy-start.1 = (bf16[1,2880,360]{1,2,0:T(8,128)(2,1)S(1)}, bf16[1,2880,360]{1,2,0:T(8,128)(2,1)}, u32[]{:S(2)}) copy-start(bf16[1,2880,360]{1,2,0:T(8,128)(2,1)} %param.27) | copy-start | bytes 6220804
  23.7 5.6 %collective-permute-start.4 = (bf16[32,768]{1,0:T(8,128)(2,1)S(1)}, bf16[32,768]{1,0:T(8,128)(2,1)S(1)}, u32[]{:S(2)}, u32[]{:S(2)}) collective-permute-start(bf16[32,768]{1,0:T(8,128)(2,1)S(1)} %get-tuple-element.27), channel_id=1, source_target_pairs={{0,8},{1,9},{2,10},{3,11},{4,12},{5,13},{6,14},{7,15},{8,0},{9,1},... | collective-permute-start | bytes 147464 | tf_op jit(solution)/shard_map/ppermute | solution.py:269
  26.3 4.1 %collective-permute-start.3 = (bf16[32,768]{1,0:T(8,128)(2,1)S(1)}, bf16[32,768]{1,0:T(8,128)(2,1)S(1)}, u32[]{:S(2)}, u32[]{:S(2)}) collective-permute-start(bf16[32,768]{1,0:T(8,128)(2,1)S(1)} %get-tuple-element.27), channel_id=1, source_target_pairs={{0,4},{1,5},{2,6},{3,7},{4,0},{5,1},{6,2},{7,3},{8,12},{9,13},{10,... | collective-permute-start | bytes 147464 | tf_op jit(solution)/shard_map/ppermute | solution.py:269
  27.9 5.9 %collective-permute-start.5 = (bf16[32,768]{1,0:T(8,128)(2,1)S(1)}, bf16[32,768]{1,0:T(8,128)(2,1)S(1)}, u32[]{:S(2)}, u32[]{:S(2)}) collective-permute-start(bf16[32,768]{1,0:T(8,128)(2,1)S(1)} %get-tuple-element.27), channel_id=1, source_target_pairs={{0,12},{1,13},{2,14},{3,15},{4,8},{5,9},{6,10},{7,11},{8,4},{9,5},... | collective-permute-start | bytes 147464 | tf_op jit(solution)/shard_map/ppermute | solution.py:269
  34.8 7.4 %collective-permute-start.8 = (bf16[72,768]{1,0:T(8,128)(2,1)S(1)}, bf16[72,768]{1,0:T(8,128)(2,1)S(1)}, u32[]{:S(2)}, u32[]{:S(2)}) collective-permute-start(bf16[72,768]{1,0:T(8,128)(2,1)S(1)} %reshape.57), channel_id=1, source_target_pairs={{0,18},{1,19},{2,16},{3,17},{4,22},{5,23},{6,20},{7,21},{8,26},{9,... | collective-permute-start | bytes 331784 | tf_op jit(solution)/shard_map/ppermute | solution.py:262
  36.6 5.5 %collective-permute-start.6 = (bf16[72,768]{1,0:T(8,128)(2,1)S(1)}, bf16[72,768]{1,0:T(8,128)(2,1)S(1)}, u32[]{:S(2)}, u32[]{:S(2)}) collective-permute-start(bf16[72,768]{1,0:T(8,128)(2,1)S(1)} %reshape.57), channel_id=1, source_target_pairs={{0,2},{1,3},{2,0},{3,1},{4,6},{5,7},{6,4},{7,5},{8,10},{9,11},{10,... | collective-permute-start | bytes 331784 | tf_op jit(solution)/shard_map/ppermute | solution.py:262
  37.3 4.8 %collective-permute-start.7 = (bf16[72,768]{1,0:T(8,128)(2,1)S(1)}, bf16[72,768]{1,0:T(8,128)(2,1)S(1)}, u32[]{:S(2)}, u32[]{:S(2)}) collective-permute-start(bf16[72,768]{1,0:T(8,128)(2,1)S(1)} %reshape.56), channel_id=1, source_target_pairs={{0,16},{1,17},{2,18},{3,19},{4,20},{5,21},{6,22},{7,23},{8,24},{9,... | collective-permute-start | bytes 331784 | tf_op jit(solution)/shard_map/ppermute | solution.py:262
  42.2 1.9 %collective-permute-start.9 = (bf16[2,144,768]{2,1,0:T(8,128)(2,1)S(1)}, bf16[2,144,768]{2,1,0:T(8,128)(2,1)S(1)}, u32[]{:S(2)}, u32[]{:S(2)}) collective-permute-start(bf16[2,144,768]{2,1,0:T(8,128)(2,1)S(1)} %pad_maximum_fusion.own_ref), channel_id=1, source_target_pairs={{0,1},{1,0},{2,3},{3,2},{4,5},{5,4},{6,7},{7,6},{8,9},{9,8},{10,11... | collective-permute-start | bytes 1327112 | tf_op jit(solution)/shard_map/ppermute | solution.py:262
  44.1 1.6 %copy-start.2 = (bf16[1,2880,360]{1,2,0:T(8,128)(2,1)S(1)}, bf16[1,2880,360]{1,2,0:T(8,128)(2,1)}, u32[]{:S(2)}) copy-start(bf16[1,2880,360]{1,2,0:T(8,128)(2,1)} %param.28) | copy-start | bytes 6220804
  45.7 1.6 %copy-start.3 = (bf16[1,360,2880]{2,1,0:T(8,128)(2,1)S(1)}, bf16[1,360,2880]{2,1,0:T(8,128)(2,1)}, u32[]{:S(2)}) copy-start(bf16[1,360,2880]{2,1,0:T(8,128)(2,1)} %down_ref.1) | copy-start | bytes 6220804
  50.0 1.9 %collective-permute-start.10 = (bf16[2,144,720]{2,1,0:T(8,128)(2,1)S(1)}, bf16[2,144,720]{2,1,0:T(8,128)(2,1)S(1)}, u32[]{:S(2)}, u32[]{:S(2)}) collective-permute-start(bf16[2,144,720]{2,1,0:T(8,128)(2,1)S(1)} %get-tuple-element.13), channel_id=1, source_target_pairs={{0,1},{1,0},{2,3},{3,2},{4,5},{5,4},{6,7},{7,6},{8,9},{9,8},{10,11... | collective-permute-start | bytes 1244168 | tf_op jit(solution)/shard_map/ppermute | solution.py:262
  52.0 5.6 %collective-permute-start.11 = (bf16[72,720]{1,0:T(8,128)(2,1)S(1)}, bf16[72,720]{1,0:T(8,128)(2,1)S(1)}, u32[]{:S(2)}, u32[]{:S(2)}) collective-permute-start(bf16[72,720]{1,0:T(8,128)(2,1)S(1)} %get-tuple-element.18), channel_id=1, source_target_pairs={{0,16},{1,17},{2,18},{3,19},{4,20},{5,21},{6,22},{7,23},{8,24},{9,... | collective-permute-start | bytes 311048 | tf_op jit(solution)/shard_map/ppermute | solution.py:262
  53.3 7.3 %collective-permute-start.13 = (bf16[72,720]{1,0:T(8,128)(2,1)S(1)}, bf16[72,720]{1,0:T(8,128)(2,1)S(1)}, u32[]{:S(2)}, u32[]{:S(2)}) collective-permute-start(bf16[72,720]{1,0:T(8,128)(2,1)S(1)} %get-tuple-element.19), channel_id=1, source_target_pairs={{0,18},{1,19},{2,16},{3,17},{4,22},{5,23},{6,20},{7,21},{8,26},{9,... | collective-permute-start | bytes 311048 | tf_op jit(solution)/shard_map/ppermute | solution.py:262
  55.1 6.9 %collective-permute-start.12 = (bf16[72,720]{1,0:T(8,128)(2,1)S(1)}, bf16[72,720]{1,0:T(8,128)(2,1)S(1)}, u32[]{:S(2)}, u32[]{:S(2)}) collective-permute-start(bf16[72,720]{1,0:T(8,128)(2,1)S(1)} %get-tuple-element.20), channel_id=1, source_target_pairs={{0,2},{1,3},{2,0},{3,1},{4,6},{5,7},{6,4},{7,5},{8,10},{9,11},{10,... | collective-permute-start | bytes 311048 | tf_op jit(solution)/shard_map/ppermute | solution.py:262
  62.6 4.4 %collective-permute-start.14 = (bf16[32,720]{1,0:T(8,128)(2,1)S(1)}, bf16[32,720]{1,0:T(8,128)(2,1)S(1)}, u32[]{:S(2)}, u32[]{:S(2)}) collective-permute-start(bf16[32,720]{1,0:T(8,128)(2,1)S(1)} %get-tuple-element.21), channel_id=1, source_target_pairs={{0,4},{1,5},{2,6},{3,7},{4,0},{5,1},{6,2},{7,3},{8,12},{9,13},{10,... | collective-permute-start | bytes 138248 | tf_op jit(solution)/shard_map/ppermute | solution.py:269
  62.7 6.0 %collective-permute-start.16 = (bf16[32,720]{1,0:T(8,128)(2,1)S(1)}, bf16[32,720]{1,0:T(8,128)(2,1)S(1)}, u32[]{:S(2)}, u32[]{:S(2)}) collective-permute-start(bf16[32,720]{1,0:T(8,128)(2,1)S(1)} %get-tuple-element.22), channel_id=1, source_target_pairs={{0,12},{1,13},{2,14},{3,15},{4,8},{5,9},{6,10},{7,11},{8,4},{9,5},... | collective-permute-start | bytes 138248 | tf_op jit(solution)/shard_map/ppermute | solution.py:269
  64.7 5.7 %collective-permute-start.15 = (bf16[32,720]{1,0:T(8,128)(2,1)S(1)}, bf16[32,720]{1,0:T(8,128)(2,1)S(1)}, u32[]{:S(2)}, u32[]{:S(2)}) collective-permute-start(bf16[32,720]{1,0:T(8,128)(2,1)S(1)} %get-tuple-element.23), channel_id=1, source_target_pairs={{0,8},{1,9},{2,10},{3,11},{4,12},{5,13},{6,14},{7,15},{8,0},{9,1},... | collective-permute-start | bytes 138248 | tf_op jit(solution)/shard_map/ppermute | solution.py:269

commit v3 on v2

--- a/solution.py
+++ b/solution.py
@@ -15,6 +15,7 @@
 
 
 epsilon = 1e-05
+COVER = 1 << 33
 
 
 def attend_kernel(
@@ -23,7 +24,7 @@
 ):
     outs, rest = rest[:parts], rest[parts:]
     len_ref, start_ref, q_ref, kn_ref, vn_ref, kbuf, vbuf, wobuf = rest[:8]
-    queries, heads, small, ksem, vsem, wsem = rest[8:]
+    queries, heads, scores, products, small, ksem, vsem, wsem = rest[8:]
     tokens, window, lanes = k_hbm.shape
     pairs = (
         (q_hbm, q_ref), (kn_hbm, kn_ref), (vn_hbm, vn_ref), (len_hbm, len_ref),
@@ -75,29 +76,37 @@
     slots = lax.broadcasted_iota(jnp.int32, (1, window), 1)
     own_keys = kn_ref[...].astype(jnp.float32)
     own_values = vn_ref[...].astype(jnp.float32)
+    block = step * n_heads
     for n in range(chunks):
         kcopy(n).wait()
-        vcopy(n).wait()
         for t in range(n * step, (n + 1) * step):
-            at = pl.ds(t, n_heads, stride=tokens)
-            query = queries[at, :]
-            scores = factor * lax.dot_general(
+            query = queries[pl.ds(t, n_heads, stride=tokens), :]
+            dots = lax.dot_general(
                 query.astype(jnp.bfloat16), kbuf[t], (((1,), (1,)), ((), ())),
                 preferred_element_type=jnp.float32,
             )
-            own = factor * jnp.sum(query * own_keys[t : t + 1, :], axis=1, keepdims=True)
             age = slots - start_ref[t]
             age = jnp.where(age < 0, age + window, age)
-            usable = age < len_ref[t]
-            masked = jnp.where(usable, scores, -1e30)
-            highest = jnp.maximum(jnp.max(masked, axis=1, keepdims=True), own)
-            lifted = jnp.where(usable, jnp.exp(masked - highest), 0.0)
-            own_lift = jnp.exp(own - highest)
-            denominator = jnp.sum(lifted, axis=1, keepdims=True) + own_lift
-            weights = (lifted / denominator).astype(jnp.bfloat16)
-            own_weight = (own_lift / denominator).astype(jnp.bfloat16).astype(jnp.float32)
-            mixed = jnp.dot(weights, vbuf[t], preferred_element_type=jnp.float32)
-            heads[at, :] = mixed + own_weight * own_values[t : t + 1, :]
+            at = pl.ds(t * n_heads, n_heads)
+            scores[at, :] = jnp.where(age < len_ref[t], factor * dots, -1e30)
+            products[at, :] = query * own_keys[t : t + 1, :]
+    for n in range(chunks):
+        at = pl.ds(n * block, block)
+        masked = scores[at, :]
+        own = factor * jnp.sum(products[at, :], axis=1, keepdims=True)
+        highest = jnp.maximum(jnp.max(masked, axis=1, keepdims=True), own)
+        lifted = jnp.exp(masked - highest)
+        own_lift = jnp.exp(own - highest)
+        denominator = jnp.sum(lifted, axis=1, keepdims=True) + own_lift
+        weights = (lifted / denominator).astype(jnp.bfloat16)
+        own_weight = (own_lift / denominator).astype(jnp.bfloat16).astype(jnp.float32)
+        vcopy(n).wait()
+        for m in range(step):
+            t = n * step + m
+            mine = slice(m * n_heads, (m + 1) * n_heads)
+            mixed = jnp.dot(weights[mine], vbuf[t], preferred_element_type=jnp.float32)
+            mixed = mixed + own_weight[mine] * own_values[t : t + 1, :]
+            heads[pl.ds(t, n_heads, stride=tokens), :] = mixed
     columns = []
     for c in range(n_heads // per):
         column = None
@@ -150,6 +159,8 @@
             pltpu.VMEM(v_cache.shape, v_cache.dtype),
             pltpu.VMEM(out_proj.shape, out_proj.dtype),
             pltpu.VMEM((n_heads * tokens, lanes), jnp.float32),
+            pltpu.VMEM((n_heads * tokens, lanes), jnp.float32),
+            pltpu.VMEM((n_heads * tokens, window), jnp.float32),
             pltpu.VMEM((n_heads * tokens, lanes), jnp.float32),
             pltpu.SemaphoreType.DMA((5,)),
             pltpu.SemaphoreType.DMA((chunks,)),
@@ -230,12 +241,170 @@
     )(place, own, other, w_gate, w_up, w_down)
 
 
-def split3(x):
-    high = lax.reduce_precision(x, 8, 7)
+def three_parts(x):
+    high = x.astype(jnp.bfloat16).astype(jnp.float32)
     rest = x - high
-    middle = lax.reduce_precision(rest, 8, 7)
-    low = rest - middle
-    return [part.astype(jnp.bfloat16) for part in (high, middle, low)]
+    middle = rest.astype(jnp.bfloat16).astype(jnp.float32)
+    return high, middle, rest - middle
+
+
+def pack_kernel(own_ref, *rest, moved):
+    arrived, rest = rest[:moved], rest[moved:]
+    residual_ref, gain_ref, router_ref, ids_ref, attended_ref, packed_ref = rest
+    stream = residual_ref[...].astype(jnp.float32) + own_ref[...]
+    for ref in arrived:
+        stream = stream + ref[...].astype(jnp.float32)
+    attended_ref[...] = stream.astype(jnp.bfloat16)
+    tokens, quarter = stream.shape
+    topk = ids_ref.shape[0]
+    scaled = (stream * gain_ref[...]).astype(jnp.bfloat16)
+    squares = jnp.sum(stream * stream, axis=1, keepdims=True)
+    logits = lax.dot_general(
+        scaled, router_ref[...], (((1,), (1,)), ((), ())), preferred_element_type=jnp.float32
+    )
+    names = lax.broadcasted_iota(jnp.int32, logits.shape, 1).astype(jnp.float32)
+    eye = (
+        lax.broadcasted_iota(jnp.int32, (topk, topk), 0)
+        == lax.broadcasted_iota(jnp.int32, (topk, topk), 1)
+    )
+    ids = lax.dot_general(
+        ids_ref[...].astype(jnp.float32).astype(jnp.bfloat16), eye.astype(jnp.bfloat16),
+        (((0,), (0,)), ((), ())), preferred_element_type=jnp.float32,
+    )
+    stats = [squares]
+    columns = []
+    for k in range(topk):
+        chosen = ids[:, k : k + 1]
+        columns.append(chosen)
+        stats.append(jnp.sum(jnp.where(names == chosen, logits, 0.0), axis=1, keepdims=True))
+    split = [three_parts(x) for x in stats]
+    for p in range(3):
+        columns.extend(x[p] for x in split)
+    tail_at = quarter // 128 * 128
+    first = quarter - tail_at
+    packed_ref[:, :quarter] = scaled
+    tile = packed_ref[:, tail_at : tail_at + 128]
+    lane = lax.broadcasted_iota(jnp.int32, (tokens, 128), 1)
+    tail = jnp.zeros((tokens, 128), jnp.float32)
+    for c, x in enumerate(columns):
+        tail = jnp.where(lane == first + c, x, tail)
+    packed_ref[:, tail_at : tail_at + 128] = jnp.where(
+        lane < first, tile.astype(jnp.float32), tail
+    ).astype(jnp.bfloat16)
+
+
+def run_pack(own, arrived, residual, gain, router, route_ids):
+    tokens, quarter = residual.shape
+    vmem = pl.BlockSpec(memory_space=pltpu.VMEM)
+    lanes = quarter // 128 * 128 + 128
+    assert quarter % 128 + 4 * route_ids.shape[0] + 3 <= 128
+    return pl.pallas_call(
+        functools.partial(pack_kernel, moved=len(arrived)),
+        in_specs=[vmem] * (5 + len(arrived)),
+        out_specs=[vmem, vmem],
+        out_shape=[
+            jax.ShapeDtypeStruct((tokens, quarter), jnp.bfloat16),
+            jax.ShapeDtypeStruct((tokens, lanes), jnp.bfloat16),
+        ],
+        compiler_params=pltpu.CompilerParams(vmem_limit_bytes=4 << 20),
+        cost_estimate=pl.CostEstimate(flops=COVER, transcendentals=0, bytes_accessed=1 << 20),
+        name="pack",
+    )(own, *arrived, residual, gain, router, route_ids)
+
+
+def select_kernel(expert_ref, *rest, n_far, n_near, cap, topk, quarter):
+    blocks, rest = rest[:n_far], rest[n_far:]
+    rows, picks = rest[:n_near], rest[n_near:]
+    tokens, lanes = blocks[0].shape
+    tail_at = quarter // 128 * 128
+    first = quarter - tail_at
+    stacked = jnp.concatenate([ref[...] for ref in blocks], axis=0)
+    ids = stacked[:, tail_at:].astype(jnp.float32)
+    n_all = n_far * tokens
+    down = lax.broadcasted_iota(jnp.int32, (tokens, tokens), 0)
+    across = lax.broadcasted_iota(jnp.int32, (tokens, tokens), 1)
+    before = (across < down).astype(jnp.bfloat16)
+    slot = lax.broadcasted_iota(jnp.int32, (n_all, n_far * cap), 1).astype(jnp.float32)
+    base = (lax.broadcasted_iota(jnp.int32, (n_all, 1), 0) // tokens * cap).astype(jnp.float32)
+    hits = []
+    for j in range(n_near):
+        expert = expert_ref[j].astype(jnp.float32)
+        hit = jnp.zeros((n_all, 1), jnp.float32)
+        for k in range(topk):
+            hit = hit + jnp.where(ids[:, first + k : first + k + 1] == expert, 1.0, 0.0)
+        hits.append(hit)
+    lane = lax.broadcasted_iota(jnp.int32, (n_all, 128), 1)
+    table = jnp.zeros((n_all, 128), jnp.float32)
+    for j in range(n_near):
+        table = jnp.where(lane == j, hits[j], table)
+    table = table.astype(jnp.bfloat16)
+    ranks = jnp.concatenate(
+        [
+            jnp.dot(
+                before, table[n * tokens : (n + 1) * tokens], preferred_element_type=jnp.float32
+            )
+            for n in range(n_far)
+        ],
+        axis=0,
+    )
+    for j in range(n_near):
+        at = jnp.where(hits[j] > 0.0, ranks[:, j : j + 1] + base, -1.0)
+        pick = jnp.where(at == slot, 1.0, 0.0).astype(jnp.bfloat16)
+        picks[j][...] = pick
+        rows[j][...] = lax.dot_general(
+            pick, stacked, (((0,), (0,)), ((), ())), preferred_element_type=jnp.float32
+        ).astype(jnp.bfloat16)
+
+
+def run_select(experts, blocks, n_near, cap, topk, quarter):
+    tokens, lanes = blocks[0].shape
+    n_far = len(blocks)
+    vmem = pl.BlockSpec(memory_space=pltpu.VMEM)
+    outs = [jax.ShapeDtypeStruct((n_far * cap, lanes), jnp.bfloat16)] * n_near
+    outs += [jax.ShapeDtypeStruct((n_far * tokens, n_far * cap), jnp.bfloat16)] * n_near
+    made = pl.pallas_call(
+        functools.partial(
+            select_kernel, n_far=n_far, n_near=n_near, cap=cap, topk=topk, quarter=quarter
+        ),
+        in_specs=[pl.BlockSpec(memory_space=pltpu.SMEM)] + [vmem] * n_far,
+        out_specs=[vmem] * len(outs),
+        out_shape=outs,
+        compiler_params=pltpu.CompilerParams(vmem_limit_bytes=12 << 20),
+        name="select",
+    )(experts, *blocks)
+    return made[:n_near], made[n_near:]
+
+
+def spread_kernel(*refs, n_near, n_role, n_far):
+    rows, refs = refs[: n_near * n_role], refs[n_near * n_role :]
+    picks, outs = refs[:n_near], refs[n_near:]
+    total = 0.0
+    for j in range(n_near):
+        row = 0.0
+        for i in range(n_role):
+            row = row + rows[j * n_role + i][...].astype(jnp.float32)
+        total = total + jnp.dot(
+            picks[j][...], row.astype(jnp.bfloat16), preferred_element_type=jnp.float32
+        )
+    tokens = total.shape[0] // n_far
+    for n in range(n_far):
+        outs[n][...] = total[n * tokens : (n + 1) * tokens].astype(outs[n].dtype)
+
+
+def run_spread(rows, picks, n_role, n_far):
+    n_near = len(picks)
+    tokens = picks[0].shape[0] // n_far
+    vmem = pl.BlockSpec(memory_space=pltpu.VMEM)
+    quarter = rows[0].shape[1]
+    kinds = [jnp.float32] + [jnp.bfloat16] * (n_far - 1)
+    return pl.pallas_call(
+        functools.partial(spread_kernel, n_near=n_near, n_role=n_role, n_far=n_far),
+        in_specs=[vmem] * (len(rows) + n_near),
+        out_specs=[vmem] * n_far,
+        out_shape=[jax.ShapeDtypeStruct((tokens, quarter), kind) for kind in kinds],
+        compiler_params=pltpu.CompilerParams(vmem_limit_bytes=12 << 20),
+        name="spread",
+    )(*rows, *picks)
 
 
 def swap_table(mesh, grp_of, role_flip, tp_flip):
@@ -285,37 +454,14 @@
         pieces = attend_project(
             place, q_new, k_new, v_new, k_cache, v_cache, cache_len, cycle_start, out_proj.T, parts
         )
-        stream = residual.astype(jnp.float32) + pieces[0]
-        for k in (2, 3, 1):
-            moved = send(pieces[k], role=k // n_tp, tp=k % n_tp)
-            stream = stream + moved.astype(jnp.float32)
-        attended = stream.astype(jnp.bfloat16)
-        gain = lax.dynamic_slice_in_dim(norm_gain, share * quarter, quarter, 0)
-        scaled = (stream * gain).astype(jnp.bfloat16)
-        squares = jnp.sum(stream * stream, axis=1, keepdims=True)
-        logits = jnp.dot(scaled, router, preferred_element_type=jnp.float32)
-        named = route_ids[:, :, None] == jnp.arange(experts, dtype=jnp.int32)
-        chosen = jnp.sum(jnp.where(named, logits[:, None, :], 0.0), axis=2)
-        stats = split3(jnp.concatenate([squares, chosen], axis=1))
-        packed = jnp.concatenate([scaled, route_ids.astype(jnp.bfloat16)] + stats, axis=1)
-        lanes = -(-packed.shape[1] // 128) * 128
-        packed = jnp.pad(packed, ((0, 0), (0, lanes - packed.shape[1])))
-        gathered = jnp.stack([packed] + [send_far(packed, k) for k in range(1, n_far)])
-        ids = gathered[:, :, quarter : quarter + topk].astype(jnp.float32)
-        rows = {}
-        selects = []
-        for j in range(n_near):
-            expert = (far * n_near + (near ^ j)).astype(jnp.float32)
-            hit = jnp.sum((ids == expert).astype(jnp.int32), axis=2)
-            rank = jnp.cumsum(hit, axis=1) - hit
-            select = (hit[:, None, :] > 0) & (
-                rank[:, None, :] == jnp.arange(cap, dtype=jnp.int32)[:, None]
-            )
-            select = select.astype(jnp.bfloat16)
-            selects.append(select)
-            rows[j] = jnp.einsum(
-                "kct,ktw->kcw", select, gathered, preferred_element_type=jnp.float32
-            ).astype(jnp.bfloat16).reshape(n_far * cap, lanes)
+        moved = [send(pieces[k], role=k // n_tp, tp=k % n_tp) for k in range(1, parts)]
+        gain = lax.dynamic_slice_in_dim(norm_gain, share * quarter, quarter, 0).reshape(1, quarter)
+        attended, packed = run_pack(pieces[0], moved, residual, gain, router.T, route_ids.T)
+        blocks = [packed] + [send_far(packed, k) for k in range(1, n_far)]
+        experts_near = jnp.stack([far * n_near + (near ^ j) for j in range(n_near)])
+        rows, picks = run_select(
+            experts_near.astype(jnp.int32), blocks, n_near, cap, topk, quarter
+        )
         arrived = {(0, 0): rows[0]}
         for j in range(n_near):
             for i in range(n_role):
@@ -334,17 +480,12 @@
         acc = acc.astype(jnp.bfloat16).reshape(n_role, n_near, n_far * cap, quarter)
         back = []
         for j in range(n_near):
-            total_rows = 0.0
             for i in range(n_role):
                 piece = acc[i, j]
                 if (j, i) != (0, 0):
                     piece = send(piece, near=j, role=i)
-                total_rows = total_rows + piece.astype(jnp.float32)
-            back.append(total_rows.astype(jnp.bfloat16).reshape(n_far, cap, quarter))
-        spread = sum(
-            jnp.einsum("kct,kcw->ktw", s, b, preferred_element_type=jnp.float32)
-            for s, b in zip(selects, back)
-        ).astype(jnp.bfloat16)
+                back.append(piece)
+        spread = run_spread(back, picks, n_role, n_far)
         mix = spread[0].astype(jnp.float32)
         for k in range(1, n_far):
             mix = mix + send_far(spread[k], k if xor_far else n_far - k).astype(jnp.float32)

time: 71.4 us -> 57.8 us (0.81)
  Pallas kernels: 17.7 us -> 11.6 us
  local copies, waits for them, and re-layouts: 4.58 us -> 0.84 us
  waiting for transfers between devices: 25.9 us -> 24 us
  other arithmetic: 2.53 us -> 0.98 us
  matrix products: 0.97 us -> 0 us
    pallas_call x1, Pallas kernels: 14.9 us -> 6.7 us  [attend_project(): pl.pallas_call(functools.partial(attend_kernel, grouped=HEADS // KV_HEADS...]
    unnamed x12, local copies, waits for them, and re-layouts: 3.22 us -> 0.03 us
    pallas_call x0 -> x3, Pallas kernels: none -> 2.14 us  [the longest x1 1.22 us: run_select(): pl.pallas_call(functools.partial(select_kernel, n_far=n_far, n_near=n_nea...]
    ppermute x6, waiting for transfers between devices: 9.96 us -> 8.46 us  [send_far(): return lax.ppermute(x, names, swap_table(mesh, grp_of, 0, 0))]
    dot_general x5 -> x0, matrix products: 0.97 us -> none  [the longest x2 0.51 us: local(): jnp.einsum('kct,kcw->ktw', s, b, preferred_element_type=jnp.float32)]
    ppermute x6, starting transfers between devices: 8 us -> 8.84 us  [send_far(): return lax.ppermute(x, names, swap_table(mesh, grp_of, 0, 0))]
where the time goes in v3:
time: 57.8 us; the launch traced here: 57.6 us
  waiting for transfers between devices  24 us (42%)
  starting transfers between devices  19.4 us (34%)
  Pallas kernels  11.6 us (20%)
  other arithmetic  0.98 us (2%)
  local copies, waits for them, and re-layouts  0.84 us (1%)
  between operations  0.78 us (1%)
    ppermute x11, waiting for transfers between devices, send(): lax.ppermute(x, names, swap_table(mesh, lambda g: g ^ near, role, tp))  15.5 us
    ppermute x11, starting transfers between devices, send(): lax.ppermute(x, names, swap_table(mesh, lambda g: g ^ near, role, tp))  10.5 us
    ppermute x6, starting transfers between devices, send_far(): return lax.ppermute(x, names, swap_table(mesh, grp_of, 0, 0))  8.84 us
    ppermute x6, waiting for transfers between devices, send_far(): return lax.ppermute(x, names, swap_table(mesh, grp_of, 0, 0))  8.46 us
    pallas_call x1, Pallas kernels, attend_project(): pl.pallas_call(functools.partial(attend_kernel, grouped=HEADS // KV_HEADS...  6.7 us
    pallas_call x1, Pallas kernels, run_expert(): pl.pallas_call(functools.partial(expert_kernel, quarter=quarter, topk=top...  2.76 us
    pallas_call x1, Pallas kernels, run_select(): pl.pallas_call(functools.partial(select_kernel, n_far=n_far, n_near=n_nea...  1.22 us
  transfers between devices with their start and end apart: 17, of which 14 were waited for; matrix products, arithmetic and copies ran while one was open for 2% of the time, Pallas kernels for 0%

profile of v3, /device:TPU:0, one launch (start us, length us, event | category | flops | bytes accessed | tf_op | source)
XLA Modules:
  0.0 57.6 jit_solution(13372931683429433296)
XLA Ops:
  0.7 6.7 %attend_project.1 = (f32[32,720]{1,0:T(8,128)S(1)}, bf16[32,720]{1,0:T(8,128)(2,1)S(1)}, bf16[32,720]{1,0:T(8,128)(2,1)S(1)}, bf16[32,720]{1,0:T(8,128)(2,1)S(1)}) custom-call(s32[1]{0:T(128)} %bitcast.share_ref, s32[32]{0:T(128)} %len_hbm.1, s32[32]{0:T(128)} %start_hbm.1, bf16[32,1024]{1,0:T(8,128)(2,1)} %q_hbm.1, bf16[32,128]{1,0:T(8,128)(2,1)} %kn_hbm.1, ...), custom_call_target="tpu_custom_call" | custom-call | tf_op jit(solution)/shard_map/attend_project/pallas_call | solution.py:145
  7.4 0.6 collective-permute-start
  7.9 2.6 %collective-permute-start.1 = (bf16[32,720]{1,0:T(8,128)(2,1)S(1)}, bf16[32,720]{1,0:T(8,128)(2,1)S(1)}, u32[]{:S(2)}, u32[]{:S(2)}) collective-permute-start(bf16[32,720]{1,0:T(8,128)(2,1)S(1)} %get-tuple-element.20), channel_id=1, source_target_pairs={{0,16},{1,17},{2,18},{3,19},{4,20},{5,21},{6,22},{7,23},{8,24},{9,... | collective-permute-start | bytes 138248 | tf_op jit(solution)/shard_map/ppermute | solution.py:431
  10.5 0.8 %dynamic_slice.3 = f32[720]{0:T(1024)S(1)} dynamic-slice(f32[2880]{0:T(1024)} %param.24, s32[]{:T(128)S(6)} %select_n.14), dynamic_slice_sizes={720} | dynamic-slice | bytes 5764 | tf_op jit(solution)/shard_map/dynamic_slice | solution.py:458
  11.3 1.5 %collective-permute-done.1.rest_1_ = bf16[32,720]{1,0:T(8,128)(2,1)S(1)} collective-permute-done((bf16[32,720]{1,0:T(8,128)(2,1)S(1)}, bf16[32,720]{1,0:T(8,128)(2,1)S(1)}, u32[]{:S(2)}, u32[]{:S(2)}) %collective-permute-start.1) | collective-permute-done | bytes 46112 | tf_op jit(solution)/shard_map/ppermute | solution.py:431
  12.8 1.4 %collective-permute-done.2.rest_2_ = bf16[32,720]{1,0:T(8,128)(2,1)S(1)} collective-permute-done((bf16[32,720]{1,0:T(8,128)(2,1)S(1)}, bf16[32,720]{1,0:T(8,128)(2,1)S(1)}, u32[]{:S(2)}, u32[]{:S(2)}) %collective-permute-start.2) | collective-permute-done | bytes 46112 | tf_op jit(solution)/shard_map/ppermute | solution.py:431
  14.2 0.7 %pack.1 = (bf16[32,720]{1,0:T(8,128)(2,1)}, bf16[32,768]{1,0:T(8,128)(2,1)S(1)}) custom-call(f32[32,720]{1,0:T(8,128)S(1)} %get-tuple-element.18.own_ref, bf16[32,720]{1,0:T(8,128)(2,1)S(1)} %collective-permute-done.rest_0_, bf16[32,720]{1,0:T(8,128)(2,1)S(1)} %collective-permute-done.1.rest_1_, bf16[32,720]{1,0:T(8,128)(2,1)S(1)} %collective-permute-done.2.rest_2_, ...), custom_call_target="tpu_custom_call" | custom-call | flops 8589934592 | bytes 1048576 | tf_op jit(solution)/shard_map/pack/pallas_call | solution.py:301
  14.9 3.6 %collective-permute-start.5 = (bf16[32,768]{1,0:T(8,128)(2,1)S(1)}, bf16[32,768]{1,0:T(8,128)(2,1)S(1)}, u32[]{:S(2)}, u32[]{:S(2)}) collective-permute-start(bf16[32,768]{1,0:T(8,128)(2,1)S(1)} %get-tuple-element.23.rest_0_), channel_id=1, source_target_pairs={{0,12},{1,13},{2,14},{3,15},{4,8},{5,9},{6,10},{7,11},{8,4},{9,5},... | collective-permute-start | bytes 147464 | tf_op jit(solution)/shard_map/ppermute | solution.py:438
  18.5 0.8 %collective-permute-start.3 = (bf16[32,768]{1,0:T(8,128)(2,1)S(1)}, bf16[32,768]{1,0:T(8,128)(2,1)S(1)}, u32[]{:S(2)}, u32[]{:S(2)}) collective-permute-start(bf16[32,768]{1,0:T(8,128)(2,1)S(1)} %get-tuple-element.23.rest_0_), channel_id=1, source_target_pairs={{0,4},{1,5},{2,6},{3,7},{4,0},{5,1},{6,2},{7,3},{8,12},{9,13},{10,... | collective-permute-start | bytes 147464 | tf_op jit(solution)/shard_map/ppermute | solution.py:438
  19.4 1.4 %collective-permute-done.5.rest_3_ = bf16[32,768]{1,0:T(8,128)(2,1)S(1)} collective-permute-done((bf16[32,768]{1,0:T(8,128)(2,1)S(1)}, bf16[32,768]{1,0:T(8,128)(2,1)S(1)}, u32[]{:S(2)}, u32[]{:S(2)}) %collective-permute-start.5) | collective-permute-done | bytes 49184 | tf_op jit(solution)/shard_map/ppermute | solution.py:438
  20.8 2.7 %collective-permute-done.4.rest_2_ = bf16[32,768]{1,0:T(8,128)(2,1)S(1)} collective-permute-done((bf16[32,768]{1,0:T(8,128)(2,1)S(1)}, bf16[32,768]{1,0:T(8,128)(2,1)S(1)}, u32[]{:S(2)}, u32[]{:S(2)}) %collective-permute-start.4) | collective-permute-done | bytes 49184 | tf_op jit(solution)/shard_map/ppermute | solution.py:438
  23.5 1.2 %select.7 = (bf16[72,768]{1,0:T(8,128)(2,1)S(1)}, bf16[72,768]{1,0:T(8,128)(2,1)S(1)}, bf16[128,72]{1,0:T(8,128)(2,1)S(1)}, bf16[128,72]{1,0:T(8,128)(2,1)S(1)}) custom-call(s32[2]{0:T(128)S(1)} %pad_add_fusion.1.expert_ref, bf16[32,768]{1,0:T(8,128)(2,1)S(1)} %get-tuple-element.23.rest_0_, bf16[32,768]{1,0:T(8,128)(2,1)S(1)} %collective-permute-done.3.rest_1_, ...), custom_call_target="tpu_custom_call" | custom-call | tf_op jit(solution)/shard_map/select/pallas_call | solution.py:365
  24.7 1.6 %collective-permute-start.6 = (bf16[72,768]{1,0:T(8,128)(2,1)S(1)}, bf16[72,768]{1,0:T(8,128)(2,1)S(1)}, u32[]{:S(2)}, u32[]{:S(2)}) collective-permute-start(bf16[72,768]{1,0:T(8,128)(2,1)S(1)} %get-tuple-element.25), channel_id=1, source_target_pairs={{0,2},{1,3},{2,0},{3,1},{4,6},{5,7},{6,4},{7,5},{8,10},{9,11},{10,... | collective-permute-start | bytes 331784 | tf_op jit(solution)/shard_map/ppermute | solution.py:431
  26.3 1.0 %collective-permute-start.8 = (bf16[72,768]{1,0:T(8,128)(2,1)S(1)}, bf16[72,768]{1,0:T(8,128)(2,1)S(1)}, u32[]{:S(2)}, u32[]{:S(2)}) collective-permute-start(bf16[72,768]{1,0:T(8,128)(2,1)S(1)} %get-tuple-element.25), channel_id=1, source_target_pairs={{0,18},{1,19},{2,16},{3,17},{4,22},{5,23},{6,20},{7,21},{8,26},{9,... | collective-permute-start | bytes 331784 | tf_op jit(solution)/shard_map/ppermute | solution.py:431
  27.3 1.0 %collective-permute-start.7 = (bf16[72,768]{1,0:T(8,128)(2,1)S(1)}, bf16[72,768]{1,0:T(8,128)(2,1)S(1)}, u32[]{:S(2)}, u32[]{:S(2)}) collective-permute-start(bf16[72,768]{1,0:T(8,128)(2,1)S(1)} %get-tuple-element.24), channel_id=1, source_target_pairs={{0,16},{1,17},{2,18},{3,19},{4,20},{5,21},{6,22},{7,23},{8,24},{9,... | collective-permute-start | bytes 331784 | tf_op jit(solution)/shard_map/ppermute | solution.py:431
  28.3 2.4 %collective-permute-done.6 = bf16[72,768]{1,0:T(8,128)(2,1)S(1)} collective-permute-done((bf16[72,768]{1,0:T(8,128)(2,1)S(1)}, bf16[72,768]{1,0:T(8,128)(2,1)S(1)}, u32[]{:S(2)}, u32[]{:S(2)}) %collective-permute-start.6) | collective-permute-done | bytes 110624 | tf_op jit(solution)/shard_map/ppermute | solution.py:431
  30.8 1.8 %collective-permute-done.7 = bf16[72,768]{1,0:T(8,128)(2,1)S(1)} collective-permute-done((bf16[72,768]{1,0:T(8,128)(2,1)S(1)}, bf16[72,768]{1,0:T(8,128)(2,1)S(1)}, u32[]{:S(2)}, u32[]{:S(2)}) %collective-permute-start.7) | collective-permute-done | bytes 110624 | tf_op jit(solution)/shard_map/ppermute | solution.py:431
  32.8 1.7 %collective-permute-done.9.other_ref = bf16[2,144,768]{2,1,0:T(8,128)(2,1)S(1)} collective-permute-done((bf16[2,144,768]{2,1,0:T(8,128)(2,1)S(1)}, bf16[2,144,768]{2,1,0:T(8,128)(2,1)S(1)}, u32[]{:S(2)}, u32[]{:S(2)}) %collective-permute-start.9) | collective-permute-done | bytes 442400 | tf_op jit(solution)/shard_map/ppermute | solution.py:431
  34.5 2.8 %expert.1 = (bf16[2,144,720]{2,1,0:T(8,128)(2,1)S(1)}, bf16[2,144,720]{2,1,0:T(8,128)(2,1)S(1)}) custom-call(s32[2]{0:T(128)S(1)} %pad_add_fusion.place_ref, bf16[2,144,768]{2,1,0:T(8,128)(2,1)S(1)} %pad_maximum_fusion.own_ref, bf16[2,144,768]{2,1,0:T(8,128)(2,1)S(1)} %collective-permute-done.9.other_ref, bf16[1,360,2880]{2,1,0:T(8,128)(2,1)S(1)} %bitcast.22, ...), custom_call_target="tpu_custom_call" | custom-call | tf_op jit(solution)/shard_map/expert/pallas_call | solution.py:233
  37.5 1.7 %collective-permute-done.10 = bf16[2,144,720]{2,1,0:T(8,128)(2,1)S(1)} collective-permute-done((bf16[2,144,720]{2,1,0:T(8,128)(2,1)S(1)}, bf16[2,144,720]{2,1,0:T(8,128)(2,1)S(1)}, u32[]{:S(2)}, u32[]{:S(2)}) %collective-permute-start.10) | collective-permute-done | bytes 414752 | tf_op jit(solution)/shard_map/ppermute | solution.py:431
  39.3 2.4 %collective-permute-start.13 = (bf16[72,720]{1,0:T(8,128)(2,1)S(1)}, bf16[72,720]{1,0:T(8,128)(2,1)S(1)}, u32[]{:S(2)}, u32[]{:S(2)}) collective-permute-start(bf16[72,720]{1,0:T(8,128)(2,1)S(1)} %get-tuple-element.34), channel_id=1, source_target_pairs={{0,18},{1,19},{2,16},{3,17},{4,22},{5,23},{6,20},{7,21},{8,26},{9,... | collective-permute-start | bytes 311048 | tf_op jit(solution)/shard_map/ppermute | solution.py:431
  41.7 0.5 collective-permute-start.12
  42.2 0.7 %collective-permute-start.11 = (bf16[72,720]{1,0:T(8,128)(2,1)S(1)}, bf16[72,720]{1,0:T(8,128)(2,1)S(1)}, u32[]{:S(2)}, u32[]{:S(2)}) collective-permute-start(bf16[72,720]{1,0:T(8,128)(2,1)S(1)} %get-tuple-element.36), channel_id=1, source_target_pairs={{0,16},{1,17},{2,18},{3,19},{4,20},{5,21},{6,22},{7,23},{8,24},{9,... | collective-permute-start | bytes 311048 | tf_op jit(solution)/shard_map/ppermute | solution.py:431
  42.9 2.6 %collective-permute-done.13.refs_3_ = bf16[72,720]{1,0:T(8,128)(2,1)S(1)} collective-permute-done((bf16[72,720]{1,0:T(8,128)(2,1)S(1)}, bf16[72,720]{1,0:T(8,128)(2,1)S(1)}, u32[]{:S(2)}, u32[]{:S(2)}) %collective-permute-start.13) | collective-permute-done | bytes 103712 | tf_op jit(solution)/shard_map/ppermute | solution.py:431
  45.5 2.3 %collective-permute-done.12.refs_2_ = bf16[72,720]{1,0:T(8,128)(2,1)S(1)} collective-permute-done((bf16[72,720]{1,0:T(8,128)(2,1)S(1)}, bf16[72,720]{1,0:T(8,128)(2,1)S(1)}, u32[]{:S(2)}, u32[]{:S(2)}) %collective-permute-start.12) | collective-permute-done | bytes 103712 | tf_op jit(solution)/shard_map/ppermute | solution.py:431
  47.9 0.3 spread.1
  48.1 0.7 %collective-permute-start.14 = (bf16[32,720]{1,0:T(8,128)(2,1)S(1)}, bf16[32,720]{1,0:T(8,128)(2,1)S(1)}, u32[]{:S(2)}, u32[]{:S(2)}) collective-permute-start(bf16[32,720]{1,0:T(8,128)(2,1)S(1)} %get-tuple-element.31), channel_id=1, source_target_pairs={{0,4},{1,5},{2,6},{3,7},{4,0},{5,1},{6,2},{7,3},{8,12},{9,13},{10,... | collective-permute-start | bytes 138248 | tf_op jit(solution)/shard_map/ppermute | solution.py:438
  48.8 2.2 %collective-permute-start.15 = (bf16[32,720]{1,0:T(8,128)(2,1)S(1)}, bf16[32,720]{1,0:T(8,128)(2,1)S(1)}, u32[]{:S(2)}, u32[]{:S(2)}) collective-permute-start(bf16[32,720]{1,0:T(8,128)(2,1)S(1)} %get-tuple-element.32), channel_id=1, source_target_pairs={{0,8},{1,9},{2,10},{3,11},{4,12},{5,13},{6,14},{7,15},{8,0},{9,1},... | collective-permute-start | bytes 138248 | tf_op jit(solution)/shard_map/ppermute | solution.py:438
  51.0 1.6 %collective-permute-start.16 = (bf16[32,720]{1,0:T(8,128)(2,1)S(1)}, bf16[32,720]{1,0:T(8,128)(2,1)S(1)}, u32[]{:S(2)}, u32[]{:S(2)}) collective-permute-start(bf16[32,720]{1,0:T(8,128)(2,1)S(1)} %get-tuple-element.33), channel_id=1, source_target_pairs={{0,12},{1,13},{2,14},{3,15},{4,8},{5,9},{6,10},{7,11},{8,4},{9,5},... | collective-permute-start | bytes 138248 | tf_op jit(solution)/shard_map/ppermute | solution.py:438
  52.8 2.8 %collective-permute-done.15 = bf16[32,720]{1,0:T(8,128)(2,1)S(1)} collective-permute-done((bf16[32,720]{1,0:T(8,128)(2,1)S(1)}, bf16[32,720]{1,0:T(8,128)(2,1)S(1)}, u32[]{:S(2)}, u32[]{:S(2)}) %collective-permute-start.15) | collective-permute-done | bytes 46112 | tf_op jit(solution)/shard_map/ppermute | solution.py:438
  55.6 1.3 %collective-permute-done.16 = bf16[32,720]{1,0:T(8,128)(2,1)S(1)} collective-permute-done((bf16[32,720]{1,0:T(8,128)(2,1)S(1)}, bf16[32,720]{1,0:T(8,128)(2,1)S(1)}, u32[]{:S(2)}, u32[]{:S(2)}) %collective-permute-start.16) | collective-permute-done | bytes 46112 | tf_op jit(solution)/shard_map/ppermute | solution.py:438
  56.9 0.6 %add_convert_fusion.1 = bf16[32,720]{1,0:T(8,128)(2,1)} fusion(bf16[32,720]{1,0:T(8,128)(2,1)S(1)} %collective-permute-done.16, bf16[32,720]{1,0:T(8,128)(2,1)S(1)} %collective-permute-done.15, f32[32,720]{1,0:T(8,128)S(1)} %get-tuple-element.30, bf16[32,720]{1,0:T(8,128)(2,1)S(1)} %collective-permute-done.14), kind=kLoop, calls=%fused_computation.8 | loop fusion | flops 161280 | bytes 276480 | tf_op jit(solution)/shard_map/convert_element_type | solution.py:492
  (29 shorter events, 1.1 us)
Async XLA Ops:
  0.6 13.6 %copy-start.3 = (bf16[32,720]{1,0:T(8,128)(2,1)S(1)}, bf16[32,720]{1,0:T(8,128)(2,1)}, u32[]{:S(2)}) copy-start(bf16[32,720]{1,0:T(8,128)(2,1)} %rest_3_.1) | copy-start | bytes 138244
  0.7 13.6 %copy-start.4 = (bf16[720,8]{0,1:T(8,128)(2,1)S(1)}, bf16[720,8]{0,1:T(8,128)(2,1)}, u32[]{:S(2)}) copy-start(bf16[720,8]{0,1:T(8,128)(2,1)} %param.25) | copy-start | bytes 34564
  0.7 13.5 %copy-start.5 = (s32[32,4]{0,1:T(4,128)S(1)}, s32[32,4]{0,1:T(4,128)}, u32[]{:S(2)}) copy-start(s32[32,4]{0,1:T(4,128)} %param.26) | copy-start | bytes 1540
  7.4 3.9 %collective-permute-start = (bf16[32,720]{1,0:T(8,128)(2,1)S(1)}, bf16[32,720]{1,0:T(8,128)(2,1)S(1)}, u32[]{:S(2)}, u32[]{:S(2)}) collective-permute-start(bf16[32,720]{1,0:T(8,128)(2,1)S(1)} %get-tuple-element.19), channel_id=1, source_target_pairs={{0,1},{1,0},{2,3},{3,2},{4,5},{5,4},{6,7},{7,6},{8,9},{9,8},{10,11... | collective-permute-start | bytes 138248 | tf_op jit(solution)/shard_map/ppermute | solution.py:431
  7.9 4.9 %collective-permute-start.1 = (bf16[32,720]{1,0:T(8,128)(2,1)S(1)}, bf16[32,720]{1,0:T(8,128)(2,1)S(1)}, u32[]{:S(2)}, u32[]{:S(2)}) collective-permute-start(bf16[32,720]{1,0:T(8,128)(2,1)S(1)} %get-tuple-element.20), channel_id=1, source_target_pairs={{0,16},{1,17},{2,18},{3,19},{4,20},{5,21},{6,22},{7,23},{8,24},{9,... | collective-permute-start | bytes 138248 | tf_op jit(solution)/shard_map/ppermute | solution.py:431
  10.5 3.7 %collective-permute-start.2 = (bf16[32,720]{1,0:T(8,128)(2,1)S(1)}, bf16[32,720]{1,0:T(8,128)(2,1)S(1)}, u32[]{:S(2)}, u32[]{:S(2)}) collective-permute-start(bf16[32,720]{1,0:T(8,128)(2,1)S(1)} %get-tuple-element.21), channel_id=1, source_target_pairs={{0,17},{1,16},{2,19},{3,18},{4,21},{5,20},{6,23},{7,22},{8,25},{9,... | collective-permute-start | bytes 138248 | tf_op jit(solution)/shard_map/ppermute | solution.py:431
  14.2 20.3 %copy-start = (bf16[1,2880,360]{1,2,0:T(8,128)(2,1)S(1)}, bf16[1,2880,360]{1,2,0:T(8,128)(2,1)}, u32[]{:S(2)}) copy-start(bf16[1,2880,360]{1,2,0:T(8,128)(2,1)} %param.27) | copy-start | bytes 6220804
  14.2 20.3 %copy-start.1 = (bf16[1,2880,360]{1,2,0:T(8,128)(2,1)S(1)}, bf16[1,2880,360]{1,2,0:T(8,128)(2,1)}, u32[]{:S(2)}) copy-start(bf16[1,2880,360]{1,2,0:T(8,128)(2,1)} %param.28) | copy-start | bytes 6220804
  14.2 20.3 %copy-start.2 = (bf16[1,360,2880]{2,1,0:T(8,128)(2,1)S(1)}, bf16[1,360,2880]{2,1,0:T(8,128)(2,1)}, u32[]{:S(2)}) copy-start(bf16[1,360,2880]{2,1,0:T(8,128)(2,1)} %down_ref.1) | copy-start | bytes 6220804
  14.9 5.9 %collective-permute-start.5 = (bf16[32,768]{1,0:T(8,128)(2,1)S(1)}, bf16[32,768]{1,0:T(8,128)(2,1)S(1)}, u32[]{:S(2)}, u32[]{:S(2)}) collective-permute-start(bf16[32,768]{1,0:T(8,128)(2,1)S(1)} %get-tuple-element.23.rest_0_), channel_id=1, source_target_pairs={{0,12},{1,13},{2,14},{3,15},{4,8},{5,9},{6,10},{7,11},{8,4},{9,5},... | collective-permute-start | bytes 147464 | tf_op jit(solution)/shard_map/ppermute | solution.py:438
  18.5 5.0 %collective-permute-start.4 = (bf16[32,768]{1,0:T(8,128)(2,1)S(1)}, bf16[32,768]{1,0:T(8,128)(2,1)S(1)}, u32[]{:S(2)}, u32[]{:S(2)}) collective-permute-start(bf16[32,768]{1,0:T(8,128)(2,1)S(1)} %get-tuple-element.23.rest_0_), channel_id=1, source_target_pairs={{0,8},{1,9},{2,10},{3,11},{4,12},{5,13},{6,14},{7,15},{8,0},{9,1},... | collective-permute-start | bytes 147464 | tf_op jit(solution)/shard_map/ppermute | solution.py:438
  18.5 5.0 %collective-permute-start.3 = (bf16[32,768]{1,0:T(8,128)(2,1)S(1)}, bf16[32,768]{1,0:T(8,128)(2,1)S(1)}, u32[]{:S(2)}, u32[]{:S(2)}) collective-permute-start(bf16[32,768]{1,0:T(8,128)(2,1)S(1)} %get-tuple-element.23.rest_0_), channel_id=1, source_target_pairs={{0,4},{1,5},{2,6},{3,7},{4,0},{5,1},{6,2},{7,3},{8,12},{9,13},{10,... | collective-permute-start | bytes 147464 | tf_op jit(solution)/shard_map/ppermute | solution.py:438
  24.7 6.0 %collective-permute-start.6 = (bf16[72,768]{1,0:T(8,128)(2,1)S(1)}, bf16[72,768]{1,0:T(8,128)(2,1)S(1)}, u32[]{:S(2)}, u32[]{:S(2)}) collective-permute-start(bf16[72,768]{1,0:T(8,128)(2,1)S(1)} %get-tuple-element.25), channel_id=1, source_target_pairs={{0,2},{1,3},{2,0},{3,1},{4,6},{5,7},{6,4},{7,5},{8,10},{9,11},{10,... | collective-permute-start | bytes 331784 | tf_op jit(solution)/shard_map/ppermute | solution.py:431
  26.3 6.3 %collective-permute-start.8 = (bf16[72,768]{1,0:T(8,128)(2,1)S(1)}, bf16[72,768]{1,0:T(8,128)(2,1)S(1)}, u32[]{:S(2)}, u32[]{:S(2)}) collective-permute-start(bf16[72,768]{1,0:T(8,128)(2,1)S(1)} %get-tuple-element.25), channel_id=1, source_target_pairs={{0,18},{1,19},{2,16},{3,17},{4,22},{5,23},{6,20},{7,21},{8,26},{9,... | collective-permute-start | bytes 331784 | tf_op jit(solution)/shard_map/ppermute | solution.py:431
  27.3 5.3 %collective-permute-start.7 = (bf16[72,768]{1,0:T(8,128)(2,1)S(1)}, bf16[72,768]{1,0:T(8,128)(2,1)S(1)}, u32[]{:S(2)}, u32[]{:S(2)}) collective-permute-start(bf16[72,768]{1,0:T(8,128)(2,1)S(1)} %get-tuple-element.24), channel_id=1, source_target_pairs={{0,16},{1,17},{2,18},{3,19},{4,20},{5,21},{6,22},{7,23},{8,24},{9,... | collective-permute-start | bytes 331784 | tf_op jit(solution)/shard_map/ppermute | solution.py:431
  32.7 1.9 %collective-permute-start.9 = (bf16[2,144,768]{2,1,0:T(8,128)(2,1)S(1)}, bf16[2,144,768]{2,1,0:T(8,128)(2,1)S(1)}, u32[]{:S(2)}, u32[]{:S(2)}) collective-permute-start(bf16[2,144,768]{2,1,0:T(8,128)(2,1)S(1)} %pad_maximum_fusion.own_ref), channel_id=1, source_target_pairs={{0,1},{1,0},{2,3},{3,2},{4,5},{5,4},{6,7},{7,6},{8,9},{9,8},{10,11... | collective-permute-start | bytes 1327112 | tf_op jit(solution)/shard_map/ppermute | solution.py:431
  37.3 1.9 %collective-permute-start.10 = (bf16[2,144,720]{2,1,0:T(8,128)(2,1)S(1)}, bf16[2,144,720]{2,1,0:T(8,128)(2,1)S(1)}, u32[]{:S(2)}, u32[]{:S(2)}) collective-permute-start(bf16[2,144,720]{2,1,0:T(8,128)(2,1)S(1)} %get-tuple-element.27), channel_id=1, source_target_pairs={{0,1},{1,0},{2,3},{3,2},{4,5},{5,4},{6,7},{7,6},{8,9},{9,8},{10,11... | collective-permute-start | bytes 1244168 | tf_op jit(solution)/shard_map/ppermute | solution.py:431
  39.3 6.2 %collective-permute-start.13 = (bf16[72,720]{1,0:T(8,128)(2,1)S(1)}, bf16[72,720]{1,0:T(8,128)(2,1)S(1)}, u32[]{:S(2)}, u32[]{:S(2)}) collective-permute-start(bf16[72,720]{1,0:T(8,128)(2,1)S(1)} %get-tuple-element.34), channel_id=1, source_target_pairs={{0,18},{1,19},{2,16},{3,17},{4,22},{5,23},{6,20},{7,21},{8,26},{9,... | collective-permute-start | bytes 311048 | tf_op jit(solution)/shard_map/ppermute | solution.py:431
  41.7 6.1 %collective-permute-start.12 = (bf16[72,720]{1,0:T(8,128)(2,1)S(1)}, bf16[72,720]{1,0:T(8,128)(2,1)S(1)}, u32[]{:S(2)}, u32[]{:S(2)}) collective-permute-start(bf16[72,720]{1,0:T(8,128)(2,1)S(1)} %get-tuple-element.35), channel_id=1, source_target_pairs={{0,2},{1,3},{2,0},{3,1},{4,6},{5,7},{6,4},{7,5},{8,10},{9,11},{10,... | collective-permute-start | bytes 311048 | tf_op jit(solution)/shard_map/ppermute | solution.py:431
  42.2 5.7 %collective-permute-start.11 = (bf16[72,720]{1,0:T(8,128)(2,1)S(1)}, bf16[72,720]{1,0:T(8,128)(2,1)S(1)}, u32[]{:S(2)}, u32[]{:S(2)}) collective-permute-start(bf16[72,720]{1,0:T(8,128)(2,1)S(1)} %get-tuple-element.36), channel_id=1, source_target_pairs={{0,16},{1,17},{2,18},{3,19},{4,20},{5,21},{6,22},{7,23},{8,24},{9,... | collective-permute-start | bytes 311048 | tf_op jit(solution)/shard_map/ppermute | solution.py:431
  48.1 4.7 %collective-permute-start.14 = (bf16[32,720]{1,0:T(8,128)(2,1)S(1)}, bf16[32,720]{1,0:T(8,128)(2,1)S(1)}, u32[]{:S(2)}, u32[]{:S(2)}) collective-permute-start(bf16[32,720]{1,0:T(8,128)(2,1)S(1)} %get-tuple-element.31), channel_id=1, source_target_pairs={{0,4},{1,5},{2,6},{3,7},{4,0},{5,1},{6,2},{7,3},{8,12},{9,13},{10,... | collective-permute-start | bytes 138248 | tf_op jit(solution)/shard_map/ppermute | solution.py:438
  48.8 6.8 %collective-permute-start.15 = (bf16[32,720]{1,0:T(8,128)(2,1)S(1)}, bf16[32,720]{1,0:T(8,128)(2,1)S(1)}, u32[]{:S(2)}, u32[]{:S(2)}) collective-permute-start(bf16[32,720]{1,0:T(8,128)(2,1)S(1)} %get-tuple-element.32), channel_id=1, source_target_pairs={{0,8},{1,9},{2,10},{3,11},{4,12},{5,13},{6,14},{7,15},{8,0},{9,1},... | collective-permute-start | bytes 138248 | tf_op jit(solution)/shard_map/ppermute | solution.py:438
  51.0 5.9 %collective-permute-start.16 = (bf16[32,720]{1,0:T(8,128)(2,1)S(1)}, bf16[32,720]{1,0:T(8,128)(2,1)S(1)}, u32[]{:S(2)}, u32[]{:S(2)}) collective-permute-start(bf16[32,720]{1,0:T(8,128)(2,1)S(1)} %get-tuple-element.33), channel_id=1, source_target_pairs={{0,12},{1,13},{2,14},{3,15},{4,8},{5,9},{6,10},{7,11},{8,4},{9,5},... | collective-permute-start | bytes 138248 | tf_op jit(solution)/shard_map/ppermute | solution.py:438

commit v4 on v3

--- a/solution.py
+++ b/solution.py
@@ -9,6 +9,7 @@
 from jax.experimental.pallas import tpu as pltpu
 from jax.sharding import PartitionSpec as P
 
+
 HEADS = 64
 KV_HEADS = 8
 HD = 64
@@ -22,7 +23,8 @@
     share_ref, len_hbm, start_hbm, q_hbm, kn_hbm, vn_hbm, k_hbm, v_hbm, wo_hbm,
     *rest, grouped, chunks, parts,
 ):
-    outs, rest = rest[:parts], rest[parts:]
+    early = parts // 2
+    outs, (stacked_ref, later_ref), rest = rest[:early], rest[early : early + 2], rest[early + 2 :]
     len_ref, start_ref, q_ref, kn_ref, vn_ref, kbuf, vbuf, wobuf = rest[:8]
     queries, heads, scores, products, small, ksem, vsem, wsem = rest[8:]
     tokens, window, lanes = k_hbm.shape
@@ -49,13 +51,12 @@
         return pl.ds(pl.multiple_of((share_ref[0] ^ k) * rows, 16), rows)
 
     def wcopy(k):
-        return pltpu.make_async_copy(wo_hbm.at[wrows(k)], wobuf.at[wrows(k)], wsem.at[k])
+        target = wobuf.at[k - early] if k >= early else later_ref.at[k]
+        return pltpu.make_async_copy(wo_hbm.at[wrows(k)], target, wsem.at[k])
 
     for n in range(chunks):
         kcopy(n).start()
         vcopy(n).start()
-    for k in reversed(range(parts)):
-        wcopy(k).start()
     for copy in firsts:
         copy.wait()
     lane = lax.broadcasted_iota(jnp.int32, (tokens, lanes), 1)
@@ -79,6 +80,9 @@
     block = step * n_heads
     for n in range(chunks):
         kcopy(n).wait()
+        if n == 0:
+            for k in reversed(range(parts)):
+                wcopy(k).start()
         for t in range(n * step, (n + 1) * step):
             query = queries[pl.ds(t, n_heads, stride=tokens), :]
             dots = lax.dot_general(
@@ -116,10 +120,22 @@
             column = x if column is None else jnp.where(lane // HD == p, x, column)
         columns.append(column.astype(jnp.bfloat16))
     stacked = jnp.concatenate(columns, axis=1)
-    for k in reversed(range(parts)):
+    stacked_ref[...] = stacked
+    for k in reversed(range(early, parts)):
         wcopy(k).wait()
         piece = lax.dot_general(
-            stacked, wobuf[wrows(k), :], (((1,), (1,)), ((), ())),
+            stacked, wobuf[k - early], (((1,), (1,)), ((), ())),
+            preferred_element_type=jnp.float32,
+        )
+        outs[k - early][...] = piece.astype(outs[k - early].dtype)
+    for k in reversed(range(early)):
+        wcopy(k).wait()
+
+
+def project_kernel(stacked_ref, later_ref, *outs):
+    for k in reversed(range(len(outs))):
+        piece = lax.dot_general(
+            stacked_ref[...], later_ref[k], (((1,), (1,)), ((), ())),
             preferred_element_type=jnp.float32,
         )
         outs[k][...] = piece.astype(outs[k].dtype)
@@ -141,14 +157,19 @@
             cache_len, cycle_start, q_new, k_new, v_new, k_cache, v_cache, out_proj
         )
     ]
-    kinds = [jnp.float32] + [jnp.bfloat16] * (parts - 1)
-    return pl.pallas_call(
+    early = parts // 2
+    piece = jax.ShapeDtypeStruct((tokens, quarter), jnp.bfloat16)
+    made = pl.pallas_call(
         functools.partial(
             attend_kernel, grouped=HEADS // KV_HEADS, chunks=chunks, parts=parts
         ),
         in_specs=[smem] + [hbm] * 8,
-        out_specs=[vmem] * parts,
-        out_shape=[jax.ShapeDtypeStruct((tokens, quarter), kind) for kind in kinds],
+        out_specs=[vmem] * (early + 2),
+        out_shape=[piece] * early
+        + [
+            jax.ShapeDtypeStruct(q_new.shape, jnp.bfloat16),
+            jax.ShapeDtypeStruct((parts - early, quarter, q_new.shape[1]), out_proj.dtype),
+        ],
         scratch_shapes=[
             pltpu.SMEM(cache_len.shape, jnp.int32),
             pltpu.SMEM(cycle_start.shape, jnp.int32),
@@ -157,7 +178,7 @@
             pltpu.VMEM(v_new.shape, v_new.dtype),
             pltpu.VMEM(k_cache.shape, k_cache.dtype),
             pltpu.VMEM(v_cache.shape, v_cache.dtype),
-            pltpu.VMEM(out_proj.shape, out_proj.dtype),
+            pltpu.VMEM((parts - early, quarter, q_new.shape[1]), out_proj.dtype),
             pltpu.VMEM((n_heads * tokens, lanes), jnp.float32),
             pltpu.VMEM((n_heads * tokens, lanes), jnp.float32),
             pltpu.VMEM((n_heads * tokens, window), jnp.float32),
@@ -170,13 +191,24 @@
         compiler_params=pltpu.CompilerParams(vmem_limit_bytes=16 << 20),
         name="attend_project",
     )(share, *inputs)
+    first, (stacked, later) = made[:early], made[early:]
+    later_call = pl.pallas_call(
+        project_kernel,
+        in_specs=[vmem, vmem],
+        out_specs=[vmem] * early,
+        out_shape=[jax.ShapeDtypeStruct((tokens, quarter), jnp.float32)] + [piece] * (early - 1),
+        compiler_params=pltpu.CompilerParams(vmem_limit_bytes=8 << 20),
+        name="project",
+    )
+    rest = later_call(stacked, later)
+    return list(rest) + list(first)
 
 
 def expert_kernel(
     place_ref, own_ref, other_ref, gate_ref, up_ref, down_ref, keep_ref, send_ref, pieces,
     *, quarter, topk,
 ):
-    n_role, items, lanes = own_ref.shape
+    n_role, _, _ = own_ref.shape
     n_tp = 2
     parts = n_role * n_tp
     share = place_ref[0]
@@ -315,45 +347,37 @@
 def select_kernel(expert_ref, *rest, n_far, n_near, cap, topk, quarter):
     blocks, rest = rest[:n_far], rest[n_far:]
     rows, picks = rest[:n_near], rest[n_near:]
-    tokens, lanes = blocks[0].shape
+    tokens, _ = blocks[0].shape
     tail_at = quarter // 128 * 128
     first = quarter - tail_at
     stacked = jnp.concatenate([ref[...] for ref in blocks], axis=0)
-    ids = stacked[:, tail_at:].astype(jnp.float32)
+    ids = stacked[:, tail_at:].astype(jnp.float32).T
     n_all = n_far * tokens
-    down = lax.broadcasted_iota(jnp.int32, (tokens, tokens), 0)
-    across = lax.broadcasted_iota(jnp.int32, (tokens, tokens), 1)
-    before = (across < down).astype(jnp.bfloat16)
-    slot = lax.broadcasted_iota(jnp.int32, (n_all, n_far * cap), 1).astype(jnp.float32)
-    base = (lax.broadcasted_iota(jnp.int32, (n_all, 1), 0) // tokens * cap).astype(jnp.float32)
+    source = lax.broadcasted_iota(jnp.int32, (n_all, n_all), 0)
+    target = lax.broadcasted_iota(jnp.int32, (n_all, n_all), 1)
+    same = source // tokens == target // tokens
+    before = jnp.where(same & (source < target), 1.0, 0.0).astype(jnp.bfloat16)
+    slot = lax.broadcasted_iota(jnp.int32, (n_far * cap, n_all), 0).astype(jnp.float32)
+    base = lax.broadcasted_iota(jnp.int32, (1, n_all), 1) // tokens * cap
     hits = []
     for j in range(n_near):
         expert = expert_ref[j].astype(jnp.float32)
-        hit = jnp.zeros((n_all, 1), jnp.float32)
+        hit = jnp.zeros((1, n_all), jnp.float32)
         for k in range(topk):
-            hit = hit + jnp.where(ids[:, first + k : first + k + 1] == expert, 1.0, 0.0)
+            hit = hit + jnp.where(ids[first + k : first + k + 1, :] == expert, 1.0, 0.0)
         hits.append(hit)
-    lane = lax.broadcasted_iota(jnp.int32, (n_all, 128), 1)
-    table = jnp.zeros((n_all, 128), jnp.float32)
+    line = lax.broadcasted_iota(jnp.int32, (8, n_all), 0)
+    table = jnp.zeros((8, n_all), jnp.float32)
     for j in range(n_near):
-        table = jnp.where(lane == j, hits[j], table)
-    table = table.astype(jnp.bfloat16)
-    ranks = jnp.concatenate(
-        [
-            jnp.dot(
-                before, table[n * tokens : (n + 1) * tokens], preferred_element_type=jnp.float32
-            )
-            for n in range(n_far)
-        ],
-        axis=0,
-    )
-    for j in range(n_near):
-        at = jnp.where(hits[j] > 0.0, ranks[:, j : j + 1] + base, -1.0)
+        table = jnp.where(line == j, hits[j], table)
+    ranks = jnp.dot(table.astype(jnp.bfloat16), before, preferred_element_type=jnp.float32)
+    for j in reversed(range(n_near)):
+        at = jnp.where(hits[j] > 0.0, ranks[j : j + 1, :] + base.astype(jnp.float32), -1.0)
         pick = jnp.where(at == slot, 1.0, 0.0).astype(jnp.bfloat16)
         picks[j][...] = pick
-        rows[j][...] = lax.dot_general(
-            pick, stacked, (((0,), (0,)), ((), ())), preferred_element_type=jnp.float32
-        ).astype(jnp.bfloat16)
+        rows[j][...] = jnp.dot(pick, stacked, preferred_element_type=jnp.float32).astype(
+            jnp.bfloat16
+        )
 
 
 def run_select(experts, blocks, n_near, cap, topk, quarter):
@@ -361,7 +385,7 @@
     n_far = len(blocks)
     vmem = pl.BlockSpec(memory_space=pltpu.VMEM)
     outs = [jax.ShapeDtypeStruct((n_far * cap, lanes), jnp.bfloat16)] * n_near
-    outs += [jax.ShapeDtypeStruct((n_far * tokens, n_far * cap), jnp.bfloat16)] * n_near
+    outs += [jax.ShapeDtypeStruct((n_far * cap, n_far * tokens), jnp.bfloat16)] * n_near
     made = pl.pallas_call(
         functools.partial(
             select_kernel, n_far=n_far, n_near=n_near, cap=cap, topk=topk, quarter=quarter
@@ -383,8 +407,9 @@
         row = 0.0
         for i in range(n_role):
             row = row + rows[j * n_role + i][...].astype(jnp.float32)
-        total = total + jnp.dot(
-            picks[j][...], row.astype(jnp.bfloat16), preferred_element_type=jnp.float32
+        total = total + lax.dot_general(
+            picks[j][...], row.astype(jnp.bfloat16), (((0,), (0,)), ((), ())),
+            preferred_element_type=jnp.float32,
         )
     tokens = total.shape[0] // n_far
     for n in range(n_far):
@@ -393,7 +418,7 @@
 
 def run_spread(rows, picks, n_role, n_far):
     n_near = len(picks)
-    tokens = picks[0].shape[0] // n_far
+    tokens = picks[0].shape[1] // n_far
     vmem = pl.BlockSpec(memory_space=pltpu.VMEM)
     quarter = rows[0].shape[1]
     kinds = [jnp.float32] + [jnp.bfloat16] * (n_far - 1)
@@ -443,7 +468,6 @@
     ):
         role, grp, tp = (lax.axis_index(n) for n in ("role", "grp", "tp"))
         tokens, quarter = residual.shape
-        width = quarter * n_role * n_tp
         topk = route_ids.shape[1]
         experts = n_grp * w_gate.shape[0]
         cap = max(3, tokens * topk // experts + 2)
@@ -454,7 +478,9 @@
         pieces = attend_project(
             place, q_new, k_new, v_new, k_cache, v_cache, cache_len, cycle_start, out_proj.T, parts
         )
-        moved = [send(pieces[k], role=k // n_tp, tp=k % n_tp) for k in range(1, parts)]
+        moved = []
+        for k in range(1, parts):
+            moved.append(send(pieces[k], role=k // n_tp, tp=k % n_tp))
         gain = lax.dynamic_slice_in_dim(norm_gain, share * quarter, quarter, 0).reshape(1, quarter)
         attended, packed = run_pack(pieces[0], moved, residual, gain, router.T, route_ids.T)
         blocks = [packed] + [send_far(packed, k) for k in range(1, n_far)]
@@ -512,8 +538,10 @@
         P("grp", None, ("role", "tp")),
         P("grp", ("role", "tp"), None),
     )
+    local = make_local(mesh)
+
     return jax.shard_map(
-        make_local(mesh),
+        local,
         mesh=mesh,
         in_specs=placed,
         out_specs=(P("grp", ("role", "tp")), P("grp", ("role", "tp"))),

time: 57.8 us -> 55.3 us (0.957)
  Pallas kernels: 11.6 us -> 9.93 us
  waiting for transfers between devices: 24 us -> 23.2 us
    pallas_call x1, Pallas kernels: 6.7 us -> 4.36 us  [attend_project(): pl.pallas_call(functools.partial(attend_kernel, grouped=HEADS // KV_HEADS...]
    pallas_call x0 -> x1, Pallas kernels: none -> 0.91 us  [attend_project(): rest = later_call(stacked, later)]
where the time goes in v4:
time: 55.3 us; the launch traced here: 55.1 us
  waiting for transfers between devices  23.2 us (42%)
  starting transfers between devices  19.3 us (35%)
  Pallas kernels  9.93 us (18%)
  other arithmetic  0.99 us (2%)
  local copies, waits for them, and re-layouts  0.85 us (2%)
  between operations  0.78 us (1%)
    ppermute x11, waiting for transfers between devices, send(): lax.ppermute(x, names, swap_table(mesh, lambda g: g ^ near, role, tp))  15.1 us
    ppermute x11, starting transfers between devices, send(): lax.ppermute(x, names, swap_table(mesh, lambda g: g ^ near, role, tp))  10.5 us
    ppermute x6, starting transfers between devices, send_far(): return lax.ppermute(x, names, swap_table(mesh, grp_of, 0, 0))  8.84 us
    ppermute x6, waiting for transfers between devices, send_far(): return lax.ppermute(x, names, swap_table(mesh, grp_of, 0, 0))  8.15 us
    pallas_call x1, Pallas kernels, attend_project(): pl.pallas_call(functools.partial(attend_kernel, grouped=HEADS // KV_HEADS...  4.36 us
    pallas_call x1, Pallas kernels, run_expert(): pl.pallas_call(functools.partial(expert_kernel, quarter=quarter, topk=top...  2.76 us
  transfers between devices with their start and end apart: 17, of which 14 were waited for; matrix products, arithmetic and copies ran while one was open for 2% of the time, Pallas kernels for 0%

profile of v4, /device:TPU:0, one launch (start us, length us, event | category | flops | bytes accessed | tf_op | source)
XLA Modules:
  0.0 55.1 jit_solution(7025955913075005608)
XLA Ops:
  0.6 4.4 %attend_project.1 = (bf16[32,720]{1,0:T(8,128)(2,1)S(1)}, bf16[32,720]{1,0:T(8,128)(2,1)S(1)}, bf16[32,1024]{1,0:T(8,128)(2,1)S(1)}, bf16[2,720,1024]{2,1,0:T(8,128)(2,1)S(1)}) custom-call(s32[1]{0:T(128)} %bitcast.share_ref, s32[32]{0:T(128)} %len_hbm.1, s32[32]{0:T(128)} %start_hbm.1, bf16[32,1024]{1,0:T(8,128)(2,1)} %q_hbm.1, bf16[32,128]{1,0:T(8,128)(2,1)} %kn_hbm.1, ...), custom_call_target="tpu_custom_call" | custom-call | tf_op jit(solution)/shard_map/attend_project/pallas_call | solution.py:162
  5.0 0.9 %project.1 = (f32[32,720]{1,0:T(8,128)S(1)}, bf16[32,720]{1,0:T(8,128)(2,1)S(1)}) custom-call(bf16[32,1024]{1,0:T(8,128)(2,1)S(1)} %get-tuple-element.20.stacked_ref, bf16[2,720,1024]{2,1,0:T(8,128)(2,1)S(1)} %get-tuple-element.21.later_ref), custom_call_target="tpu_custom_call" | custom-call | tf_op jit(solution)/shard_map/project/pallas_call | solution.py:203
  6.0 0.5 collective-permute-start
  6.5 2.5 %collective-permute-start.1 = (bf16[32,720]{1,0:T(8,128)(2,1)S(1)}, bf16[32,720]{1,0:T(8,128)(2,1)S(1)}, u32[]{:S(2)}, u32[]{:S(2)}) collective-permute-start(bf16[32,720]{1,0:T(8,128)(2,1)S(1)} %get-tuple-element.24), channel_id=1, source_target_pairs={{0,16},{1,17},{2,18},{3,19},{4,20},{5,21},{6,22},{7,23},{8,24},{9,... | collective-permute-start | bytes 138248 | tf_op jit(solution)/shard_map/ppermute | solution.py:456
  9.1 0.8 %dynamic_slice.3 = f32[720]{0:T(1024)S(1)} dynamic-slice(f32[2880]{0:T(1024)} %param.24, s32[]{:T(128)S(6)} %select_n.14), dynamic_slice_sizes={720} | dynamic-slice | bytes 5764 | tf_op jit(solution)/shard_map/dynamic_slice | solution.py:484
  9.8 1.5 %collective-permute-done.1.rest_1_ = bf16[32,720]{1,0:T(8,128)(2,1)S(1)} collective-permute-done((bf16[32,720]{1,0:T(8,128)(2,1)S(1)}, bf16[32,720]{1,0:T(8,128)(2,1)S(1)}, u32[]{:S(2)}, u32[]{:S(2)}) %collective-permute-start.1) | collective-permute-done | bytes 46112 | tf_op jit(solution)/shard_map/ppermute | solution.py:456
  11.3 1.4 %collective-permute-done.2.rest_2_ = bf16[32,720]{1,0:T(8,128)(2,1)S(1)} collective-permute-done((bf16[32,720]{1,0:T(8,128)(2,1)S(1)}, bf16[32,720]{1,0:T(8,128)(2,1)S(1)}, u32[]{:S(2)}, u32[]{:S(2)}) %collective-permute-start.2) | collective-permute-done | bytes 46112 | tf_op jit(solution)/shard_map/ppermute | solution.py:456
  12.8 0.7 %pack.1 = (bf16[32,720]{1,0:T(8,128)(2,1)}, bf16[32,768]{1,0:T(8,128)(2,1)S(1)}) custom-call(f32[32,720]{1,0:T(8,128)S(1)} %get-tuple-element.22.own_ref, bf16[32,720]{1,0:T(8,128)(2,1)S(1)} %collective-permute-done.rest_0_, bf16[32,720]{1,0:T(8,128)(2,1)S(1)} %collective-permute-done.1.rest_1_, bf16[32,720]{1,0:T(8,128)(2,1)S(1)} %collective-permute-done.2.rest_2_, ...), custom_call_target="tpu_custom_call" | custom-call | flops 8589934592 | bytes 1048576 | tf_op jit(solution)/shard_map/pack/pallas_call | solution.py:333
  13.4 1.6 %collective-permute-start.3 = (bf16[32,768]{1,0:T(8,128)(2,1)S(1)}, bf16[32,768]{1,0:T(8,128)(2,1)S(1)}, u32[]{:S(2)}, u32[]{:S(2)}) collective-permute-start(bf16[32,768]{1,0:T(8,128)(2,1)S(1)} %get-tuple-element.27.rest_0_), channel_id=1, source_target_pairs={{0,4},{1,5},{2,6},{3,7},{4,0},{5,1},{6,2},{7,3},{8,12},{9,13},{10,... | collective-permute-start | bytes 147464 | tf_op jit(solution)/shard_map/ppermute | solution.py:463
  15.0 2.6 %collective-permute-start.4 = (bf16[32,768]{1,0:T(8,128)(2,1)S(1)}, bf16[32,768]{1,0:T(8,128)(2,1)S(1)}, u32[]{:S(2)}, u32[]{:S(2)}) collective-permute-start(bf16[32,768]{1,0:T(8,128)(2,1)S(1)} %get-tuple-element.27.rest_0_), channel_id=1, source_target_pairs={{0,8},{1,9},{2,10},{3,11},{4,12},{5,13},{6,14},{7,15},{8,0},{9,1},... | collective-permute-start | bytes 147464 | tf_op jit(solution)/shard_map/ppermute | solution.py:463
  17.9 3.0 %collective-permute-done.4.rest_2_ = bf16[32,768]{1,0:T(8,128)(2,1)S(1)} collective-permute-done((bf16[32,768]{1,0:T(8,128)(2,1)S(1)}, bf16[32,768]{1,0:T(8,128)(2,1)S(1)}, u32[]{:S(2)}, u32[]{:S(2)}) %collective-permute-start.4) | collective-permute-done | bytes 49184 | tf_op jit(solution)/shard_map/ppermute | solution.py:463
  20.9 2.6 %collective-permute-done.5.rest_3_ = bf16[32,768]{1,0:T(8,128)(2,1)S(1)} collective-permute-done((bf16[32,768]{1,0:T(8,128)(2,1)S(1)}, bf16[32,768]{1,0:T(8,128)(2,1)S(1)}, u32[]{:S(2)}, u32[]{:S(2)}) %collective-permute-start.5) | collective-permute-done | bytes 49184 | tf_op jit(solution)/shard_map/ppermute | solution.py:463
  23.5 1.0 %select.7 = (bf16[72,768]{1,0:T(8,128)(2,1)S(1)}, bf16[72,768]{1,0:T(8,128)(2,1)S(1)}, bf16[72,128]{1,0:T(8,128)(2,1)S(1)}, bf16[72,128]{1,0:T(8,128)(2,1)S(1)}) custom-call(s32[2]{0:T(128)S(1)} %pad_add_fusion.1.expert_ref, bf16[32,768]{1,0:T(8,128)(2,1)S(1)} %get-tuple-element.27.rest_0_, bf16[32,768]{1,0:T(8,128)(2,1)S(1)} %collective-permute-done.3.rest_1_, ...), custom_call_target="tpu_custom_call" | custom-call | tf_op jit(solution)/shard_map/select/pallas_call | solution.py:389
  24.4 1.6 %collective-permute-start.6 = (bf16[72,768]{1,0:T(8,128)(2,1)S(1)}, bf16[72,768]{1,0:T(8,128)(2,1)S(1)}, u32[]{:S(2)}, u32[]{:S(2)}) collective-permute-start(bf16[72,768]{1,0:T(8,128)(2,1)S(1)} %get-tuple-element.29), channel_id=1, source_target_pairs={{0,2},{1,3},{2,0},{3,1},{4,6},{5,7},{6,4},{7,5},{8,10},{9,11},{10,... | collective-permute-start | bytes 331784 | tf_op jit(solution)/shard_map/ppermute | solution.py:456
  26.0 0.9 %collective-permute-start.8 = (bf16[72,768]{1,0:T(8,128)(2,1)S(1)}, bf16[72,768]{1,0:T(8,128)(2,1)S(1)}, u32[]{:S(2)}, u32[]{:S(2)}) collective-permute-start(bf16[72,768]{1,0:T(8,128)(2,1)S(1)} %get-tuple-element.29), channel_id=1, source_target_pairs={{0,18},{1,19},{2,16},{3,17},{4,22},{5,23},{6,20},{7,21},{8,26},{9,... | collective-permute-start | bytes 331784 | tf_op jit(solution)/shard_map/ppermute | solution.py:456
  26.9 1.1 %collective-permute-start.7 = (bf16[72,768]{1,0:T(8,128)(2,1)S(1)}, bf16[72,768]{1,0:T(8,128)(2,1)S(1)}, u32[]{:S(2)}, u32[]{:S(2)}) collective-permute-start(bf16[72,768]{1,0:T(8,128)(2,1)S(1)} %get-tuple-element.28), channel_id=1, source_target_pairs={{0,16},{1,17},{2,18},{3,19},{4,20},{5,21},{6,22},{7,23},{8,24},{9,... | collective-permute-start | bytes 331784 | tf_op jit(solution)/shard_map/ppermute | solution.py:456
  28.0 2.1 %collective-permute-done.6 = bf16[72,768]{1,0:T(8,128)(2,1)S(1)} collective-permute-done((bf16[72,768]{1,0:T(8,128)(2,1)S(1)}, bf16[72,768]{1,0:T(8,128)(2,1)S(1)}, u32[]{:S(2)}, u32[]{:S(2)}) %collective-permute-start.6) | collective-permute-done | bytes 110624 | tf_op jit(solution)/shard_map/ppermute | solution.py:456
  30.1 1.6 %collective-permute-done.8 = bf16[72,768]{1,0:T(8,128)(2,1)S(1)} collective-permute-done((bf16[72,768]{1,0:T(8,128)(2,1)S(1)}, bf16[72,768]{1,0:T(8,128)(2,1)S(1)}, u32[]{:S(2)}, u32[]{:S(2)}) %collective-permute-start.8) | collective-permute-done | bytes 110624 | tf_op jit(solution)/shard_map/ppermute | solution.py:456
  32.1 1.7 %collective-permute-done.9.other_ref = bf16[2,144,768]{2,1,0:T(8,128)(2,1)S(1)} collective-permute-done((bf16[2,144,768]{2,1,0:T(8,128)(2,1)S(1)}, bf16[2,144,768]{2,1,0:T(8,128)(2,1)S(1)}, u32[]{:S(2)}, u32[]{:S(2)}) %collective-permute-start.9) | collective-permute-done | bytes 442400 | tf_op jit(solution)/shard_map/ppermute | solution.py:456
  33.8 2.8 %expert.1 = (bf16[2,144,720]{2,1,0:T(8,128)(2,1)S(1)}, bf16[2,144,720]{2,1,0:T(8,128)(2,1)S(1)}) custom-call(s32[2]{0:T(128)S(1)} %pad_add_fusion.place_ref, bf16[2,144,768]{2,1,0:T(8,128)(2,1)S(1)} %pad_maximum_fusion.own_ref, bf16[2,144,768]{2,1,0:T(8,128)(2,1)S(1)} %collective-permute-done.9.other_ref, bf16[1,360,2880]{2,1,0:T(8,128)(2,1)S(1)} %bitcast.22, ...), custom_call_target="tpu_custom_call" | custom-call | tf_op jit(solution)/shard_map/expert/pallas_call | solution.py:265
  36.8 1.7 %collective-permute-done.10 = bf16[2,144,720]{2,1,0:T(8,128)(2,1)S(1)} collective-permute-done((bf16[2,144,720]{2,1,0:T(8,128)(2,1)S(1)}, bf16[2,144,720]{2,1,0:T(8,128)(2,1)S(1)}, u32[]{:S(2)}, u32[]{:S(2)}) %collective-permute-start.10) | collective-permute-done | bytes 414752 | tf_op jit(solution)/shard_map/ppermute | solution.py:456
  38.6 1.0 %collective-permute-start.11 = (bf16[72,720]{1,0:T(8,128)(2,1)S(1)}, bf16[72,720]{1,0:T(8,128)(2,1)S(1)}, u32[]{:S(2)}, u32[]{:S(2)}) collective-permute-start(bf16[72,720]{1,0:T(8,128)(2,1)S(1)} %get-tuple-element.40), channel_id=1, source_target_pairs={{0,16},{1,17},{2,18},{3,19},{4,20},{5,21},{6,22},{7,23},{8,24},{9,... | collective-permute-start | bytes 311048 | tf_op jit(solution)/shard_map/ppermute | solution.py:456
  39.6 1.5 %collective-permute-start.12 = (bf16[72,720]{1,0:T(8,128)(2,1)S(1)}, bf16[72,720]{1,0:T(8,128)(2,1)S(1)}, u32[]{:S(2)}, u32[]{:S(2)}) collective-permute-start(bf16[72,720]{1,0:T(8,128)(2,1)S(1)} %get-tuple-element.39), channel_id=1, source_target_pairs={{0,2},{1,3},{2,0},{3,1},{4,6},{5,7},{6,4},{7,5},{8,10},{9,11},{10,... | collective-permute-start | bytes 311048 | tf_op jit(solution)/shard_map/ppermute | solution.py:456
  41.1 1.0 %collective-permute-start.13 = (bf16[72,720]{1,0:T(8,128)(2,1)S(1)}, bf16[72,720]{1,0:T(8,128)(2,1)S(1)}, u32[]{:S(2)}, u32[]{:S(2)}) collective-permute-start(bf16[72,720]{1,0:T(8,128)(2,1)S(1)} %get-tuple-element.38), channel_id=1, source_target_pairs={{0,18},{1,19},{2,16},{3,17},{4,22},{5,23},{6,20},{7,21},{8,26},{9,... | collective-permute-start | bytes 311048 | tf_op jit(solution)/shard_map/ppermute | solution.py:456
  42.2 2.1 %collective-permute-done.11.refs_1_ = bf16[72,720]{1,0:T(8,128)(2,1)S(1)} collective-permute-done((bf16[72,720]{1,0:T(8,128)(2,1)S(1)}, bf16[72,720]{1,0:T(8,128)(2,1)S(1)}, u32[]{:S(2)}, u32[]{:S(2)}) %collective-permute-start.11) | collective-permute-done | bytes 103712 | tf_op jit(solution)/shard_map/ppermute | solution.py:456
  44.3 1.5 %collective-permute-done.12.refs_2_ = bf16[72,720]{1,0:T(8,128)(2,1)S(1)} collective-permute-done((bf16[72,720]{1,0:T(8,128)(2,1)S(1)}, bf16[72,720]{1,0:T(8,128)(2,1)S(1)}, u32[]{:S(2)}, u32[]{:S(2)}) %collective-permute-start.12) | collective-permute-done | bytes 103712 | tf_op jit(solution)/shard_map/ppermute | solution.py:456
  45.9 1.2 %collective-permute-done.13.refs_3_ = bf16[72,720]{1,0:T(8,128)(2,1)S(1)} collective-permute-done((bf16[72,720]{1,0:T(8,128)(2,1)S(1)}, bf16[72,720]{1,0:T(8,128)(2,1)S(1)}, u32[]{:S(2)}, u32[]{:S(2)}) %collective-permute-start.13) | collective-permute-done | bytes 103712 | tf_op jit(solution)/shard_map/ppermute | solution.py:456
  47.4 1.1 %collective-permute-start.16 = (bf16[32,720]{1,0:T(8,128)(2,1)S(1)}, bf16[32,720]{1,0:T(8,128)(2,1)S(1)}, u32[]{:S(2)}, u32[]{:S(2)}) collective-permute-start(bf16[32,720]{1,0:T(8,128)(2,1)S(1)} %get-tuple-element.37), channel_id=1, source_target_pairs={{0,12},{1,13},{2,14},{3,15},{4,8},{5,9},{6,10},{7,11},{8,4},{9,5},... | collective-permute-start | bytes 138248 | tf_op jit(solution)/shard_map/ppermute | solution.py:463
  48.5 3.3 %collective-permute-start.14 = (bf16[32,720]{1,0:T(8,128)(2,1)S(1)}, bf16[32,720]{1,0:T(8,128)(2,1)S(1)}, u32[]{:S(2)}, u32[]{:S(2)}) collective-permute-start(bf16[32,720]{1,0:T(8,128)(2,1)S(1)} %get-tuple-element.35), channel_id=1, source_target_pairs={{0,4},{1,5},{2,6},{3,7},{4,0},{5,1},{6,2},{7,3},{8,12},{9,13},{10,... | collective-permute-start | bytes 138248 | tf_op jit(solution)/shard_map/ppermute | solution.py:463
  51.9 1.5 %collective-permute-done.16 = bf16[32,720]{1,0:T(8,128)(2,1)S(1)} collective-permute-done((bf16[32,720]{1,0:T(8,128)(2,1)S(1)}, bf16[32,720]{1,0:T(8,128)(2,1)S(1)}, u32[]{:S(2)}, u32[]{:S(2)}) %collective-permute-start.16) | collective-permute-done | bytes 46112 | tf_op jit(solution)/shard_map/ppermute | solution.py:463
  53.4 1.0 %collective-permute-done.15 = bf16[32,720]{1,0:T(8,128)(2,1)S(1)} collective-permute-done((bf16[32,720]{1,0:T(8,128)(2,1)S(1)}, bf16[32,720]{1,0:T(8,128)(2,1)S(1)}, u32[]{:S(2)}, u32[]{:S(2)}) %collective-permute-start.15) | collective-permute-done | bytes 46112 | tf_op jit(solution)/shard_map/ppermute | solution.py:463
  54.4 0.6 %add_convert_fusion.1 = bf16[32,720]{1,0:T(8,128)(2,1)} fusion(bf16[32,720]{1,0:T(8,128)(2,1)S(1)} %collective-permute-done.16, bf16[32,720]{1,0:T(8,128)(2,1)S(1)} %collective-permute-done.15, f32[32,720]{1,0:T(8,128)S(1)} %get-tuple-element.34, bf16[32,720]{1,0:T(8,128)(2,1)S(1)} %collective-permute-done.14), kind=kLoop, calls=%fused_computation.8 | loop fusion | flops 161280 | bytes 276480 | tf_op jit(solution)/shard_map/convert_element_type | solution.py:518
  (30 shorter events, 1.5 us)
Async XLA Ops:
  5.0 7.7 %copy-start.3 = (bf16[32,720]{1,0:T(8,128)(2,1)S(1)}, bf16[32,720]{1,0:T(8,128)(2,1)}, u32[]{:S(2)}) copy-start(bf16[32,720]{1,0:T(8,128)(2,1)} %rest_3_.1) | copy-start | bytes 138244
  5.0 7.7 %copy-start.4 = (bf16[720,8]{0,1:T(8,128)(2,1)S(1)}, bf16[720,8]{0,1:T(8,128)(2,1)}, u32[]{:S(2)}) copy-start(bf16[720,8]{0,1:T(8,128)(2,1)} %param.25) | copy-start | bytes 34564
  5.0 7.7 %copy-start.5 = (s32[32,4]{0,1:T(4,128)S(1)}, s32[32,4]{0,1:T(4,128)}, u32[]{:S(2)}) copy-start(s32[32,4]{0,1:T(4,128)} %param.26) | copy-start | bytes 1540
  6.0 3.9 %collective-permute-start = (bf16[32,720]{1,0:T(8,128)(2,1)S(1)}, bf16[32,720]{1,0:T(8,128)(2,1)S(1)}, u32[]{:S(2)}, u32[]{:S(2)}) collective-permute-start(bf16[32,720]{1,0:T(8,128)(2,1)S(1)} %get-tuple-element.23), channel_id=1, source_target_pairs={{0,1},{1,0},{2,3},{3,2},{4,5},{5,4},{6,7},{7,6},{8,9},{9,8},{10,11... | collective-permute-start | bytes 138248 | tf_op jit(solution)/shard_map/ppermute | solution.py:456
  6.5 4.9 %collective-permute-start.1 = (bf16[32,720]{1,0:T(8,128)(2,1)S(1)}, bf16[32,720]{1,0:T(8,128)(2,1)S(1)}, u32[]{:S(2)}, u32[]{:S(2)}) collective-permute-start(bf16[32,720]{1,0:T(8,128)(2,1)S(1)} %get-tuple-element.24), channel_id=1, source_target_pairs={{0,16},{1,17},{2,18},{3,19},{4,20},{5,21},{6,22},{7,23},{8,24},{9,... | collective-permute-start | bytes 138248 | tf_op jit(solution)/shard_map/ppermute | solution.py:456
  9.0 3.7 %collective-permute-start.2 = (bf16[32,720]{1,0:T(8,128)(2,1)S(1)}, bf16[32,720]{1,0:T(8,128)(2,1)S(1)}, u32[]{:S(2)}, u32[]{:S(2)}) collective-permute-start(bf16[32,720]{1,0:T(8,128)(2,1)S(1)} %get-tuple-element.25), channel_id=1, source_target_pairs={{0,17},{1,16},{2,19},{3,18},{4,21},{5,20},{6,23},{7,22},{8,25},{9,... | collective-permute-start | bytes 138248 | tf_op jit(solution)/shard_map/ppermute | solution.py:456
  12.7 21.1 %copy-start = (bf16[1,2880,360]{1,2,0:T(8,128)(2,1)S(1)}, bf16[1,2880,360]{1,2,0:T(8,128)(2,1)}, u32[]{:S(2)}) copy-start(bf16[1,2880,360]{1,2,0:T(8,128)(2,1)} %param.27) | copy-start | bytes 6220804
  12.7 21.1 %copy-start.1 = (bf16[1,2880,360]{1,2,0:T(8,128)(2,1)S(1)}, bf16[1,2880,360]{1,2,0:T(8,128)(2,1)}, u32[]{:S(2)}) copy-start(bf16[1,2880,360]{1,2,0:T(8,128)(2,1)} %param.28) | copy-start | bytes 6220804
  12.7 21.1 %copy-start.2 = (bf16[1,360,2880]{2,1,0:T(8,128)(2,1)S(1)}, bf16[1,360,2880]{2,1,0:T(8,128)(2,1)}, u32[]{:S(2)}) copy-start(bf16[1,360,2880]{2,1,0:T(8,128)(2,1)} %down_ref.1) | copy-start | bytes 6220804
  13.4 4.5 %collective-permute-start.3 = (bf16[32,768]{1,0:T(8,128)(2,1)S(1)}, bf16[32,768]{1,0:T(8,128)(2,1)S(1)}, u32[]{:S(2)}, u32[]{:S(2)}) collective-permute-start(bf16[32,768]{1,0:T(8,128)(2,1)S(1)} %get-tuple-element.27.rest_0_), channel_id=1, source_target_pairs={{0,4},{1,5},{2,6},{3,7},{4,0},{5,1},{6,2},{7,3},{8,12},{9,13},{10,... | collective-permute-start | bytes 147464 | tf_op jit(solution)/shard_map/ppermute | solution.py:463
  15.0 5.9 %collective-permute-start.4 = (bf16[32,768]{1,0:T(8,128)(2,1)S(1)}, bf16[32,768]{1,0:T(8,128)(2,1)S(1)}, u32[]{:S(2)}, u32[]{:S(2)}) collective-permute-start(bf16[32,768]{1,0:T(8,128)(2,1)S(1)} %get-tuple-element.27.rest_0_), channel_id=1, source_target_pairs={{0,8},{1,9},{2,10},{3,11},{4,12},{5,13},{6,14},{7,15},{8,0},{9,1},... | collective-permute-start | bytes 147464 | tf_op jit(solution)/shard_map/ppermute | solution.py:463
  17.6 5.9 %collective-permute-start.5 = (bf16[32,768]{1,0:T(8,128)(2,1)S(1)}, bf16[32,768]{1,0:T(8,128)(2,1)S(1)}, u32[]{:S(2)}, u32[]{:S(2)}) collective-permute-start(bf16[32,768]{1,0:T(8,128)(2,1)S(1)} %get-tuple-element.27.rest_0_), channel_id=1, source_target_pairs={{0,12},{1,13},{2,14},{3,15},{4,8},{5,9},{6,10},{7,11},{8,4},{9,5},... | collective-permute-start | bytes 147464 | tf_op jit(solution)/shard_map/ppermute | solution.py:463
  24.4 5.6 %collective-permute-start.6 = (bf16[72,768]{1,0:T(8,128)(2,1)S(1)}, bf16[72,768]{1,0:T(8,128)(2,1)S(1)}, u32[]{:S(2)}, u32[]{:S(2)}) collective-permute-start(bf16[72,768]{1,0:T(8,128)(2,1)S(1)} %get-tuple-element.29), channel_id=1, source_target_pairs={{0,2},{1,3},{2,0},{3,1},{4,6},{5,7},{6,4},{7,5},{8,10},{9,11},{10,... | collective-permute-start | bytes 331784 | tf_op jit(solution)/shard_map/ppermute | solution.py:456
  26.0 5.6 %collective-permute-start.8 = (bf16[72,768]{1,0:T(8,128)(2,1)S(1)}, bf16[72,768]{1,0:T(8,128)(2,1)S(1)}, u32[]{:S(2)}, u32[]{:S(2)}) collective-permute-start(bf16[72,768]{1,0:T(8,128)(2,1)S(1)} %get-tuple-element.29), channel_id=1, source_target_pairs={{0,18},{1,19},{2,16},{3,17},{4,22},{5,23},{6,20},{7,21},{8,26},{9,... | collective-permute-start | bytes 331784 | tf_op jit(solution)/shard_map/ppermute | solution.py:456
  26.9 5.0 %collective-permute-start.7 = (bf16[72,768]{1,0:T(8,128)(2,1)S(1)}, bf16[72,768]{1,0:T(8,128)(2,1)S(1)}, u32[]{:S(2)}, u32[]{:S(2)}) collective-permute-start(bf16[72,768]{1,0:T(8,128)(2,1)S(1)} %get-tuple-element.28), channel_id=1, source_target_pairs={{0,16},{1,17},{2,18},{3,19},{4,20},{5,21},{6,22},{7,23},{8,24},{9,... | collective-permute-start | bytes 331784 | tf_op jit(solution)/shard_map/ppermute | solution.py:456
  32.0 1.9 %collective-permute-start.9 = (bf16[2,144,768]{2,1,0:T(8,128)(2,1)S(1)}, bf16[2,144,768]{2,1,0:T(8,128)(2,1)S(1)}, u32[]{:S(2)}, u32[]{:S(2)}) collective-permute-start(bf16[2,144,768]{2,1,0:T(8,128)(2,1)S(1)} %pad_maximum_fusion.own_ref), channel_id=1, source_target_pairs={{0,1},{1,0},{2,3},{3,2},{4,5},{5,4},{6,7},{7,6},{8,9},{9,8},{10,11... | collective-permute-start | bytes 1327112 | tf_op jit(solution)/shard_map/ppermute | solution.py:456
  36.6 1.9 %collective-permute-start.10 = (bf16[2,144,720]{2,1,0:T(8,128)(2,1)S(1)}, bf16[2,144,720]{2,1,0:T(8,128)(2,1)S(1)}, u32[]{:S(2)}, u32[]{:S(2)}) collective-permute-start(bf16[2,144,720]{2,1,0:T(8,128)(2,1)S(1)} %get-tuple-element.31), channel_id=1, source_target_pairs={{0,1},{1,0},{2,3},{3,2},{4,5},{5,4},{6,7},{7,6},{8,9},{9,8},{10,11... | collective-permute-start | bytes 1244168 | tf_op jit(solution)/shard_map/ppermute | solution.py:456
  38.6 5.7 %collective-permute-start.11 = (bf16[72,720]{1,0:T(8,128)(2,1)S(1)}, bf16[72,720]{1,0:T(8,128)(2,1)S(1)}, u32[]{:S(2)}, u32[]{:S(2)}) collective-permute-start(bf16[72,720]{1,0:T(8,128)(2,1)S(1)} %get-tuple-element.40), channel_id=1, source_target_pairs={{0,16},{1,17},{2,18},{3,19},{4,20},{5,21},{6,22},{7,23},{8,24},{9,... | collective-permute-start | bytes 311048 | tf_op jit(solution)/shard_map/ppermute | solution.py:456
  39.6 6.3 %collective-permute-start.12 = (bf16[72,720]{1,0:T(8,128)(2,1)S(1)}, bf16[72,720]{1,0:T(8,128)(2,1)S(1)}, u32[]{:S(2)}, u32[]{:S(2)}) collective-permute-start(bf16[72,720]{1,0:T(8,128)(2,1)S(1)} %get-tuple-element.39), channel_id=1, source_target_pairs={{0,2},{1,3},{2,0},{3,1},{4,6},{5,7},{6,4},{7,5},{8,10},{9,11},{10,... | collective-permute-start | bytes 311048 | tf_op jit(solution)/shard_map/ppermute | solution.py:456
  41.1 6.0 %collective-permute-start.13 = (bf16[72,720]{1,0:T(8,128)(2,1)S(1)}, bf16[72,720]{1,0:T(8,128)(2,1)S(1)}, u32[]{:S(2)}, u32[]{:S(2)}) collective-permute-start(bf16[72,720]{1,0:T(8,128)(2,1)S(1)} %get-tuple-element.38), channel_id=1, source_target_pairs={{0,18},{1,19},{2,16},{3,17},{4,22},{5,23},{6,20},{7,21},{8,26},{9,... | collective-permute-start | bytes 311048 | tf_op jit(solution)/shard_map/ppermute | solution.py:456
  47.4 6.0 %collective-permute-start.16 = (bf16[32,720]{1,0:T(8,128)(2,1)S(1)}, bf16[32,720]{1,0:T(8,128)(2,1)S(1)}, u32[]{:S(2)}, u32[]{:S(2)}) collective-permute-start(bf16[32,720]{1,0:T(8,128)(2,1)S(1)} %get-tuple-element.37), channel_id=1, source_target_pairs={{0,12},{1,13},{2,14},{3,15},{4,8},{5,9},{6,10},{7,11},{8,4},{9,5},... | collective-permute-start | bytes 138248 | tf_op jit(solution)/shard_map/ppermute | solution.py:463
  48.5 5.9 %collective-permute-start.15 = (bf16[32,720]{1,0:T(8,128)(2,1)S(1)}, bf16[32,720]{1,0:T(8,128)(2,1)S(1)}, u32[]{:S(2)}, u32[]{:S(2)}) collective-permute-start(bf16[32,720]{1,0:T(8,128)(2,1)S(1)} %get-tuple-element.36), channel_id=1, source_target_pairs={{0,8},{1,9},{2,10},{3,11},{4,12},{5,13},{6,14},{7,15},{8,0},{9,1},... | collective-permute-start | bytes 138248 | tf_op jit(solution)/shard_map/ppermute | solution.py:463
  48.5 5.9 %collective-permute-start.14 = (bf16[32,720]{1,0:T(8,128)(2,1)S(1)}, bf16[32,720]{1,0:T(8,128)(2,1)S(1)}, u32[]{:S(2)}, u32[]{:S(2)}) collective-permute-start(bf16[32,720]{1,0:T(8,128)(2,1)S(1)} %get-tuple-element.35), channel_id=1, source_target_pairs={{0,4},{1,5},{2,6},{3,7},{4,0},{5,1},{6,2},{7,3},{8,12},{9,13},{10,... | collective-permute-start | bytes 138248 | tf_op jit(solution)/shard_map/ppermute | solution.py:463

commit v5 on v4

--- a/solution.py
+++ b/solution.py
@@ -204,73 +204,156 @@
     return list(rest) + list(first)
 
 
-def expert_kernel(
-    place_ref, own_ref, other_ref, gate_ref, up_ref, down_ref, keep_ref, send_ref, pieces,
-    *, quarter, topk,
+def for_each_share(place_ref, parts, body):
+    for share in range(parts):
+        pl.when(place_ref[0] == share)(functools.partial(body, share))
+
+
+def window_of(place, quarter):
+    first, last = place * quarter, (place + 1) * quarter
+    start = first // 128 * 128
+    return slice(start, last), first - start
+
+
+def partial_products(refs, places, gate_ref, up_ref, quarter):
+    turned = (((1,), (1,)), ((), ()))
+    gate_lin = up_lin = 0.0
+    for x, p in zip(refs, places):
+        at, shift = window_of(p, quarter)
+        x = x[:, :quarter]
+        if shift:
+            x = jnp.concatenate([jnp.zeros((x.shape[0], shift), x.dtype), x], axis=1)
+        gate_lin = gate_lin + lax.dot_general(
+            x, gate_ref[0, :, at], turned, preferred_element_type=jnp.float32
+        )
+        up_lin = up_lin + lax.dot_general(
+            x, up_ref[0, :, at], turned, preferred_element_type=jnp.float32
+        )
+    return gate_lin, up_lin
+
+
+def down_products(activated, weight, place, down_ref, quarter):
+    at, shift = window_of(place, quarter)
+    result = jnp.dot(activated, down_ref[0, :, at], preferred_element_type=jnp.float32) * weight
+    return result[:, shift:].astype(jnp.bfloat16)
+
+
+def first_kernel(place_ref, own_ref, gate_ref, up_ref, gate_out, up_out, *, quarter, n_tp):
+    n_role = own_ref.shape[0]
+
+    def body(share):
+        places = [share ^ (i * n_tp) for i in range(n_role)]
+        gate_out[...], up_out[...] = partial_products(
+            [own_ref[i] for i in range(n_role)], places, gate_ref, up_ref, quarter
+        )
+
+    for_each_share(place_ref, n_role * n_tp, body)
+
+
+def second_kernel(
+    place_ref, own_ref, other_ref, gate_in, up_in, gate_ref, up_ref, down_ref, send_ref,
+    activated_ref, weight_ref, *, quarter, topk, n_tp,
+):
+    def body(share):
+        second_body(
+            share, place_ref, own_ref, other_ref, gate_in, up_in, gate_ref, up_ref, down_ref,
+            send_ref, activated_ref, weight_ref, quarter, topk, n_tp,
+        )
+
+    for_each_share(place_ref, own_ref.shape[0] * n_tp, body)
+
+
+def second_body(
+    share, place_ref, own_ref, other_ref, gate_in, up_in, gate_ref, up_ref, down_ref,
+    send_ref, activated_ref, weight_ref, quarter, topk, n_tp,
 ):
     n_role, _, _ = own_ref.shape
-    n_tp = 2
-    parts = n_role * n_tp
-    share = place_ref[0]
     tail_at = quarter // 128 * 128
     first = quarter - tail_at
+    places = [share ^ (i * n_tp + 1) for i in range(n_role)]
+    gate_lin, up_lin = partial_products(
+        [other_ref[i] for i in range(n_role)], places, gate_ref, up_ref, quarter
+    )
     tail = 0.0
-    columns = []
-    for p in range(parts):
-        slot = share ^ p
-        i, l = slot // n_tp, slot % n_tp
-        x = jnp.where(l == 0, own_ref[i], other_ref[i])
-        tail = tail + x[:, tail_at:].astype(jnp.float32)
-        columns.append(x[:, :quarter])
-    inputs = jnp.concatenate(columns, axis=1)
-    turned = (((1,), (1,)), ((), ()))
-    gate_lin = lax.dot_general(inputs, gate_ref[0], turned, preferred_element_type=jnp.float32)
-    up_lin = lax.dot_general(inputs, up_ref[0], turned, preferred_element_type=jnp.float32)
-    ids = own_ref[0, :, tail_at:].astype(jnp.float32)
+    for ref in (own_ref, other_ref):
+        for i in range(n_role):
+            tail = tail + ref[i, :, tail_at:].astype(jnp.float32)
+    ids = pltpu.roll(own_ref[0, :, tail_at:].astype(jnp.float32), topk + 1, 1)
     n_stat = 1 + topk
-
-    def total(c):
-        at = first + topk + c
-        return sum(tail[:, at + p * n_stat : at + p * n_stat + 1] for p in range(3))
-
-    scale = lax.rsqrt(total(0) / (parts * quarter) + epsilon)
-    picked = [total(1 + k) * scale for k in range(topk)]
-    top = functools.reduce(jnp.maximum, picked)
-    lifted = [jnp.exp(x - top) for x in picked]
+    span = tail.shape[1]
+    tail = tail + pltpu.roll(tail, span - n_stat, 1) + pltpu.roll(tail, span - 2 * n_stat, 1)
+    at = first + topk
+    scale = lax.rsqrt(tail[:, at : at + 1] / down_ref.shape[2] + epsilon)
+    lane = lax.broadcasted_iota(jnp.int32, tail.shape, 1)
+    chosen = (lane > at) & (lane <= at + topk)
+    picked = jnp.where(chosen, tail * scale, -1e30)
+    lifted = jnp.exp(picked - jnp.max(picked, axis=1, keepdims=True))
     expert = place_ref[1].astype(jnp.float32)
-    mine = sum(
-        jnp.where(ids[:, first + k : first + k + 1] == expert, lifted[k], 0.0)
-        for k in range(topk)
-    )
-    weight = mine / sum(lifted)
-    gate_lin = gate_lin * scale
-    up_lin = up_lin * scale
+    mine = jnp.where(chosen & (ids == expert), lifted, 0.0)
+    weight = jnp.sum(mine, axis=1, keepdims=True) / jnp.sum(lifted, axis=1, keepdims=True)
+    gate_lin = (gate_lin + gate_in[...]) * scale
+    up_lin = (up_lin + up_in[...]) * scale
     activated = gate_lin * jax.nn.sigmoid(1.702 * gate_lin) * (up_lin + 1.0)
-    result = jnp.dot(
-        activated.astype(jnp.bfloat16), down_ref[0], preferred_element_type=jnp.float32
-    )
-    result = result * weight
-    for p in range(parts):
-        pieces[p ^ share] = result[:, p * quarter : (p + 1) * quarter].astype(jnp.bfloat16)
+    activated = activated.astype(jnp.bfloat16)
+    activated_ref[...] = activated
+    weight_ref[...] = jnp.broadcast_to(weight, weight_ref.shape)
     for i in range(n_role):
-        keep_ref[i] = pieces[i * n_tp]
-        send_ref[i] = pieces[i * n_tp + 1]
-
-
-def run_expert(place, own, other, w_gate, w_up, w_down, quarter, topk):
+        send_ref[i] = down_products(activated, weight, places[i], down_ref, quarter)
+
+
+def third_kernel(place_ref, activated_ref, weight_ref, down_ref, keep_ref, *, quarter, n_tp):
+    n_role = keep_ref.shape[0]
+
+    def body(share):
+        weight = weight_ref[:, :1]
+        for i in range(n_role):
+            place = share ^ (i * n_tp)
+            keep_ref[i] = down_products(activated_ref[...], weight, place, down_ref, quarter)
+
+    for_each_share(place_ref, n_role * n_tp, body)
+
+
+def run_first(place, own, w_gate, w_up, quarter, n_tp):
+    vmem = pl.BlockSpec(memory_space=pltpu.VMEM)
+    partial = jax.ShapeDtypeStruct((own.shape[1], w_gate.shape[1]), jnp.float32)
+    return pl.pallas_call(
+        functools.partial(first_kernel, quarter=quarter, n_tp=n_tp),
+        in_specs=[pl.BlockSpec(memory_space=pltpu.SMEM)] + [vmem] * 3,
+        out_specs=[vmem, vmem],
+        out_shape=[partial, partial],
+        compiler_params=pltpu.CompilerParams(vmem_limit_bytes=16 << 20),
+        name="expert_first",
+    )(place, own, w_gate, w_up)
+
+
+def run_second(place, own, other, partials, w_gate, w_up, w_down, quarter, topk, n_tp):
     n_role, items, _ = own.shape
-    smem = pl.BlockSpec(memory_space=pltpu.SMEM)
     vmem = pl.BlockSpec(memory_space=pltpu.VMEM)
-    shape = jax.ShapeDtypeStruct((n_role, items, quarter), jnp.bfloat16)
     return pl.pallas_call(
-        functools.partial(expert_kernel, quarter=quarter, topk=topk),
-        in_specs=[smem] + [vmem] * 5,
-        out_specs=[vmem, vmem],
-        out_shape=[shape, shape],
-        scratch_shapes=[pltpu.VMEM((2 * n_role, items, quarter), jnp.bfloat16)],
+        functools.partial(second_kernel, quarter=quarter, topk=topk, n_tp=n_tp),
+        in_specs=[pl.BlockSpec(memory_space=pltpu.SMEM)] + [vmem] * 7,
+        out_specs=[vmem] * 3,
+        out_shape=[
+            jax.ShapeDtypeStruct((n_role, items, quarter), jnp.bfloat16),
+            jax.ShapeDtypeStruct((items, w_gate.shape[1]), jnp.bfloat16),
+            jax.ShapeDtypeStruct((items, 128), jnp.float32),
+        ],
         compiler_params=pltpu.CompilerParams(vmem_limit_bytes=24 << 20),
-        name="expert",
-    )(place, own, other, w_gate, w_up, w_down)
+        name="expert_second",
+    )(place, own, other, *partials, w_gate, w_up, w_down)
+
+
+def run_third(place, activated, weight, w_down, n_role, quarter, n_tp):
+    vmem = pl.BlockSpec(memory_space=pltpu.VMEM)
+    items = activated.shape[0]
+    return pl.pallas_call(
+        functools.partial(third_kernel, quarter=quarter, n_tp=n_tp),
+        in_specs=[pl.BlockSpec(memory_space=pltpu.SMEM)] + [vmem] * 3,
+        out_specs=vmem,
+        out_shape=jax.ShapeDtypeStruct((n_role, items, quarter), jnp.bfloat16),
+        compiler_params=pltpu.CompilerParams(vmem_limit_bytes=12 << 20),
+        name="expert_third",
+    )(place, activated, weight, w_down)
 
 
 def three_parts(x):
@@ -498,11 +581,14 @@
         )
         other = send(half, tp=1)
         place = jnp.stack([share, grp]).astype(jnp.int32)
-        kept, sent = run_expert(
-            place, half, other, jnp.swapaxes(w_gate, 1, 2), jnp.swapaxes(w_up, 1, 2), w_down,
-            quarter, topk,
-        )
-        acc = kept.astype(jnp.float32) + send(sent, tp=1).astype(jnp.float32)
+        gate_turned, up_turned = jnp.swapaxes(w_gate, 1, 2), jnp.swapaxes(w_up, 1, 2)
+        partials = run_first(place, half, gate_turned, up_turned, quarter, n_tp)
+        sent, activated, weight = run_second(
+            place, half, other, partials, gate_turned, up_turned, w_down, quarter, topk, n_tp
+        )
+        returned = send(sent, tp=1)
+        kept = run_third(place, activated, weight, w_down, n_role, quarter, n_tp)
+        acc = kept.astype(jnp.float32) + returned.astype(jnp.float32)
         acc = acc.astype(jnp.bfloat16).reshape(n_role, n_near, n_far * cap, quarter)
         back = []
         for j in range(n_near):

time: 55.3 us -> 54.7 us (0.989)
  waiting for transfers between devices: 23.2 us -> 20.7 us
  Pallas kernels: 9.93 us -> 11.8 us
    ppermute x11, waiting for transfers between devices: 15.1 us -> 12.6 us  [send(): lax.ppermute(x, names, swap_table(mesh, lambda g: g ^ near, role, tp))]
    pallas_call x1 -> x3, Pallas kernels: 2.76 us -> 4.65 us  [the longest x1 2.19 us: run_second(): pl.pallas_call(functools.partial(second_kernel, quarter=quarter, topk=top...]
  transfers between devices with their start and end apart: 17 -> 17, of which waited for: 14 -> 14; matrix products, arithmetic and copies ran while one was open for 2% -> 2% of each run, Pallas kernels for 0% -> 5%
where the time goes in v5:
time: 54.7 us; the launch traced here: 54.5 us
  waiting for transfers between devices  20.7 us (38%)
  starting transfers between devices  19.4 us (35%)
  Pallas kernels  11.8 us (22%)
  other arithmetic  0.99 us (2%)
  local copies, waits for them, and re-layouts  0.84 us (2%)
  between operations  0.79 us (1%)
    ppermute x11, waiting for transfers between devices, send(): lax.ppermute(x, names, swap_table(mesh, lambda g: g ^ near, role, tp))  12.6 us
    ppermute x11, starting transfers between devices, send(): lax.ppermute(x, names, swap_table(mesh, lambda g: g ^ near, role, tp))  10.5 us
    ppermute x6, starting transfers between devices, send_far(): return lax.ppermute(x, names, swap_table(mesh, grp_of, 0, 0))  8.84 us
    ppermute x6, waiting for transfers between devices, send_far(): return lax.ppermute(x, names, swap_table(mesh, grp_of, 0, 0))  8.15 us
    pallas_call x1, Pallas kernels, attend_project(): pl.pallas_call(functools.partial(attend_kernel, grouped=HEADS // KV_HEADS...  4.36 us
    pallas_call x1, Pallas kernels, run_second(): pl.pallas_call(functools.partial(second_kernel, quarter=quarter, topk=top...  2.19 us
    pallas_call x1, Pallas kernels, run_first(): pl.pallas_call(functools.partial(first_kernel, quarter=quarter, n_tp=n_tp...  1.44 us
  transfers between devices with their start and end apart: 17, of which 14 were waited for; matrix products, arithmetic and copies ran while one was open for 2% of the time, Pallas kernels for 5%

profile of v5, /device:TPU:0, one launch (start us, length us, event | category | flops | bytes accessed | tf_op | source)
XLA Modules:
  0.0 54.5 jit_solution(6382728224730300306)
XLA Ops:
  0.6 4.4 %attend_project.1 = (bf16[32,720]{1,0:T(8,128)(2,1)S(1)}, bf16[32,720]{1,0:T(8,128)(2,1)S(1)}, bf16[32,1024]{1,0:T(8,128)(2,1)S(1)}, bf16[2,720,1024]{2,1,0:T(8,128)(2,1)S(1)}) custom-call(s32[1]{0:T(128)} %bitcast.share_ref, s32[32]{0:T(128)} %len_hbm.1, s32[32]{0:T(128)} %start_hbm.1, bf16[32,1024]{1,0:T(8,128)(2,1)} %q_hbm.1, bf16[32,128]{1,0:T(8,128)(2,1)} %kn_hbm.1, ...), custom_call_target="tpu_custom_call" | custom-call | tf_op jit(solution)/shard_map/attend_project/pallas_call | solution.py:162
  5.0 0.9 %project.1 = (f32[32,720]{1,0:T(8,128)S(1)}, bf16[32,720]{1,0:T(8,128)(2,1)S(1)}) custom-call(bf16[32,1024]{1,0:T(8,128)(2,1)S(1)} %get-tuple-element.23.stacked_ref, bf16[2,720,1024]{2,1,0:T(8,128)(2,1)S(1)} %get-tuple-element.24.later_ref), custom_call_target="tpu_custom_call" | custom-call | tf_op jit(solution)/shard_map/project/pallas_call | solution.py:203
  6.5 2.5 %collective-permute-start.1 = (bf16[32,720]{1,0:T(8,128)(2,1)S(1)}, bf16[32,720]{1,0:T(8,128)(2,1)S(1)}, u32[]{:S(2)}, u32[]{:S(2)}) collective-permute-start(bf16[32,720]{1,0:T(8,128)(2,1)S(1)} %get-tuple-element.27), channel_id=1, source_target_pairs={{0,16},{1,17},{2,18},{3,19},{4,20},{5,21},{6,22},{7,23},{8,24},{9,... | collective-permute-start | bytes 138248 | tf_op jit(solution)/shard_map/ppermute | solution.py:539
  9.1 0.8 %dynamic_slice.3 = f32[720]{0:T(1024)S(1)} dynamic-slice(f32[2880]{0:T(1024)} %param.24, s32[]{:T(128)S(6)} %select_n.14), dynamic_slice_sizes={720} | dynamic-slice | bytes 5764 | tf_op jit(solution)/shard_map/dynamic_slice | solution.py:567
  9.8 1.5 %collective-permute-done.1.rest_1_ = bf16[32,720]{1,0:T(8,128)(2,1)S(1)} collective-permute-done((bf16[32,720]{1,0:T(8,128)(2,1)S(1)}, bf16[32,720]{1,0:T(8,128)(2,1)S(1)}, u32[]{:S(2)}, u32[]{:S(2)}) %collective-permute-start.1) | collective-permute-done | bytes 46112 | tf_op jit(solution)/shard_map/ppermute | solution.py:539
  11.3 1.4 %collective-permute-done.2.rest_2_ = bf16[32,720]{1,0:T(8,128)(2,1)S(1)} collective-permute-done((bf16[32,720]{1,0:T(8,128)(2,1)S(1)}, bf16[32,720]{1,0:T(8,128)(2,1)S(1)}, u32[]{:S(2)}, u32[]{:S(2)}) %collective-permute-start.2) | collective-permute-done | bytes 46112 | tf_op jit(solution)/shard_map/ppermute | solution.py:539
  12.7 0.7 %pack.1 = (bf16[32,720]{1,0:T(8,128)(2,1)}, bf16[32,768]{1,0:T(8,128)(2,1)S(1)}) custom-call(f32[32,720]{1,0:T(8,128)S(1)} %get-tuple-element.25.own_ref, bf16[32,720]{1,0:T(8,128)(2,1)S(1)} %collective-permute-done.rest_0_, bf16[32,720]{1,0:T(8,128)(2,1)S(1)} %collective-permute-done.1.rest_1_, bf16[32,720]{1,0:T(8,128)(2,1)S(1)} %collective-permute-done.2.rest_2_, ...), custom_call_target="tpu_custom_call" | custom-call | flops 8589934592 | bytes 1048576 | tf_op jit(solution)/shard_map/pack/pallas_call | solution.py:416
  13.4 1.6 %collective-permute-start.3 = (bf16[32,768]{1,0:T(8,128)(2,1)S(1)}, bf16[32,768]{1,0:T(8,128)(2,1)S(1)}, u32[]{:S(2)}, u32[]{:S(2)}) collective-permute-start(bf16[32,768]{1,0:T(8,128)(2,1)S(1)} %get-tuple-element.30.rest_0_), channel_id=1, source_target_pairs={{0,4},{1,5},{2,6},{3,7},{4,0},{5,1},{6,2},{7,3},{8,12},{9,13},{10,... | collective-permute-start | bytes 147464 | tf_op jit(solution)/shard_map/ppermute | solution.py:546
  15.0 2.6 %collective-permute-start.4 = (bf16[32,768]{1,0:T(8,128)(2,1)S(1)}, bf16[32,768]{1,0:T(8,128)(2,1)S(1)}, u32[]{:S(2)}, u32[]{:S(2)}) collective-permute-start(bf16[32,768]{1,0:T(8,128)(2,1)S(1)} %get-tuple-element.30.rest_0_), channel_id=1, source_target_pairs={{0,8},{1,9},{2,10},{3,11},{4,12},{5,13},{6,14},{7,15},{8,0},{9,1},... | collective-permute-start | bytes 147464 | tf_op jit(solution)/shard_map/ppermute | solution.py:546
  17.9 3.0 %collective-permute-done.4.rest_2_ = bf16[32,768]{1,0:T(8,128)(2,1)S(1)} collective-permute-done((bf16[32,768]{1,0:T(8,128)(2,1)S(1)}, bf16[32,768]{1,0:T(8,128)(2,1)S(1)}, u32[]{:S(2)}, u32[]{:S(2)}) %collective-permute-start.4) | collective-permute-done | bytes 49184 | tf_op jit(solution)/shard_map/ppermute | solution.py:546
  20.9 2.6 %collective-permute-done.5.rest_3_ = bf16[32,768]{1,0:T(8,128)(2,1)S(1)} collective-permute-done((bf16[32,768]{1,0:T(8,128)(2,1)S(1)}, bf16[32,768]{1,0:T(8,128)(2,1)S(1)}, u32[]{:S(2)}, u32[]{:S(2)}) %collective-permute-start.5) | collective-permute-done | bytes 49184 | tf_op jit(solution)/shard_map/ppermute | solution.py:546
  23.5 1.0 %select.7 = (bf16[72,768]{1,0:T(8,128)(2,1)S(1)}, bf16[72,768]{1,0:T(8,128)(2,1)S(1)}, bf16[72,128]{1,0:T(8,128)(2,1)S(1)}, bf16[72,128]{1,0:T(8,128)(2,1)S(1)}) custom-call(s32[2]{0:T(128)S(1)} %pad_add_fusion.1.expert_ref, bf16[32,768]{1,0:T(8,128)(2,1)S(1)} %get-tuple-element.30.rest_0_, bf16[32,768]{1,0:T(8,128)(2,1)S(1)} %collective-permute-done.3.rest_1_, ...), custom_call_target="tpu_custom_call" | custom-call | tf_op jit(solution)/shard_map/select/pallas_call | solution.py:472
  24.4 1.6 %collective-permute-start.6 = (bf16[72,768]{1,0:T(8,128)(2,1)S(1)}, bf16[72,768]{1,0:T(8,128)(2,1)S(1)}, u32[]{:S(2)}, u32[]{:S(2)}) collective-permute-start(bf16[72,768]{1,0:T(8,128)(2,1)S(1)} %get-tuple-element.32), channel_id=1, source_target_pairs={{0,2},{1,3},{2,0},{3,1},{4,6},{5,7},{6,4},{7,5},{8,10},{9,11},{10,... | collective-permute-start | bytes 331784 | tf_op jit(solution)/shard_map/ppermute | solution.py:539
  26.0 0.9 %collective-permute-start.8 = (bf16[72,768]{1,0:T(8,128)(2,1)S(1)}, bf16[72,768]{1,0:T(8,128)(2,1)S(1)}, u32[]{:S(2)}, u32[]{:S(2)}) collective-permute-start(bf16[72,768]{1,0:T(8,128)(2,1)S(1)} %get-tuple-element.32), channel_id=1, source_target_pairs={{0,18},{1,19},{2,16},{3,17},{4,22},{5,23},{6,20},{7,21},{8,26},{9,... | collective-permute-start | bytes 331784 | tf_op jit(solution)/shard_map/ppermute | solution.py:539
  26.9 1.1 %collective-permute-start.7 = (bf16[72,768]{1,0:T(8,128)(2,1)S(1)}, bf16[72,768]{1,0:T(8,128)(2,1)S(1)}, u32[]{:S(2)}, u32[]{:S(2)}) collective-permute-start(bf16[72,768]{1,0:T(8,128)(2,1)S(1)} %get-tuple-element.31), channel_id=1, source_target_pairs={{0,16},{1,17},{2,18},{3,19},{4,20},{5,21},{6,22},{7,23},{8,24},{9,... | collective-permute-start | bytes 331784 | tf_op jit(solution)/shard_map/ppermute | solution.py:539
  28.0 2.1 %collective-permute-done.6 = bf16[72,768]{1,0:T(8,128)(2,1)S(1)} collective-permute-done((bf16[72,768]{1,0:T(8,128)(2,1)S(1)}, bf16[72,768]{1,0:T(8,128)(2,1)S(1)}, u32[]{:S(2)}, u32[]{:S(2)}) %collective-permute-start.6) | collective-permute-done | bytes 110624 | tf_op jit(solution)/shard_map/ppermute | solution.py:539
  30.1 1.6 %collective-permute-done.8 = bf16[72,768]{1,0:T(8,128)(2,1)S(1)} collective-permute-done((bf16[72,768]{1,0:T(8,128)(2,1)S(1)}, bf16[72,768]{1,0:T(8,128)(2,1)S(1)}, u32[]{:S(2)}, u32[]{:S(2)}) %collective-permute-start.8) | collective-permute-done | bytes 110624 | tf_op jit(solution)/shard_map/ppermute | solution.py:539
  32.1 1.4 %expert_first.1 = (f32[144,360]{1,0:T(8,128)S(1)}, f32[144,360]{1,0:T(8,128)S(1)}) custom-call(s32[2]{0:T(128)S(1)} %pad_add_fusion.place_ref, bf16[2,144,768]{2,1,0:T(8,128)(2,1)S(1)} %pad_maximum_fusion.own_ref, bf16[1,360,2880]{2,1,0:T(8,128)(2,1)S(1)} %bitcast.22, bf16[1,360,2880]{2,1,0:T(8,128)(2,1)S(1)} %bitcast.24), custom_call_target="tpu_custom_call" | custom-call | tf_op jit(solution)/shard_map/expert_first/pallas_call | solution.py:319
  33.8 2.2 %expert_second.1 = (bf16[2,144,720]{2,1,0:T(8,128)(2,1)S(1)}, bf16[144,360]{1,0:T(8,128)(2,1)S(1)}, f32[144,128]{1,0:T(8,128)S(1)}) custom-call(s32[2]{0:T(128)S(1)} %pad_add_fusion.place_ref, bf16[2,144,768]{2,1,0:T(8,128)(2,1)S(1)} %pad_maximum_fusion.own_ref, bf16[2,144,768]{2,1,0:T(8,128)(2,1)S(1)} %collective-permute-done.9.other_ref, ...), custom_call_target="tpu_custom_call" | custom-call | tf_op jit(solution)/shard_map/expert_second/pallas_call | solution.py:332
  36.3 1.0 %expert_third.1 = bf16[2,144,720]{2,1,0:T(8,128)(2,1)S(1)} custom-call(s32[2]{0:T(128)S(1)} %pad_add_fusion.place_ref, bf16[144,360]{1,0:T(8,128)(2,1)S(1)} %get-tuple-element.35.activated_ref, f32[144,128]{1,0:T(8,128)S(1)} %get-tuple-element.36.weight_ref, bf16[1,360,2880]{2,1,0:T(8,128)(2,1)S(1)} %copy-done.2), custom_call_target="tpu_custom_call" | custom-call | tf_op jit(solution)/shard_map/expert_third/pallas_call | solution.py:349
  37.3 0.6 %collective-permute-done.10 = bf16[2,144,720]{2,1,0:T(8,128)(2,1)S(1)} collective-permute-done((bf16[2,144,720]{2,1,0:T(8,128)(2,1)S(1)}, bf16[2,144,720]{2,1,0:T(8,128)(2,1)S(1)}, u32[]{:S(2)}, u32[]{:S(2)}) %collective-permute-start.10) | collective-permute-done | bytes 414752 | tf_op jit(solution)/shard_map/ppermute | solution.py:539
  38.0 1.0 %collective-permute-start.11 = (bf16[72,720]{1,0:T(8,128)(2,1)S(1)}, bf16[72,720]{1,0:T(8,128)(2,1)S(1)}, u32[]{:S(2)}, u32[]{:S(2)}) collective-permute-start(bf16[72,720]{1,0:T(8,128)(2,1)S(1)} %get-tuple-element.46), channel_id=1, source_target_pairs={{0,16},{1,17},{2,18},{3,19},{4,20},{5,21},{6,22},{7,23},{8,24},{9,... | collective-permute-start | bytes 311048 | tf_op jit(solution)/shard_map/ppermute | solution.py:539
  39.0 1.5 %collective-permute-start.12 = (bf16[72,720]{1,0:T(8,128)(2,1)S(1)}, bf16[72,720]{1,0:T(8,128)(2,1)S(1)}, u32[]{:S(2)}, u32[]{:S(2)}) collective-permute-start(bf16[72,720]{1,0:T(8,128)(2,1)S(1)} %get-tuple-element.45), channel_id=1, source_target_pairs={{0,2},{1,3},{2,0},{3,1},{4,6},{5,7},{6,4},{7,5},{8,10},{9,11},{10,... | collective-permute-start | bytes 311048 | tf_op jit(solution)/shard_map/ppermute | solution.py:539
  40.5 1.1 %collective-permute-start.13 = (bf16[72,720]{1,0:T(8,128)(2,1)S(1)}, bf16[72,720]{1,0:T(8,128)(2,1)S(1)}, u32[]{:S(2)}, u32[]{:S(2)}) collective-permute-start(bf16[72,720]{1,0:T(8,128)(2,1)S(1)} %get-tuple-element.44), channel_id=1, source_target_pairs={{0,18},{1,19},{2,16},{3,17},{4,22},{5,23},{6,20},{7,21},{8,26},{9,... | collective-permute-start | bytes 311048 | tf_op jit(solution)/shard_map/ppermute | solution.py:539
  41.6 2.2 %collective-permute-done.11.refs_1_ = bf16[72,720]{1,0:T(8,128)(2,1)S(1)} collective-permute-done((bf16[72,720]{1,0:T(8,128)(2,1)S(1)}, bf16[72,720]{1,0:T(8,128)(2,1)S(1)}, u32[]{:S(2)}, u32[]{:S(2)}) %collective-permute-start.11) | collective-permute-done | bytes 103712 | tf_op jit(solution)/shard_map/ppermute | solution.py:539
  43.8 1.4 %collective-permute-done.12.refs_2_ = bf16[72,720]{1,0:T(8,128)(2,1)S(1)} collective-permute-done((bf16[72,720]{1,0:T(8,128)(2,1)S(1)}, bf16[72,720]{1,0:T(8,128)(2,1)S(1)}, u32[]{:S(2)}, u32[]{:S(2)}) %collective-permute-start.12) | collective-permute-done | bytes 103712 | tf_op jit(solution)/shard_map/ppermute | solution.py:539
  45.3 1.3 %collective-permute-done.13.refs_3_ = bf16[72,720]{1,0:T(8,128)(2,1)S(1)} collective-permute-done((bf16[72,720]{1,0:T(8,128)(2,1)S(1)}, bf16[72,720]{1,0:T(8,128)(2,1)S(1)}, u32[]{:S(2)}, u32[]{:S(2)}) %collective-permute-start.13) | collective-permute-done | bytes 103712 | tf_op jit(solution)/shard_map/ppermute | solution.py:539
  46.8 1.1 %collective-permute-start.16 = (bf16[32,720]{1,0:T(8,128)(2,1)S(1)}, bf16[32,720]{1,0:T(8,128)(2,1)S(1)}, u32[]{:S(2)}, u32[]{:S(2)}) collective-permute-start(bf16[32,720]{1,0:T(8,128)(2,1)S(1)} %get-tuple-element.43), channel_id=1, source_target_pairs={{0,12},{1,13},{2,14},{3,15},{4,8},{5,9},{6,10},{7,11},{8,4},{9,5},... | collective-permute-start | bytes 138248 | tf_op jit(solution)/shard_map/ppermute | solution.py:546
  48.0 3.3 %collective-permute-start.14 = (bf16[32,720]{1,0:T(8,128)(2,1)S(1)}, bf16[32,720]{1,0:T(8,128)(2,1)S(1)}, u32[]{:S(2)}, u32[]{:S(2)}) collective-permute-start(bf16[32,720]{1,0:T(8,128)(2,1)S(1)} %get-tuple-element.41), channel_id=1, source_target_pairs={{0,4},{1,5},{2,6},{3,7},{4,0},{5,1},{6,2},{7,3},{8,12},{9,13},{10,... | collective-permute-start | bytes 138248 | tf_op jit(solution)/shard_map/ppermute | solution.py:546
  51.3 1.5 %collective-permute-done.16 = bf16[32,720]{1,0:T(8,128)(2,1)S(1)} collective-permute-done((bf16[32,720]{1,0:T(8,128)(2,1)S(1)}, bf16[32,720]{1,0:T(8,128)(2,1)S(1)}, u32[]{:S(2)}, u32[]{:S(2)}) %collective-permute-start.16) | collective-permute-done | bytes 46112 | tf_op jit(solution)/shard_map/ppermute | solution.py:546
  52.8 1.0 %collective-permute-done.15 = bf16[32,720]{1,0:T(8,128)(2,1)S(1)} collective-permute-done((bf16[32,720]{1,0:T(8,128)(2,1)S(1)}, bf16[32,720]{1,0:T(8,128)(2,1)S(1)}, u32[]{:S(2)}, u32[]{:S(2)}) %collective-permute-start.15) | collective-permute-done | bytes 46112 | tf_op jit(solution)/shard_map/ppermute | solution.py:546
  53.9 0.6 %add_convert_fusion.1 = bf16[32,720]{1,0:T(8,128)(2,1)} fusion(bf16[32,720]{1,0:T(8,128)(2,1)S(1)} %collective-permute-done.16, bf16[32,720]{1,0:T(8,128)(2,1)S(1)} %collective-permute-done.15, f32[32,720]{1,0:T(8,128)S(1)} %get-tuple-element.40, bf16[32,720]{1,0:T(8,128)(2,1)S(1)} %collective-permute-done.14), kind=kLoop, calls=%fused_computation.8 | loop fusion | flops 161280 | bytes 276480 | tf_op jit(solution)/shard_map/convert_element_type | solution.py:604
  (32 shorter events, 2.3 us)
Async XLA Ops:
  5.0 7.7 %copy-start.3 = (bf16[32,720]{1,0:T(8,128)(2,1)S(1)}, bf16[32,720]{1,0:T(8,128)(2,1)}, u32[]{:S(2)}) copy-start(bf16[32,720]{1,0:T(8,128)(2,1)} %rest_3_.1) | copy-start | bytes 138244
  5.0 7.7 %copy-start.4 = (bf16[720,8]{0,1:T(8,128)(2,1)S(1)}, bf16[720,8]{0,1:T(8,128)(2,1)}, u32[]{:S(2)}) copy-start(bf16[720,8]{0,1:T(8,128)(2,1)} %param.25) | copy-start | bytes 34564
  5.0 7.7 %copy-start.5 = (s32[32,4]{0,1:T(4,128)S(1)}, s32[32,4]{0,1:T(4,128)}, u32[]{:S(2)}) copy-start(s32[32,4]{0,1:T(4,128)} %param.26) | copy-start | bytes 1540
  6.0 3.9 %collective-permute-start = (bf16[32,720]{1,0:T(8,128)(2,1)S(1)}, bf16[32,720]{1,0:T(8,128)(2,1)S(1)}, u32[]{:S(2)}, u32[]{:S(2)}) collective-permute-start(bf16[32,720]{1,0:T(8,128)(2,1)S(1)} %get-tuple-element.26), channel_id=1, source_target_pairs={{0,1},{1,0},{2,3},{3,2},{4,5},{5,4},{6,7},{7,6},{8,9},{9,8},{10,11... | collective-permute-start | bytes 138248 | tf_op jit(solution)/shard_map/ppermute | solution.py:539
  6.5 4.9 %collective-permute-start.1 = (bf16[32,720]{1,0:T(8,128)(2,1)S(1)}, bf16[32,720]{1,0:T(8,128)(2,1)S(1)}, u32[]{:S(2)}, u32[]{:S(2)}) collective-permute-start(bf16[32,720]{1,0:T(8,128)(2,1)S(1)} %get-tuple-element.27), channel_id=1, source_target_pairs={{0,16},{1,17},{2,18},{3,19},{4,20},{5,21},{6,22},{7,23},{8,24},{9,... | collective-permute-start | bytes 138248 | tf_op jit(solution)/shard_map/ppermute | solution.py:539
  9.0 3.7 %collective-permute-start.2 = (bf16[32,720]{1,0:T(8,128)(2,1)S(1)}, bf16[32,720]{1,0:T(8,128)(2,1)S(1)}, u32[]{:S(2)}, u32[]{:S(2)}) collective-permute-start(bf16[32,720]{1,0:T(8,128)(2,1)S(1)} %get-tuple-element.28), channel_id=1, source_target_pairs={{0,17},{1,16},{2,19},{3,18},{4,21},{5,20},{6,23},{7,22},{8,25},{9,... | collective-permute-start | bytes 138248 | tf_op jit(solution)/shard_map/ppermute | solution.py:539
  12.7 19.4 %copy-start = (bf16[1,2880,360]{1,2,0:T(8,128)(2,1)S(1)}, bf16[1,2880,360]{1,2,0:T(8,128)(2,1)}, u32[]{:S(2)}) copy-start(bf16[1,2880,360]{1,2,0:T(8,128)(2,1)} %param.27) | copy-start | bytes 6220804
  12.7 19.4 %copy-start.1 = (bf16[1,2880,360]{1,2,0:T(8,128)(2,1)S(1)}, bf16[1,2880,360]{1,2,0:T(8,128)(2,1)}, u32[]{:S(2)}) copy-start(bf16[1,2880,360]{1,2,0:T(8,128)(2,1)} %param.28) | copy-start | bytes 6220804
  13.4 4.5 %collective-permute-start.3 = (bf16[32,768]{1,0:T(8,128)(2,1)S(1)}, bf16[32,768]{1,0:T(8,128)(2,1)S(1)}, u32[]{:S(2)}, u32[]{:S(2)}) collective-permute-start(bf16[32,768]{1,0:T(8,128)(2,1)S(1)} %get-tuple-element.30.rest_0_), channel_id=1, source_target_pairs={{0,4},{1,5},{2,6},{3,7},{4,0},{5,1},{6,2},{7,3},{8,12},{9,13},{10,... | collective-permute-start | bytes 147464 | tf_op jit(solution)/shard_map/ppermute | solution.py:546
  15.0 5.9 %collective-permute-start.4 = (bf16[32,768]{1,0:T(8,128)(2,1)S(1)}, bf16[32,768]{1,0:T(8,128)(2,1)S(1)}, u32[]{:S(2)}, u32[]{:S(2)}) collective-permute-start(bf16[32,768]{1,0:T(8,128)(2,1)S(1)} %get-tuple-element.30.rest_0_), channel_id=1, source_target_pairs={{0,8},{1,9},{2,10},{3,11},{4,12},{5,13},{6,14},{7,15},{8,0},{9,1},... | collective-permute-start | bytes 147464 | tf_op jit(solution)/shard_map/ppermute | solution.py:546
  17.6 5.9 %collective-permute-start.5 = (bf16[32,768]{1,0:T(8,128)(2,1)S(1)}, bf16[32,768]{1,0:T(8,128)(2,1)S(1)}, u32[]{:S(2)}, u32[]{:S(2)}) collective-permute-start(bf16[32,768]{1,0:T(8,128)(2,1)S(1)} %get-tuple-element.30.rest_0_), channel_id=1, source_target_pairs={{0,12},{1,13},{2,14},{3,15},{4,8},{5,9},{6,10},{7,11},{8,4},{9,5},... | collective-permute-start | bytes 147464 | tf_op jit(solution)/shard_map/ppermute | solution.py:546
  24.4 5.6 %collective-permute-start.6 = (bf16[72,768]{1,0:T(8,128)(2,1)S(1)}, bf16[72,768]{1,0:T(8,128)(2,1)S(1)}, u32[]{:S(2)}, u32[]{:S(2)}) collective-permute-start(bf16[72,768]{1,0:T(8,128)(2,1)S(1)} %get-tuple-element.32), channel_id=1, source_target_pairs={{0,2},{1,3},{2,0},{3,1},{4,6},{5,7},{6,4},{7,5},{8,10},{9,11},{10,... | collective-permute-start | bytes 331784 | tf_op jit(solution)/shard_map/ppermute | solution.py:539
  26.0 5.6 %collective-permute-start.8 = (bf16[72,768]{1,0:T(8,128)(2,1)S(1)}, bf16[72,768]{1,0:T(8,128)(2,1)S(1)}, u32[]{:S(2)}, u32[]{:S(2)}) collective-permute-start(bf16[72,768]{1,0:T(8,128)(2,1)S(1)} %get-tuple-element.32), channel_id=1, source_target_pairs={{0,18},{1,19},{2,16},{3,17},{4,22},{5,23},{6,20},{7,21},{8,26},{9,... | collective-permute-start | bytes 331784 | tf_op jit(solution)/shard_map/ppermute | solution.py:539
  26.9 5.0 %collective-permute-start.7 = (bf16[72,768]{1,0:T(8,128)(2,1)S(1)}, bf16[72,768]{1,0:T(8,128)(2,1)S(1)}, u32[]{:S(2)}, u32[]{:S(2)}) collective-permute-start(bf16[72,768]{1,0:T(8,128)(2,1)S(1)} %get-tuple-element.31), channel_id=1, source_target_pairs={{0,16},{1,17},{2,18},{3,19},{4,20},{5,21},{6,22},{7,23},{8,24},{9,... | collective-permute-start | bytes 331784 | tf_op jit(solution)/shard_map/ppermute | solution.py:539
  32.0 1.9 %collective-permute-start.9 = (bf16[2,144,768]{2,1,0:T(8,128)(2,1)S(1)}, bf16[2,144,768]{2,1,0:T(8,128)(2,1)S(1)}, u32[]{:S(2)}, u32[]{:S(2)}) collective-permute-start(bf16[2,144,768]{2,1,0:T(8,128)(2,1)S(1)} %pad_maximum_fusion.own_ref), channel_id=1, source_target_pairs={{0,1},{1,0},{2,3},{3,2},{4,5},{5,4},{6,7},{7,6},{8,9},{9,8},{10,11... | collective-permute-start | bytes 1327112 | tf_op jit(solution)/shard_map/ppermute | solution.py:539
  32.1 1.7 %copy-start.2 = (bf16[1,360,2880]{2,1,0:T(8,128)(2,1)S(1)}, bf16[1,360,2880]{2,1,0:T(8,128)(2,1)}, u32[]{:S(2)}) copy-start(bf16[1,360,2880]{2,1,0:T(8,128)(2,1)} %down_ref.3) | copy-start | bytes 6220804
  36.0 1.9 %collective-permute-start.10 = (bf16[2,144,720]{2,1,0:T(8,128)(2,1)S(1)}, bf16[2,144,720]{2,1,0:T(8,128)(2,1)S(1)}, u32[]{:S(2)}, u32[]{:S(2)}) collective-permute-start(bf16[2,144,720]{2,1,0:T(8,128)(2,1)S(1)} %get-tuple-element.37), channel_id=1, source_target_pairs={{0,1},{1,0},{2,3},{3,2},{4,5},{5,4},{6,7},{7,6},{8,9},{9,8},{10,11... | collective-permute-start | bytes 1244168 | tf_op jit(solution)/shard_map/ppermute | solution.py:539
  38.0 5.8 %collective-permute-start.11 = (bf16[72,720]{1,0:T(8,128)(2,1)S(1)}, bf16[72,720]{1,0:T(8,128)(2,1)S(1)}, u32[]{:S(2)}, u32[]{:S(2)}) collective-permute-start(bf16[72,720]{1,0:T(8,128)(2,1)S(1)} %get-tuple-element.46), channel_id=1, source_target_pairs={{0,16},{1,17},{2,18},{3,19},{4,20},{5,21},{6,22},{7,23},{8,24},{9,... | collective-permute-start | bytes 311048 | tf_op jit(solution)/shard_map/ppermute | solution.py:539
  39.0 6.3 %collective-permute-start.12 = (bf16[72,720]{1,0:T(8,128)(2,1)S(1)}, bf16[72,720]{1,0:T(8,128)(2,1)S(1)}, u32[]{:S(2)}, u32[]{:S(2)}) collective-permute-start(bf16[72,720]{1,0:T(8,128)(2,1)S(1)} %get-tuple-element.45), channel_id=1, source_target_pairs={{0,2},{1,3},{2,0},{3,1},{4,6},{5,7},{6,4},{7,5},{8,10},{9,11},{10,... | collective-permute-start | bytes 311048 | tf_op jit(solution)/shard_map/ppermute | solution.py:539
  40.5 6.0 %collective-permute-start.13 = (bf16[72,720]{1,0:T(8,128)(2,1)S(1)}, bf16[72,720]{1,0:T(8,128)(2,1)S(1)}, u32[]{:S(2)}, u32[]{:S(2)}) collective-permute-start(bf16[72,720]{1,0:T(8,128)(2,1)S(1)} %get-tuple-element.44), channel_id=1, source_target_pairs={{0,18},{1,19},{2,16},{3,17},{4,22},{5,23},{6,20},{7,21},{8,26},{9,... | collective-permute-start | bytes 311048 | tf_op jit(solution)/shard_map/ppermute | solution.py:539
  46.8 6.0 %collective-permute-start.16 = (bf16[32,720]{1,0:T(8,128)(2,1)S(1)}, bf16[32,720]{1,0:T(8,128)(2,1)S(1)}, u32[]{:S(2)}, u32[]{:S(2)}) collective-permute-start(bf16[32,720]{1,0:T(8,128)(2,1)S(1)} %get-tuple-element.43), channel_id=1, source_target_pairs={{0,12},{1,13},{2,14},{3,15},{4,8},{5,9},{6,10},{7,11},{8,4},{9,5},... | collective-permute-start | bytes 138248 | tf_op jit(solution)/shard_map/ppermute | solution.py:546
  48.0 5.9 %collective-permute-start.15 = (bf16[32,720]{1,0:T(8,128)(2,1)S(1)}, bf16[32,720]{1,0:T(8,128)(2,1)S(1)}, u32[]{:S(2)}, u32[]{:S(2)}) collective-permute-start(bf16[32,720]{1,0:T(8,128)(2,1)S(1)} %get-tuple-element.42), channel_id=1, source_target_pairs={{0,8},{1,9},{2,10},{3,11},{4,12},{5,13},{6,14},{7,15},{8,0},{9,1},... | collective-permute-start | bytes 138248 | tf_op jit(solution)/shard_map/ppermute | solution.py:546
  48.0 5.9 %collective-permute-start.14 = (bf16[32,720]{1,0:T(8,128)(2,1)S(1)}, bf16[32,720]{1,0:T(8,128)(2,1)S(1)}, u32[]{:S(2)}, u32[]{:S(2)}) collective-permute-start(bf16[32,720]{1,0:T(8,128)(2,1)S(1)} %get-tuple-element.41), channel_id=1, source_target_pairs={{0,4},{1,5},{2,6},{3,7},{4,0},{5,1},{6,2},{7,3},{8,12},{9,13},{10,... | collective-permute-start | bytes 138248 | tf_op jit(solution)/shard_map/ppermute | solution.py:546
